TPU v7x, 256 devices: a whole 4x4x8 slice. The times are simulated.
256 devices in a mesh: frame: 32 (over z, y_lo, core), rec: 8 (over y_hi, x).
Axes of the slice: x: 4, y: 4 (y_hi: 2, y_lo: 2; y = y_hi * 2 + y_lo), z: 8, core: 2. Of those that a mesh axis runs over, the one named last changes fastest.
Arguments:
- code_indices: int32 [8, 8192, 8], P('rec', 'frame'), may hold values from 0 to 7
- lengths: int32 [8], P('rec'), may hold values from 4096 to 8192
- cotangent: bfloat16 [8, 2621440], P('rec', 'frame'), may hold values from -6 to 6
- embed_weight: float32 [8, 512], replicated, may hold values from -2 to 2
- embed_bias: float32 [512], replicated, may hold values from -3 to 3
- depth_kernel: float32 [7, 512], replicated, may hold values from -2 to 2
- depth_bias: float32 [512], replicated, may hold values from -3 to 3
- norm_gain: float32 [512], replicated, may hold values from 0.5 to 1.5
- norm_bias: float32 [512], replicated, may hold values from -1.75 to 1.75
- up_weight: bfloat16 [512, 1536], replicated, may hold values from -0.25 to 0.25
- up_bias: float32 [1536], replicated, may hold values from -3 to 3
- down_weight: bfloat16 [1536, 512], replicated, may hold values from -0.15625 to 0.15625
- down_bias: float32 [512], replicated, may hold values from -1.75 to 1.75
- layer_scale: float32 [512], replicated, may hold values from 0.3 to 1
- head_weight: bfloat16 [512, 1280], replicated, may hold values from -0.25 to 0.25
- head_bias: float32 [1280], replicated, may hold values from -3 to 3
Outputs:
- embed_weight_grad: float32 [8, 512], P(None, 'frame')
- embed_bias_grad: float32 [512], P('frame')
- depth_kernel_grad: float32 [7, 512], P(None, 'frame')
- depth_bias_grad: float32 [512], P('frame')
- norm_gain_grad: float32 [512], P('frame')
- norm_bias_grad: float32 [512], P('frame')
- up_weight_grad: float32 [512, 1536], P('frame')
- up_bias_grad: float32 [1536], P('frame')
- down_weight_grad: float32 [1536, 512], P('frame')
- down_bias_grad: float32 [512], P('frame')
- layer_scale_grad: float32 [512], P('frame')
- head_weight_grad: float32 [512, 1280], P('frame')
- head_bias_grad: float32 [1280], P('frame')
Inputs may be any that keep to these rules, and one draw needn't show every extreme that they name: `lengths`: frames at or after a recording's length are padding.
All inputs are finite; a program needn't handle non-finite values.
Results may differ from a plain program's by a relative error of at most 0.011.
Values may be sent and summed in bfloat16 or wider, within the bound.
No kernel may reach another device: no remote copies, remote signals or barrier semaphores. Data moves between devices by JAX's collectives and lax.ppermute only.
A program may use at most 64 MiB of HBM per device.

v0:
```python
import jax
import jax.numpy as jnp
from jax import lax
from jax.sharding import PartitionSpec as P

LEVELS = 8
KERNEL = 7
NFFT = 1280
HOP = 320
BINS = 640
PAD = 480


EPSILON = 1e-06


def padded_2(block, sides, width):
    for axis, dim in sides:
        count = lax.axis_size(axis)
        forward = [(i, i + 1) for i in range(count - 1)]
        backward = [(target, source) for source, target in forward]
        low = lax.ppermute(
            lax.slice_in_dim(block, block.shape[dim] - width, None, axis=dim), axis, forward
        )
        high = lax.ppermute(lax.slice_in_dim(block, 0, width, axis=dim), axis, backward)
        block = jnp.concatenate([low, block, high], axis=dim)
    return block


def cut_along(array, dim, size):
    shape = array.shape
    parts = array.reshape(*shape[:dim], size, shape[dim] // size, *shape[dim + 1 :])
    return jnp.moveaxis(parts, dim, 0)


def sum_together(arrays, axis, dims):
    size = lax.axis_size(axis)
    parts = [cut_along(a, dim, size) for a, dim in zip(arrays, dims)]
    lines = jnp.concatenate([b.reshape(size, -1) for b in parts], axis=1)
    extent = max(16, -(-lines.shape[1] // 1024) * 8)
    lines = jnp.pad(lines, ((0, 0), (0, extent * 128 - lines.shape[1]))).reshape(-1, 128)
    line, at, gathered = (lax.psum_scatter(lines, axis, tiled=True).reshape(-1), 0, [])
    for b in parts:
        part = b[0]
        gathered.append(line[at : at + part.size].reshape(part.shape))
        at += part.size
    return tuple(gathered)


def from_everyone(array, axis):
    copies = jnp.broadcast_to(array, (lax.axis_size(axis), *array.shape))
    return lax.all_to_all(copies, axis, split_axis=0, concat_axis=0, tiled=True)


def taken_together(array, axis):
    return from_everyone(array, axis).sum(axis=0)


def together(arrays, axis):
    ends = [0]
    for a in arrays:
        ends.append(ends[-1] + a.size)
    running = taken_together(jnp.concatenate([a.ravel() for a in arrays]), axis)
    return tuple((running[b:e].reshape(a.shape) for a, b, e in zip(arrays, ends, ends[1:])))


def hann_square(position, fft_size):
    window = 0.5 - 0.5 * jnp.cos(2.0 * jnp.pi / fft_size * position)
    return window * window


def synthesis(fft_size, bin_count):
    sample = jnp.arange(fft_size, dtype=jnp.int32)[:, None]
    frequency = jnp.arange(bin_count, dtype=jnp.int32)[None, :]
    turn_count = (sample * frequency % fft_size).astype(jnp.float32)
    angles = 2.0 * jnp.pi / fft_size * turn_count
    window = 0.5 - 0.5 * jnp.cos(2.0 * jnp.pi / fft_size * sample.astype(jnp.float32))
    factor = jnp.where(frequency == 0, 1.0, 2.0).astype(jnp.float32) * window / fft_size
    real_part = factor * jnp.cos(angles)
    imag_part = jnp.where(frequency == 0, 0.0, -factor * jnp.sin(angles))
    return jnp.concatenate([real_part, imag_part], axis=1).astype(jnp.bfloat16)


def sample_scale(first_sample, sample_count, total_frames, hop_size, fft_size, length):
    pad_size = (fft_size - hop_size) // 2
    sample = first_sample + jnp.arange(sample_count, dtype=jnp.int32)
    block_id = sample // hop_size
    offset = sample - block_id * hop_size + pad_size
    envelope = jnp.zeros((sample_count,), jnp.float32)
    for step_back in range(-2, 3):
        frame_id = block_id - step_back
        inside = offset + step_back * hop_size
        usable = (frame_id >= 0) & (frame_id < total_frames) & (inside >= 0) & (inside < fft_size)
        square = hann_square(inside.astype(jnp.float32), fft_size)
        envelope = envelope + jnp.where(usable, square, 0.0)
    alive_mask = sample < length * hop_size
    return jnp.where(alive_mask, 1.0 / envelope, 0.0)


def layer_norm(conv_out, norm_gain, norm_bias):
    centre = conv_out - jnp.mean(conv_out, axis=-1, keepdims=True)
    spread = jnp.mean(centre * centre, axis=-1, keepdims=True)
    return centre * lax.rsqrt(spread + EPSILON) * norm_gain + norm_bias


def exact_gelu(hidden_pre):
    return jax.nn.gelu(hidden_pre, approximate=False)


def head_map(logits):
    bin_count = logits.shape[1] // 2
    magnitude = jnp.exp(logits[:, :bin_count])
    phase_angle = logits[:, bin_count:]
    return jnp.concatenate(
        [magnitude * jnp.cos(phase_angle), magnitude * jnp.sin(phase_angle)], axis=1
    )


def contract_rows(former, latter, precision=None):
    return lax.dot_general(
        former,
        latter,
        (((0,), (0,)), ((), ())),
        precision=precision,
        preferred_element_type=jnp.float32,
    )


def contract_cols(former, latter):
    return lax.dot_general(
        former, latter, (((1,), (1,)), ((), ())), preferred_element_type=jnp.float32
    )


def embed_rows(code_rows, valid_rows, embed_weight, embed_bias):
    levels_half = (LEVELS - 1) / 2.0
    values = (code_rows.astype(jnp.float32) - levels_half) / levels_half
    projected = jnp.dot(values, embed_weight, precision=lax.Precision.HIGHEST) + embed_bias
    return (values, (valid_rows[:, None] * projected).astype(jnp.bfloat16))


def body(
    code_indices,
    lengths,
    cotangent,
    embed_weight,
    embed_bias,
    depth_kernel,
    depth_bias,
    norm_gain,
    norm_bias,
    up_weight,
    up_bias,
    down_weight,
    down_bias,
    layer_scale,
    head_weight,
    head_bias,
):
    code_rows = code_indices[0]
    frame_count = code_rows.shape[0]
    total_frames = frame_count * lax.axis_size("frame")
    first_frame = lax.axis_index("frame") * frame_count
    length = lengths[0]
    frame_ids = first_frame + jnp.arange(frame_count, dtype=jnp.int32)
    valid = (frame_ids < length).astype(jnp.float32)
    values, features = embed_rows(code_rows, valid, embed_weight, embed_bias)
    padded = padded_2(features, (("frame", 0),), 3)
    conv_out = jnp.zeros((frame_count, features.shape[1]), jnp.float32) + depth_bias
    for tap_index in range(KERNEL):
        conv_out = conv_out + depth_kernel[tap_index] * padded[
            tap_index : tap_index + frame_count
        ].astype(jnp.float32)
    normed, norm_pullback = jax.vjp(layer_norm, conv_out, norm_gain, norm_bias)
    normed_low = normed.astype(jnp.bfloat16)
    hidden_pre = jnp.dot(normed_low, up_weight, preferred_element_type=jnp.float32) + up_bias
    activated, gelu_pullback = jax.vjp(exact_gelu, hidden_pre)
    activated_low = activated.astype(jnp.bfloat16)
    branch = jnp.dot(activated_low, down_weight, preferred_element_type=jnp.float32) + down_bias
    latent = (features.astype(jnp.float32) + layer_scale * branch).astype(jnp.bfloat16)
    logits = jnp.dot(latent, head_weight, preferred_element_type=jnp.float32) + head_bias
    spectrum, head_pullback = jax.vjp(head_map, logits)
    sample_weight = sample_scale(
        first_frame * HOP, frame_count * HOP, total_frames, HOP, NFFT, length
    )
    sample_grad = (cotangent[0].astype(jnp.float32) * sample_weight).astype(jnp.bfloat16)
    extended = padded_2(sample_grad, (("frame", 0),), PAD)
    hop_rows = extended.reshape(frame_count + 3, HOP)
    frame_grad = jnp.concatenate(
        [hop_rows[quarter : quarter + frame_count] for quarter in range(4)], axis=1
    )
    spec_grad = jnp.dot(frame_grad, synthesis(NFFT, BINS), preferred_element_type=jnp.float32)
    logit_grad = head_pullback(spec_grad)[0]
    logit_low = logit_grad.astype(jnp.bfloat16)
    head_weight_grad = contract_rows(latent, logit_low)
    head_bias_grad = jnp.sum(logit_grad, axis=0)
    latent_grad = contract_cols(logit_low, head_weight)
    layer_scale_grad = jnp.sum(latent_grad * branch, axis=0)
    branch_grad = layer_scale * latent_grad
    down_bias_grad = jnp.sum(branch_grad, axis=0)
    branch_low = branch_grad.astype(jnp.bfloat16)
    down_weight_grad = contract_rows(activated_low, branch_low)
    activated_grad = contract_cols(branch_low, down_weight)
    hidden_grad = gelu_pullback(activated_grad)[0]
    up_bias_grad = jnp.sum(hidden_grad, axis=0)
    hidden_low = hidden_grad.astype(jnp.bfloat16)
    up_weight_grad = contract_rows(normed_low, hidden_low)
    normed_grad = contract_cols(hidden_low, up_weight)
    conv_grad, norm_gain_grad, norm_bias_grad = norm_pullback(normed_grad)
    depth_kernel_grad = jnp.stack(
        [
            jnp.sum(
                conv_grad * padded[tap_index : tap_index + frame_count].astype(jnp.float32), axis=0
            )
            for tap_index in range(KERNEL)
        ],
        axis=0,
    )
    depth_bias_grad = jnp.sum(conv_grad, axis=0)
    conv_rims = padded_2(conv_grad.astype(jnp.bfloat16), (("frame", 0),), 3).astype(conv_grad.dtype)
    feature_grad = latent_grad
    for tap_index in range(KERNEL):
        feature_grad = (
            feature_grad
            + depth_kernel[tap_index] * conv_rims[6 - tap_index : 6 - tap_index + frame_count]
        )
    feature_grad = valid[:, None] * feature_grad
    embed_weight_grad = contract_rows(values, feature_grad, lax.Precision.HIGHEST)
    embed_bias_grad = jnp.sum(feature_grad, axis=0)
    shares = sum_together(
        (
            embed_weight_grad,
            embed_bias_grad,
            depth_kernel_grad,
            depth_bias_grad,
            norm_gain_grad,
            norm_bias_grad,
            up_weight_grad,
            up_bias_grad,
            down_weight_grad,
            down_bias_grad,
            layer_scale_grad,
            head_weight_grad,
            head_bias_grad,
        ),
        "frame",
        (1, 0, 1, 0, 0, 0, 0, 0, 0, 0, 0, 0, 0),
    )
    totals = together(
        (
            shares[0],
            shares[1],
            shares[2],
            shares[3],
            shares[4],
            shares[5],
            shares[6],
            shares[7],
            shares[8],
            shares[9],
            shares[10],
            shares[11],
            shares[12],
        ),
        "rec",
    )
    return (
        totals[0],
        totals[1],
        totals[2],
        totals[3],
        totals[4],
        totals[5],
        totals[6],
        totals[7],
        totals[8],
        totals[9],
        totals[10],
        totals[11],
        totals[12],
    )


def solution(mesh):
    return jax.shard_map(
        body,
        mesh=mesh,
        in_specs=(
            P("rec", "frame", None),
            P("rec"),
            P("rec", "frame"),
            P(),
            P(),
            P(),
            P(),
            P(),
            P(),
            P(),
            P(),
            P(),
            P(),
            P(),
            P(),
            P(),
        ),
        out_specs=(
            P(None, "frame"),
            P("frame"),
            P(None, "frame"),
            P("frame"),
            P("frame"),
            P("frame"),
            P("frame", None),
            P("frame"),
            P("frame", None),
            P("frame"),
            P("frame"),
            P("frame", None),
            P("frame"),
        ),
        check_vma=False,
    )
```

profile of v0, /device:TPU:2, one launch (start us, length us, event | category | flops | bytes accessed | tf_op | source)
XLA Modules:
  0.0 473.6 jit_solution(2158948526670754654)
XLA Ops:
  8.0 1.3 fusion.16
  9.4 1.7 collective-permute-start
  11.1 1.3 collective-permute-start.1
  12.4 1.3 convert_element_type.138
  13.8 6.5 %multiply_convert_fusion.3 = bf16[81920]{0:T(1024)(128)(2,1)S(1)} fusion(f32[81920]{0:T(1024)S(1)} %bitcast.49, s32[]{:T(128)S(6)} %mul.441, s32[]{:T(128)S(6)} %mul.440), kind=kLoop, calls=%fused_computation.109 | loop fusion | flops 7700480 | bytes 491528 | tf_op jit(solution)/shard_map/convert_element_type | solution.py:186
  20.3 4.4 collective-permute-start.2
  24.7 1.5 collective-permute-start.3
  26.3 15.2 %multiply_convert_fusion = (bf16[1280,640]{1,0:T(8,128)(2,1)S(1)}, bf16[1280,640]{1,0:T(8,128)(2,1)}) fusion(f32[1280]{0:T(1024)S(1)} %multiply_subtract_fusion.1, f32[640]{0:T(1024)S(1)} %broadcast_select_fusion, pred[640]{0:T(1024)(128)(4,1)S(1)} %iota_compare_fusion), kind=kLoop, calls=%fused_computation.8 | loop fusion | flops 13926400 | bytes 3285120 | tf_op jit(solution)/shard_map/convert.1
  41.6 1.2 pad_maximum_fusion.3
  42.7 1.8 slice.227
  44.5 1.8 slice.229
  46.3 1.8 slice.232
  48.1 1.8 slice.234
  49.9 2.1 concatenate.42
  52.0 2.7 fusion.2
  55.7 3.8 multiply_convert_fusion.1
  59.5 1.4 fusion.32
  61.4 2.9 multiply_add_fusion.1
  64.8 1.0 fusion.100
  66.6 2.4 fusion.43
  69.0 2.3 fusion.67
  71.2 2.0 fusion.69
  75.4 4.3 collective-permute-start.4
  79.7 1.3 collective-permute-start.5
  81.6 3.4 reshape_reshape.9
  85.1 3.4 reshape_reshape.10
  88.4 3.2 reshape_reshape.11
  92.6 1.3 convolution_bitcast_fusion
  94.8 1.4 dynamic-update-slice.1
  96.2 1.5 dynamic-update-slice.2
  97.7 1.3 dynamic-update-slice.3
  99.0 1.5 dynamic-update-slice.4
  100.5 1.5 dynamic-update-slice.5
  102.0 12.2 %dynamic-update-slice.6 = f32[32,70056]{1,0:T(8,128)} dynamic-update-slice(f32[32,70056]{1,0:T(8,128)} %dynamic-update-slice.5, f32[32,24576]{1,0:T(8,128)} %reshape_reshape.9, s32[]{} %constant.167, s32[]{} %constant.173) | dynamic-update-slice | bytes 6291460
  114.2 1.5 dynamic-update-slice.7
  115.7 12.1 %dynamic-update-slice.8 = f32[32,70056]{1,0:T(8,128)} dynamic-update-slice(f32[32,70056]{1,0:T(8,128)} %dynamic-update-slice.7, f32[32,24576]{1,0:T(8,128)} %reshape_reshape.10, s32[]{} %constant.167, s32[]{} %constant.175) | dynamic-update-slice | bytes 6291460
  127.8 1.5 dynamic-update-slice.9
  129.3 1.5 dynamic-update-slice.10
  130.8 3.4 constant_dynamic-update-slice_fusion.8
  134.8 7.6 %pad.12 = f32[32,70656]{1,0:T(8,128)} pad(f32[32,70056]{1,0:T(8,128)} %constant_dynamic-update-slice_fusion.7, f32[]{:T(128)} %constant.60.clone.1), padding=0_0x0_600 | pad | bytes 18011140 | tf_op jit(solution)/shard_map/jit(_pad)/pad | solution.py:41
  142.4 7.7 %reshape.199 = f32[17664,128]{1,0:T(8,128)} reshape(f32[32,70656]{1,0:T(8,128)} %pad.12) | data formatting | bytes 18087936 | tf_op jit(solution)/shard_map/reshape | solution.py:41
  152.1 263.7 %all-reduce.6.cloned.1.call-done = f32[17664,128]{1,0:T(8,128)} async-done(((f32[17664,128]{1,0:T(8,128)}), f32[17664,128]{1,0:T(8,128)}) %all-reduce.6.cloned.1.call-update) | async-done | bytes 9043984
  415.8 1.0 dynamic-slice_bitcast_fusion
  417.5 0.9 dynamic-slice_bitcast_fusion.1
  418.4 0.9 dynamic-slice_bitcast_fusion.2
  419.4 1.2 broadcast_in_dim.60
  420.5 37.7 %all_to_all.6 = f32[8,1,70056]{2,1,0:T(1,128)} all-to-all(f32[8,1,70056]{2,1,0:T(1,128)S(1)} %broadcast_in_dim.60), channel_id=1, replica_groups=mesh['frame'=32,'rec'=8] {'rec'}, dimensions={0} | all-to-all | bytes 4483584 | tf_op jit(solution)/shard_map/all_to_all | solution.py:52
  458.2 3.3 reduce_sum.215
  (109 shorter events, 15.2 us)
Async XLA Ops:
  7.2 48.4 %copy-start = (bf16[512,1536]{1,0:T(8,128)(2,1)S(1)}, bf16[512,1536]{1,0:T(8,128)(2,1)}, u32[]{:S(2)}) copy-start(bf16[512,1536]{1,0:T(8,128)(2,1)} %param.25) | copy-start | bytes 4718596
  7.2 408.6 %all-reduce.6.cloned.1.call-start = ((), (), s32[]{:S(2)}) async-start(), calls=%async_computation.1 | async-start | bytes 18087936
  9.4 50.1 %copy-start.3 = (bf16[256,512]{1,0:T(8,128)(2,1)}, bf16[256,512]{1,0:T(8,128)(2,1)S(1)}, u32[]{:S(2)}) copy-start(bf16[256,512]{1,0:T(8,128)(2,1)S(1)} %fusion.16) | copy-start | bytes 786436
  9.4 45.3 %collective-permute-start = (bf16[3,512]{1,0:T(4,128)(2,1)S(1)}, bf16[3,512]{1,0:T(4,128)(2,1)S(1)}, u32[]{:S(2)}, u32[]{:S(2)}) collective-permute-start(bf16[3,512]{1,0:T(4,128)(2,1)S(1)} %get-tuple-element.52), channel_id=1, source_target_pairs={{0,8},{8,16},{16,24},{24,32},{32,40},{40,48},{48,56},{56,64},{64,7... | collective-permute-start | bytes 9224 | tf_op jit(solution)/shard_map/ppermute | solution.py:22
  11.1 43.6 %collective-permute-start.1 = (bf16[3,512]{1,0:T(4,128)(2,1)S(1)}, bf16[3,512]{1,0:T(4,128)(2,1)S(1)}, u32[]{:S(2)}, u32[]{:S(2)}) collective-permute-start(bf16[3,512]{1,0:T(4,128)(2,1)S(1)} %get-tuple-element.53), channel_id=1, source_target_pairs={{8,0},{16,8},{24,16},{32,24},{40,32},{48,40},{56,48},{64,56},{72,6... | collective-permute-start | bytes 9224 | tf_op jit(solution)/shard_map/ppermute | solution.py:25
  20.3 21.2 %collective-permute-start.2 = (bf16[480]{0:T(512)(128)(2,1)S(1)}, bf16[480]{0:T(512)(128)(2,1)S(1)}, u32[]{:S(2)}, u32[]{:S(2)}) collective-permute-start(bf16[480]{0:T(512)(128)(2,1)S(1)} %get-tuple-element.61), channel_id=1, source_target_pairs={{0,8},{8,16},{16,24},{24,32},{32,40},{40,48},{48,56},{56,64},{64,7... | collective-permute-start | bytes 2888 | tf_op jit(solution)/shard_map/ppermute | solution.py:22
  24.7 16.9 %collective-permute-start.3 = (bf16[480]{0:T(512)(128)(2,1)S(1)}, bf16[480]{0:T(512)(128)(2,1)S(1)}, u32[]{:S(2)}, u32[]{:S(2)}) collective-permute-start(bf16[480]{0:T(512)(128)(2,1)S(1)} %get-tuple-element.60), channel_id=1, source_target_pairs={{8,0},{16,8},{24,16},{32,24},{40,32},{48,40},{56,48},{64,56},{72,6... | collective-permute-start | bytes 2888 | tf_op jit(solution)/shard_map/ppermute | solution.py:25
  26.3 15.3 %copy-start.8 = (f32[7,512]{1,0:T(8,128)S(1)}, f32[7,512]{1,0:T(8,128)}, u32[]{:S(2)}) copy-start(f32[7,512]{1,0:T(8,128)} %param.21) | copy-start | bytes 43012
  52.0 2.7 copy-start.12
  52.0 3.6 copy-start.11
  52.0 3.6 copy-start.13
  52.0 3.6 copy-start.15
  55.6 3.8 copy-start.6
  55.6 3.8 copy-start.7
  55.6 3.8 copy-start.14
  59.5 1.4 copy-start.2
  59.5 1.4 copy-start.9
  73.3 0.9 copy-start.4
  75.4 16.3 %collective-permute-start.4 = (bf16[3,512]{1,0:T(4,128)(2,1)S(1)}, bf16[3,512]{1,0:T(4,128)(2,1)S(1)}, u32[]{:S(2)}, u32[]{:S(2)}) collective-permute-start(bf16[3,512]{1,0:T(4,128)(2,1)S(1)} %get-tuple-element.50), channel_id=1, source_target_pairs={{0,8},{8,16},{16,24},{24,32},{32,40},{40,48},{48,56},{56,64},{64,7... | collective-permute-start | bytes 9224 | tf_op jit(solution)/shard_map/ppermute | solution.py:22
  79.7 12.0 %collective-permute-start.5 = (bf16[3,512]{1,0:T(4,128)(2,1)S(1)}, bf16[3,512]{1,0:T(4,128)(2,1)S(1)}, u32[]{:S(2)}, u32[]{:S(2)}) collective-permute-start(bf16[3,512]{1,0:T(4,128)(2,1)S(1)} %get-tuple-element.51), channel_id=1, source_target_pairs={{8,0},{16,8},{24,16},{32,24},{40,32},{48,40},{56,48},{64,56},{72,6... | collective-permute-start | bytes 9224 | tf_op jit(solution)/shard_map/ppermute | solution.py:25
  88.4 3.4 copy-start.5
  91.8 0.8 copy-start.10
  150.1 0.7 copy-start.16
  420.5 46.2 %copy-start.1 = (bf16[512,1536]{1,0:T(8,128)(2,1)S(1)}, bf16[512,1536]{1,0:T(8,128)(2,1)}, u32[]{:S(2)}) copy-start(bf16[512,1536]{1,0:T(8,128)(2,1)} %param.25) | copy-start | bytes 4718596
Sparse Core Ops, SparseCore 0:
  150.3 265.4 all-reduce.5
where the time goes:
time: 477 us; the launch traced here: 474 us
  waiting for transfers between devices  264 us (55%)
  local copies, waits for them, and re-layouts  88.8 us (19%)
  blocking collectives  37.7 us (8%)
  other arithmetic  32.8 us (7%)
  matrix products  20 us (4%)
  between operations  16 us (3%)
  starting transfers between devices  14.5 us (3%)
    unnamed x2, waiting for transfers between devices  264 us
    unnamed x53, local copies, waits for them, and re-layouts  42 us
    all_to_all x1, blocking collectives, from_everyone(): return lax.all_to_all(copies, axis, split_axis=0, concat_axis=0, tiled=True)  37.7 us
    another operation x1, other arithmetic  15.2 us
    ppermute x3, starting transfers between devices, padded_2(): lax.ppermute(lax.slice_in_dim(block, block.shape[dim] - width, None, axis...  10.4 us
    another operation x3, local copies, waits for them, and re-layouts, sum_together(): lines = jnp.concatenate([b.reshape(size, -1) for b in parts], axis=1)  9.96 us
  transfers between devices with their start and end apart: 7, of which 1 were waited for; matrix products, arithmetic and copies ran while one was open for 10% of the time, Pallas kernels for 0%

commit v1 on v0

v1 whole, which is shorter than its diff:
```python
import jax
import jax.numpy as jnp
import numpy as np
from jax import lax
from jax.experimental import pallas as pl
from jax.experimental.pallas import tpu as pltpu
from jax.sharding import PartitionSpec as P

D = 512
FF = 1536
Q = 8
KERNEL = 7
NFFT = 1280
HOP = 320
BINS = 640
PAD = 480
EPSILON = 1e-06
HALF = 3.5

FRAMES = 256
PAIRS = FRAMES // 2
ROWS = FRAMES + 16
LEFT = 24
SUB = 72
TAB = 1472
f32 = jnp.float32
bf16 = jnp.bfloat16


def tables():
    n = np.arange(16)[:, None]
    k = np.arange(BINS)[None, :]
    turn = 2.0 * np.pi / NFFT
    out = np.zeros((40, BINS), np.float64)
    out[0:16] = np.cos(turn * (n * k % NFFT))
    out[16:32] = np.sin(turn * (n * k % NFFT))
    out[32] = np.cos(turn * (16 * k[0] % NFFT))
    out[33] = np.sin(turn * (16 * k[0] % NFFT))
    out[34] = np.where(k[0] == 0, 1.0, 2.0) / NFFT
    out[35] = np.where(k[0] == 0, 0.0, -2.0) / NFFT
    return out.astype(np.float32)


def edges():
    def square(i):
        return np.where((i >= 0) & (i < NFFT), (0.5 - 0.5 * np.cos(2.0 * np.pi / NFFT * i)) ** 2, 0.0)

    s = np.arange(512)
    first = sum(square(s + PAD - HOP * t) for t in range(4))
    last = sum(square(s - 32 + HOP * t) for t in range(1, 5))
    out = np.zeros((8, 128), np.float64)
    out[0:4] = (1.0 / first).reshape(4, 128)
    out[4:8] = (1.0 / last).reshape(4, 128)
    return out.astype(np.float32)


def dot(a, b):
    return lax.dot_general(a, b, (((1,), (0,)), ((), ())), preferred_element_type=f32)


def dot_rows(a, b):
    return lax.dot_general(a, b, (((0,), (0,)), ((), ())), preferred_element_type=f32)


def dot_cols(a, b):
    return lax.dot_general(a, b, (((1,), (1,)), ((), ())), preferred_element_type=f32)


def sine_cosine(p):
    k = jnp.round(p * np.float32(2.0 / np.pi))
    r = p - k * np.float32(1.5703125)
    r = r - k * np.float32(4.837512969970703125e-4)
    r = r - k * np.float32(7.54978995489188216e-8)
    z = r * r
    s = r + r * z * (np.float32(-1.6666654611e-1) + z * (np.float32(8.3321608736e-3) + z * np.float32(-1.9515295891e-4)))
    c = 1.0 - 0.5 * z + z * z * (
        np.float32(4.166664568298827e-2) + z * (np.float32(-1.388731625493765e-3) + z * np.float32(2.443315711809948e-5))
    )
    q = k.astype(jnp.int32)
    odd = (q & 1) == 1
    sine = jnp.where(odd, c, s)
    cosine = jnp.where(odd, s, c)
    sine = jnp.where((q & 2) == 2, -sine, sine)
    cosine = jnp.where(((q + 1) & 2) == 2, -cosine, cosine)
    return sine, cosine


def split3(w):
    hi = w.astype(bf16)
    rest = w - hi.astype(f32)
    mid = rest.astype(bf16)
    low = (rest - mid.astype(f32)).astype(bf16)
    return hi, mid, low


def local_kernel(
    pos, codes, cot, left, right, embed_w, embed_b, depth_k, depth_b, gain, bias, up_w, up_b, down_w, down_b,
    scale, head_w, head_b, trig, edge, out,
    tab, feat, conv, cgrad, latg, samp, pair_rows, spec_in, xhat, rstd, normed, hid, dgelu, act, branch, latent, re, im,
    logit_low, low, big, spec, lg, row_sums, sums, tiles,
):
    first_frame, length = pos[0], pos[1]
    last_frame = pos[2]

    tab[0:96, :] = jnp.zeros((96, NFFT), bf16)
    tab[1376:TAB, :] = jnp.zeros((TAB - 1376, NFFT), bf16)
    cs, sn = trig[32:33, :], trig[33:34, :]
    real_row, imag_row = trig[34:35, :], trig[35:36, :]

    def table_step(i, carry):
        c, s = carry
        window = 0.5 - 0.5 * c[:, 1:2]
        at = pl.multiple_of(96 + i * 16, 16)
        tab[pl.ds(at, 16), 0:BINS] = (c * (window * real_row)).astype(bf16)
        tab[pl.ds(at, 16), BINS:] = (s * (window * imag_row)).astype(bf16)
        return c * cs - s * sn, s * cs + c * sn

    lax.fori_loop(0, NFFT // 16, table_step, (trig[0:16, :], trig[16:32, :]))

    w_hi, w_mid, w_low = split3(embed_w[...])

    def project(c):
        c = c.astype(bf16)
        return (dot_rows(c, w_hi) + dot_rows(c, w_mid) + dot_rows(c, w_low)) * np.float32(1.0 / HALF) + embed_b[...]

    own_codes = codes[...].astype(f32) - HALF
    feat[0:16, :] = jnp.zeros((16, D), f32)
    feat[16 + FRAMES :, :] = jnp.zeros((feat.shape[0] - 16 - FRAMES, D), f32)
    feat[16 : 16 + FRAMES, :] = project(own_codes)
    feat[8:16, :] = project(left[LEFT:, :].astype(f32) - HALF)[120:128, :]
    feat[16 + FRAMES : 24 + FRAMES, :] = project(right[LEFT:, :].astype(f32) - HALF)[0:8, :]

    def mask_step(i, _):
        at = pl.multiple_of(8 + i * 8, 8)
        frame = first_frame + (at - 16) + lax.broadcasted_iota(jnp.int32, (8, D), 0)
        keep = (frame >= 0) & (frame < length)
        feat[pl.ds(at, 8), :] = jnp.where(keep, feat[pl.ds(at, 8), :], 0.0).astype(bf16).astype(f32)
        return 0

    lax.fori_loop(0, (FRAMES + 16) // 8, mask_step, 0)

    taps = [depth_k[j : j + 1, :] for j in range(KERNEL)]
    total = jnp.broadcast_to(depth_b[...], (FRAMES + 16, D))
    for j in range(KERNEL):
        total = total + taps[j] * feat[5 + j : 5 + j + FRAMES + 16, :]
    conv[...] = total

    def to_rows(ref, base, dst):
        dst[0:FRAMES, :] = ref[base : base + FRAMES, :]
        dst[FRAMES : FRAMES + 8, :] = ref[base - 8 : base, :]
        dst[FRAMES + 8 :, :] = ref[base + FRAMES : base + FRAMES + 8, :]

    to_rows(conv, 8, xhat)

    def norm_step(i, _):
        at = pl.ds(pl.multiple_of(i * 16, 16), 16)
        x = xhat[at, :]
        centre = x - jnp.mean(x, axis=1, keepdims=True)
        r = lax.rsqrt(jnp.mean(centre * centre, axis=1, keepdims=True) + EPSILON)
        x = centre * r
        xhat[at, :] = x
        rstd[at, :] = jnp.broadcast_to(r, (16, 128))
        normed[at, :] = (x * gain[...] + bias[...]).astype(bf16)
        return 0

    lax.fori_loop(0, ROWS // 16, norm_step, 0)

    hid[...] = dot(normed[...], up_w[...])

    def gelu_step(i, _):
        at = pl.ds(pl.multiple_of(i * 16, 16), 16)
        x = hid[at, :] + up_b[...]
        cdf = 0.5 + 0.5 * lax.erf(x * np.float32(0.7071067811865476))
        act[at, :] = (x * cdf).astype(bf16)
        dgelu[at, :] = cdf + x * (jnp.exp(-0.5 * x * x) * np.float32(0.3989422804014327))
        return 0

    lax.fori_loop(0, ROWS // 16, gelu_step, 0)

    branch[...] = dot(act[...], down_w[...]) + down_b[...]
    to_rows(feat, 16, lg)
    latent[...] = (lg[...] + scale[...] * branch[...]).astype(bf16)

    big[0:ROWS, 0:NFFT] = dot(latent[...], head_w[...])

    def head_step(i, _):
        at = pl.ds(pl.multiple_of(i * 16, 16), 16)
        magnitude = jnp.exp(big[at, 0:BINS] + head_b[:, 0:BINS])
        sine, cosine = sine_cosine(big[at, BINS:NFFT] + head_b[:, BINS:])
        re[at, :] = magnitude * cosine
        im[at, :] = magnitude * sine
        return 0

    lax.fori_loop(0, ROWS // 16, head_step, 0)

    samp[0:LEFT, :] = left[0:LEFT, :].astype(f32)
    samp[LEFT : LEFT + 640, :] = cot[...]
    samp[LEFT + 640 :, :] = right[0:LEFT, :].astype(f32)
    start = first_frame * HOP
    limit = length * HOP

    def sample_step(i, _):
        at = pl.multiple_of(i * 8, 8)
        row = at - LEFT + lax.broadcasted_iota(jnp.int32, (8, 128), 0)
        s = start + row * 128 + lax.broadcasted_iota(jnp.int32, (8, 128), 1)
        x = samp[pl.ds(at, 8), :] * np.float32(2.0 / 3.0)
        samp[pl.ds(at, 8), :] = jnp.where(s < limit, x, 0.0)
        return 0

    def fix(at, values):
        row = at - LEFT + lax.broadcasted_iota(jnp.int32, (4, 128), 0)
        s = start + row * 128 + lax.broadcasted_iota(jnp.int32, (4, 128), 1)
        samp[at : at + 4, :] = jnp.where(s < limit, cot[at - LEFT : at - LEFT + 4, :] * values, 0.0)

    lax.fori_loop(0, (LEFT * 2 + 640) // 8, sample_step, 0)

    @pl.when(first_frame == 0)
    def _():
        fix(LEFT, edge[0:4, :])

    @pl.when(first_frame + FRAMES == last_frame)
    def _():
        fix(LEFT + 636, edge[4:8, :])

    for d in range(3):
        for k in range(5):
            column = (d * 5 + k) * 128
            base = LEFT + (d - 1) * 5 + k
            spec_in[0:PAIRS, column : column + 128] = samp[pl.ds(base, PAIRS, stride=5), :].astype(bf16)
            pair_rows[0:2, column : column + 128] = samp[pl.ds(base - 10, 2, stride=5), :]
            pair_rows[2:4, column : column + 128] = samp[pl.ds(base + 640, 2, stride=5), :]
    pair_rows[4:16, :] = jnp.zeros((12, 1920), f32)
    spec_in[PAIRS : PAIRS + 16, :] = pair_rows[...].astype(bf16)

    even = dot(spec_in[:, 128:1536], tab[64:1472, :])
    odd = dot(spec_in[:, 384:1792], tab[0:1408, :])
    for t in range(10):
        column = slice(128 * t, 128 * t + 128)
        spec[t, FRAMES:, :] = jnp.zeros((16, 128), f32)
        for part, parity in ((even, 0), (odd, 1)):
            spec[t, pl.ds(parity, PAIRS, stride=2), :] = part[0:PAIRS, column]
            spec[t, pl.ds(FRAMES + 4 + parity, 4, stride=2), :] = part[PAIRS : PAIRS + 4, column]

    def logit_grad_of(at):
        das, dps = [], []
        for t in range(5):
            column = slice(128 * t, 128 * t + 128)
            g_re, g_im = spec[t, at, :], spec[t + 5, at, :]
            r, m = re[at, column], im[at, column]
            da = g_re * r + g_im * m
            dp = g_im * r - g_re * m
            logit_low[at, column] = da.astype(bf16)
            logit_low[at, BINS + 128 * t : BINS + 128 * t + 128] = dp.astype(bf16)
            das.append(da)
            dps.append(dp)
        return jnp.concatenate(das, axis=1), jnp.concatenate(dps, axis=1)

    def logit_step(i, carry):
        da, dp = logit_grad_of(pl.ds(pl.multiple_of(i * 16, 16), 16))
        return carry[0] + da[0:8] + da[8:16], carry[1] + dp[0:8] + dp[8:16]

    zero = jnp.zeros((8, BINS), f32)
    da, dp = lax.fori_loop(0, FRAMES // 16, logit_step, (zero, zero))
    logit_grad_of(pl.ds(FRAMES, 16))
    head_sum = jnp.concatenate([jnp.sum(da, axis=0, keepdims=True), jnp.sum(dp, axis=0, keepdims=True)], axis=1)
    for t in range(10):
        tiles[16 + t : 17 + t, :] = head_sum[:, 128 * t : 128 * t + 128]

    latg[...] = dot_cols(logit_low[...], head_w[...])

    def scatter(columns, height, row):
        def step(f, _):
            z, yl, c = f // 4, (f // 2) % 2, f % 2
            for j in range(columns):
                for h in range(height // 8):
                    o = row + j * height + h * 8
                    at = pl.multiple_of(f * height + h * 8, 8)
                    out[c, yl, o // SUB, z, o % SUB : o % SUB + 8, :] = big[pl.ds(at, 8), 128 * j : 128 * j + 128].astype(bf16)
            return 0

        lax.fori_loop(0, 32, step, 0)

    big[0:D, 0:NFFT] = dot_rows(latent[0:FRAMES, :], logit_low[0:FRAMES, :])
    scatter(10, 16, 192)

    def latent_step(i, carry):
        at = pl.ds(pl.multiple_of(i * 16, 16), 16)
        g = latg[at, :]
        low[at, :] = (scale[...] * g).astype(bf16)
        b = g * branch[at, :]
        return carry[0] + b[0:8] + b[8:16], carry[1] + g[0:8] + g[8:16]

    zero = jnp.zeros((8, D), f32)
    scale_sum, latent_sum = lax.fori_loop(0, FRAMES // 16, latent_step, (zero, zero))
    low[FRAMES:, :] = (scale[...] * latg[FRAMES:, :]).astype(bf16)
    sums[20:21, :] = jnp.sum(scale_sum, axis=0, keepdims=True)
    sums[19:20, :] = jnp.sum(latent_sum, axis=0, keepdims=True) * scale[...]

    big[:, 0:D] = dot_rows(act[0:FRAMES, :], low[0:FRAMES, :])
    scatter(4, 48, 352)

    hid[...] = dot_cols(low[...], down_w[...])

    def hidden_grad_of(at):
        g = hid[at, :] * dgelu[at, :]
        act[at, :] = g.astype(bf16)
        return g

    def hidden_step(i, carry):
        g = hidden_grad_of(pl.ds(pl.multiple_of(i * 16, 16), 16))
        return carry + g[0:8] + g[8:16]

    up_sum = lax.fori_loop(0, FRAMES // 16, hidden_step, jnp.zeros((8, FF), f32))
    hidden_grad_of(pl.ds(FRAMES, 16))
    up_sum = jnp.sum(up_sum, axis=0, keepdims=True)
    for t in range(12):
        tiles[t : t + 1, :] = up_sum[:, 128 * t : 128 * t + 128]

    big[0:D, 0:FF] = dot_rows(normed[0:FRAMES, :], act[0:FRAMES, :])
    scatter(12, 16, 0)

    lg[...] = dot_cols(act[...], up_w[...])

    def norm_grad_of(at):
        g, x = lg[at, :], xhat[at, :]
        dx = g * gain[...]
        m1 = jnp.mean(dx, axis=1, keepdims=True)
        m2 = jnp.mean(dx * x, axis=1, keepdims=True)
        lg[at, :] = rstd[at, 0:1] * (dx - m1 - x * m2)
        return g, g * x

    def norm_grad_step(i, carry):
        g, gx = norm_grad_of(pl.ds(pl.multiple_of(i * 16, 16), 16))
        return carry[0] + g[0:8] + g[8:16], carry[1] + gx[0:8] + gx[8:16]

    bias_sum, gain_sum = lax.fori_loop(0, FRAMES // 16, norm_grad_step, (zero, zero))
    norm_grad_of(pl.ds(FRAMES, 16))
    sums[17:18, :] = jnp.sum(gain_sum, axis=0, keepdims=True)
    sums[18:19, :] = jnp.sum(bias_sum, axis=0, keepdims=True)

    i = lax.broadcasted_iota(jnp.int32, (16, D), 0)
    frame = jnp.where(i < 8, i - 8, i + (FRAMES - 8)) + first_frame
    inside = (frame >= 0) & (frame < last_frame)
    edge_rows = jnp.where(inside, lg[FRAMES:, :], 0.0)

    cgrad[0:8, :] = edge_rows[0:8]
    cgrad[8 : 8 + FRAMES, :] = lg[0:FRAMES, :]
    cgrad[8 + FRAMES :, :] = edge_rows[8:16]

    own = cgrad[8 : 8 + FRAMES, :]
    sums[16:17, :] = jnp.sum(own, axis=0, keepdims=True)
    total = latg[0:FRAMES, :]
    for j in range(KERNEL):
        sums[9 + j : 10 + j, :] = jnp.sum(own * feat[13 + j : 13 + j + FRAMES, :], axis=0, keepdims=True)
        total = total + taps[j] * cgrad[11 - j : 11 - j + FRAMES, :]
    frame = first_frame + lax.broadcasted_iota(jnp.int32, (FRAMES, D), 0)
    total = jnp.where(frame < length, total, 0.0)
    sums[8:9, :] = jnp.sum(total, axis=0, keepdims=True)
    hi, mid, rest = split3(total)
    own_low = own_codes.astype(bf16)
    sums[0:8, :] = (dot(own_low, hi) + dot(own_low, mid) + dot(own_low, rest)) * np.float32(1.0 / HALF)
    sums[21:24, :] = jnp.zeros((3, D), f32)

    def small_step(f, _):
        z, yl, c = f // 4, (f // 2) % 2, f % 2
        row_sums[...] = jnp.zeros((8, 128), f32)
        row_sums[0:2, :] = tiles[pl.ds((48 * f) // 128, 2), :]
        row_sums[2:4, :] = tiles[pl.ds(16 + (40 * f) // 128, 2), :]
        out[c, yl, 7, z, 64:72, :] = row_sums[...].astype(bf16)
        return 0

    tiles[12:16, :] = jnp.zeros((4, 128), f32)
    tiles[26:32, :] = jnp.zeros((6, 128), f32)
    lax.fori_loop(0, 32, small_step, 0)
    for f in range(32):
        column = 128 * (f // 8)
        out[f % 2, (f // 2) % 2, 7, f // 4, 40:64, :] = sums[:, column : column + 128].astype(bf16)


def local_grads(pos, codes, cot, left, right, weights):
    vmem = pltpu.VMEM
    scratch = [
        vmem((TAB, NFFT), bf16),
        vmem((FRAMES + 32, D), f32),
        vmem((FRAMES + 16, D), f32),
        vmem((FRAMES + 16, D), f32),
        vmem((ROWS, D), f32),
        vmem((640 + 2 * LEFT, 128), f32),
        vmem((16, 1920), f32),
        vmem((PAIRS + 16, 1920), bf16),
        vmem((ROWS, D), f32),
        vmem((ROWS, 128), f32),
        vmem((ROWS, D), bf16),
        vmem((ROWS, FF), f32),
        vmem((ROWS, FF), f32),
        vmem((ROWS, FF), bf16),
        vmem((ROWS, D), f32),
        vmem((ROWS, D), bf16),
        vmem((ROWS, BINS), f32),
        vmem((ROWS, BINS), f32),
        vmem((ROWS, NFFT), bf16),
        vmem((ROWS, D), bf16),
        vmem((FF, FF), f32),
        vmem((10, ROWS, 128), f32),
        vmem((ROWS, D), f32),
        vmem((8, 128), f32),
        vmem((24, D), f32),
        vmem((32, 128), f32),
    ]
    whole = pl.BlockSpec(memory_space=pltpu.VMEM)
    arrays = [codes, cot, left, right, *weights, jnp.asarray(tables()), jnp.asarray(edges())]
    return pl.pallas_call(
        local_kernel,
        out_shape=jax.ShapeDtypeStruct((2, 2, 8, 8, SUB, 128), bf16),
        in_specs=[pl.BlockSpec(memory_space=pltpu.SMEM)] + [whole] * len(arrays),
        out_specs=whole,
        scratch_shapes=scratch,
        compiler_params=pltpu.CompilerParams(vmem_limit_bytes=56 * 1024 * 1024),
        name="local_grads",
    )(pos, *arrays)


def unpack_kernel(pos, t, up_g, head_g, down_g, embed_w, embed_b, depth_k, vectors, up_b, head_b):
    f = pos[0]

    def tile(o):
        return t[o // SUB, o % SUB : o % SUB + 8, :]

    for columns, height, row, ref in ((12, 16, 0, up_g), (10, 16, 192, head_g), (4, 48, 352, down_g)):
        for j in range(columns):
            for h in range(height // 8):
                ref[h * 8 : h * 8 + 8, 128 * j : 128 * j + 128] = tile(row + j * height + h * 8)
    shift = 16 * (f % 8)
    back = lax.rem(128 - shift, 128)

    def rolled(x, by):
        return pltpu.roll(x, by, 1)

    embed_w[...] = rolled(tile(544), back)[:, 0:16]
    second = rolled(tile(552), back)
    third = rolled(tile(560), back)
    embed_b[...] = second[0:1, 0:16]
    depth_k[...] = second[1:8, 0:16]
    vectors[...] = third[0:8, 0:16]
    last = tile(568)
    lane = lax.broadcasted_iota(jnp.int32, (1, 128), 1)
    for row, width, ref in ((0, 48, up_b), (2, 40, head_b)):
        shift = lax.rem(width * f, 128)
        back = lax.rem(128 - shift, 128)
        moved = rolled(last, back)
        joined = jnp.where(lane < 128 - shift, moved[row : row + 1, :], moved[row + 1 : row + 2, :])
        ref[...] = joined[:, 0:width]


def unpack(pos, t):
    def shape(*s):
        return jax.ShapeDtypeStruct(s, f32)

    whole = pl.BlockSpec(memory_space=pltpu.VMEM)
    return pl.pallas_call(
        unpack_kernel,
        out_shape=(
            shape(16, FF), shape(16, NFFT), shape(48, D), shape(8, 16), shape(1, 16), shape(7, 16), shape(8, 16), shape(1, 48), shape(1, 40),
        ),
        in_specs=[pl.BlockSpec(memory_space=pltpu.SMEM), whole],
        out_specs=(whole,) * 9,
        name="unpack",
    )(pos, t)


AXES = ("frame", "rec")


def index_of(z, yl, c, yh, x):
    return ((z * 2 + yl) * 2 + c) * 8 + yh * 4 + x


def groups_over(which):
    sizes = dict(z=8, yl=2, c=2, yh=2, x=4)
    kept = [n for n in sizes if n not in which]

    def walk(names, fixed):
        if not names:
            return [fixed]
        return [r for v in range(sizes[names[0]]) for r in walk(names[1:], {**fixed, names[0]: v})]

    return [[index_of(**g) for g in walk(list(which), fixed)] for fixed in walk(kept, {})]


def exchange(array, which):
    return lax.all_to_all(array, AXES, split_axis=0, concat_axis=0, axis_index_groups=groups_over(which), tiled=True)


def summed(array):
    return jnp.sum(array.astype(f32), axis=0)


def reduce_all(packed):
    both = exchange(packed.reshape(2, -1, 128), ("c",))
    half = summed(both).astype(bf16).reshape(16, 8 * SUB, 128)
    part = summed(exchange(half, ("yl", "yh", "x"))).astype(bf16).reshape(8, SUB, 128)
    mine = summed(exchange(part, ("z",)))
    return lax.all_to_all(jnp.broadcast_to(mine, (8, SUB, 128)), "rec", split_axis=0, concat_axis=0, tiled=True)


def body(code_indices, lengths, cotangent, *weights):
    count = lax.axis_size("frame")
    me = lax.axis_index("frame")
    codes = code_indices[0].T
    samples = cotangent[0].astype(f32).reshape(640, 128)
    low = samples.astype(bf16)
    codes_low = codes.astype(bf16)
    forward = [(i, i + 1) for i in range(count - 1)]
    backward = [(b, a) for a, b in forward]
    left = lax.ppermute(jnp.concatenate([low[640 - LEFT :], codes_low[:, FRAMES - 128 :]]), "frame", forward)
    right = lax.ppermute(jnp.concatenate([low[:LEFT], codes_low[:, :128]]), "frame", backward)
    pos = jnp.stack([me * FRAMES, lengths[0], count * FRAMES]).astype(jnp.int32)
    flat = [w if w.ndim == 2 else w[None] for w in weights]
    packed = local_grads(pos, codes, samples, left, right, flat)
    t = reduce_all(packed)
    up_g, head_g, down_g, embed_w, embed_b, depth_k, vectors, up_b, head_b = unpack(me.astype(jnp.int32)[None], t)
    depth_b, gain, bias, down_b, scale = (vectors[i] for i in range(5))
    return (
        embed_w, embed_b[0], depth_k, depth_b, gain, bias, up_g, up_b[0], down_g, down_b, scale, head_g, head_b[0],
    )


def solution(mesh):
    return jax.shard_map(
        body,
        mesh=mesh,
        in_specs=(P("rec", "frame", None), P("rec"), P("rec", "frame")) + (P(),) * 13,
        out_specs=(
            P(None, "frame"), P("frame"), P(None, "frame"), P("frame"), P("frame"), P("frame"), P("frame", None),
            P("frame"), P("frame", None), P("frame"), P("frame"), P("frame", None), P("frame"),
        ),
        check_vma=False,
    )
```

time: 477 us -> 137 us (0.29)
  waiting for transfers between devices: 264 us -> 0.01 us
  local copies, waits for them, and re-layouts: 88.8 us -> 5.4 us
  blocking collectives: 37.7 us -> 84.7 us
  Pallas kernels: 0 us -> 33.3 us
  other arithmetic: 32.8 us -> 8.79 us
  matrix products: 20 us -> 0 us
  between operations: 16 us -> 1.36 us
  starting transfers between devices: 14.5 us -> 3.03 us
    unnamed x2 -> x0, waiting for transfers between devices: 264 us -> none
    all_to_all x1 -> x4, blocking collectives: 37.7 us -> 84.7 us  [the longest x3 72.4 us: exchange(): lax.all_to_all(array, AXES, split_axis=0, concat_axis=0, axis_index_group...]
    unnamed x53 -> x4, local copies, waits for them, and re-layouts: 42 us -> 0.59 us
    pallas_call x0 -> x2, Pallas kernels: none -> 33.3 us  [the longest x1 31.6 us: local_grads(): pl.pallas_call(local_kernel, out_shape=jax.ShapeDtypeStruct((2, 2, 8, 8,...]
    dot_general x12 -> x0, matrix products: 20 us -> none  [the longest x4 8 us: contract_rows(): lax.dot_general(former, latter, (((0,), (0,)), ((), ())), precision=preci...]
    another operation x1, other arithmetic: 15.2 us -> 0.59 us  [body(): pos = jnp.stack([me * FRAMES, lengths[0], count * FRAMES]).astype(jnp.int32)]
    reshape x17 -> x0, local copies, waits for them, and re-layouts: 12.7 us -> none  [the longest x1 7.73 us: sum_together(): jnp.pad(lines, ((0, 0), (0, extent * 128 - lines.shape[1])))]
    ppermute x6 -> x2, starting transfers between devices: 14.4 us -> 3.03 us  [the longest x1 1.74 us: body(): lax.ppermute(jnp.concatenate([low[640 - LEFT:], codes_low[:, FRAMES - 128...]
  transfers between devices with their start and end apart: 7 -> 2, of which waited for: 1 -> 0; matrix products, arithmetic and copies ran while one was open for 10% -> 4% of each run, Pallas kernels for 0% -> 0%
where the time goes in v1:
time: 137 us
  blocking collectives  84.7 us (62%)
  Pallas kernels  33.3 us (24%)
  other arithmetic  8.79 us (6%)
  local copies, waits for them, and re-layouts  5.4 us (4%)
  starting transfers between devices  3.03 us (2%)
    all_to_all x3, blocking collectives, exchange(): lax.all_to_all(array, AXES, split_axis=0, concat_axis=0, axis_index_group...  72.4 us
    pallas_call x1, Pallas kernels, local_grads(): pl.pallas_call(local_kernel, out_shape=jax.ShapeDtypeStruct((2, 2, 8, 8,...  31.6 us
    all_to_all x1, blocking collectives, reduce_all(): lax.all_to_all(jnp.broadcast_to(mine, (8, SUB, 128)), 'rec', split_axis=0...  12.3 us
    reduce_sum x3, other arithmetic, summed(): return jnp.sum(array.astype(f32), axis=0)  5.45 us
  transfers between devices with their start and end apart: 2, of which 0 were waited for; matrix products, arithmetic and copies ran while one was open for 4% of the time, Pallas kernels for 0%

profile of v1, /device:TPU:2, one launch (start us, length us, event | category | flops | bytes accessed | tf_op | source)
XLA Modules:
  0.0 136.6 jit_solution(8154724647023482713)
XLA Ops:
  0.6 0.7 bitcast_convert_fusion
  1.4 0.8 slice_reduce_fusion
  2.2 1.7 %collective-permute-start = (bf16[32,128]{1,0:T(8,128)(2,1)S(1)}, bf16[32,128]{1,0:T(8,128)(2,1)S(1)}, u32[]{:S(2)}, u32[]{:S(2)}) collective-permute-start(bf16[32,128]{1,0:T(8,128)(2,1)S(1)} %pad_maximum_fusion), channel_id=1, source_target_pairs={{0,8},{8,16},{16,24},{24,32},{32,40},{40,48},{48,56},{56,64},{64,7... | collective-permute-start | bytes 24584 | tf_op jit(solution)/shard_map/ppermute | solution.py:515
  3.9 1.3 collective-permute-start.1
  5.9 0.6 pad_add_fusion.pos
  6.5 2.0 %convert_element_type.22 = f32[1,81920]{1,0:T(1,128)} convert(bf16[1,81920]{1,0:T(2,128)(2,1)} %param.20) | non-fusion elementwise | flops 81920 | bytes 491520 | tf_op jit(solution)/shard_map/convert_element_type | solution.py:510
  8.5 1.3 broadcast_in_dim.38.head_b
  9.8 1.3 broadcast_in_dim.35.up_b
  11.1 0.0 collective-permute-done.left
  11.1 0.0 copy-start
  11.1 0.0 collective-permute-done.1.right
  11.1 0.0 copy-start.1
  11.1 0.6 copy-done
  11.7 0.0 copy-done.1
  11.7 31.6 %local_grads.1 = bf16[2,2,8,8,72,128]{5,4,3,2,1,0:T(8,128)(2,1)} custom-call(s32[3]{0:T(128)} %pad_add_fusion.pos, s32[8,256]{1,0:T(8,128)} %bitcast.35, f32[640,128]{1,0:T(8,128)} %bitcast.33, bf16[32,128]{1,0:T(8,128)(2,1)} %copy-done, bf16[32,128]{1,0:T(8,128)(2,1)} %copy-done.1, f32[8,512]{1,0:T(8,128)} %embed_w.1, f32[1,512]{1,0:T(1,128)} %bitcast.38, ...), custom_call_target="tpu_custom_call" | custom-call | tf_op jit(solution)/shard_map/local_grads/pallas_call | solution.py:412
  43.3 14.7 %all_to_all.20 = bf16[2,9216,128]{2,1,0:T(8,128)(2,1)} all-to-all(bf16[2,9216,128]{2,1,0:T(8,128)(2,1)} %bitcast.31), channel_id=1, replica_groups={{0,8},{1,9},{2,10},{3,11},{4,12},{5,13},{6,14},{7,15},{16,24},{17,25},{..., dimensions={0} | all-to-all | bytes 9437184 | tf_op jit(solution)/shard_map/all_to_all | solution.py:491
  58.0 3.4 %reduce_sum.33 = bf16[9216,128]{1,0:T(8,128)(2,1)S(1)} reduce(bf16[2,9216,128]{2,1,0:T(8,128)(2,1)} %all_to_all.20, bf16[]{:T(256)} %constant.17.clone.1), dimensions={0}, to_apply=%region_0.0 | reduce | flops 1179648 | bytes 7077890 | tf_op jit(solution)/shard_map/reduce_sum | solution.py:495
  61.5 37.9 %all_to_all.21 = bf16[16,576,128]{2,1,0:T(8,128)(2,1)} all-to-all(bf16[16,576,128]{2,1,0:T(8,128)(2,1)S(1)} %bitcast.32), channel_id=1, replica_groups={{0,1,2,3,4,5,6,7,16,17,18,19,20,21,22,23},{8,9,10,11,12,13,14,15,24,25,..., dimensions={0} | all-to-all | bytes 4718592 | tf_op jit(solution)/shard_map/all_to_all | solution.py:491
  99.3 2.0 %reduce_sum.34 = bf16[576,128]{1,0:T(8,128)(2,1)S(1)} reduce(bf16[16,576,128]{2,1,0:T(8,128)(2,1)} %all_to_all.21, bf16[]{:T(256)} %constant.17.clone.1), dimensions={0}, to_apply=%region_1.0 | reduce | flops 1105920 | bytes 2506754 | tf_op jit(solution)/shard_map/reduce_sum | solution.py:495
  101.3 19.8 %all_to_all.22 = bf16[8,72,128]{2,1,0:T(8,128)(2,1)S(1)} all-to-all(bf16[8,72,128]{2,1,0:T(8,128)(2,1)S(1)} %bitcast.34), channel_id=1, replica_groups={{0,32,64,96,128,160,192,224},{1,33,65,97,129,161,193,225},{2,34,66,98,1..., dimensions={0} | all-to-all | bytes 294912 | tf_op jit(solution)/shard_map/all_to_all | solution.py:491
  121.2 12.3 %all_to_all.23.t = f32[8,72,128]{2,1,0:T(8,128)} all-to-all(f32[8,72,128]{2,1,0:T(8,128)S(1)} %broadcast_in_dim.39), channel_id=1, replica_groups=mesh['frame'=32,'rec'=8] {'rec'}, dimensions={0} | all-to-all | bytes 589824 | tf_op jit(solution)/shard_map/all_to_all | solution.py:503
  133.5 1.7 %unpack.1 = (f32[16,1536]{1,0:T(8,128)}, f32[16,1280]{1,0:T(8,128)}, f32[48,512]{1,0:T(8,128)}, f32[8,16]{1,0:T(8,128)}, f32[1,16]{1,0:T(1,128)}, /*index=5*/f32...) custom-call(s32[1]{0:T(128)} %bitcast.pos, f32[8,72,128]{2,1,0:T(8,128)} %all_to_all.23.t), custom_call_target="tpu_custom_call" | custom-call | tf_op jit(solution)/shard_map/unpack/pallas_call | solution.py:460
  135.2 1.4 %slice_bitcast_fusion = (f32[16]{0:T(128)}, f32[16]{0:T(128)}, f32[16]{0:T(128)}, f32[16]{0:T(128)}, f32[16]{0:T(128)}) fusion(f32[8,16]{1,0:T(8,128)} %get-tuple-element.25), kind=kLoop, calls=%fused_computation.6 | loop fusion | bytes 640 | tf_op jit(solution)/shard_map/squeeze | solution.py:522
  (5 shorter events, 0.1 us)
Async XLA Ops:
  2.2 8.9 %collective-permute-start = (bf16[32,128]{1,0:T(8,128)(2,1)S(1)}, bf16[32,128]{1,0:T(8,128)(2,1)S(1)}, u32[]{:S(2)}, u32[]{:S(2)}) collective-permute-start(bf16[32,128]{1,0:T(8,128)(2,1)S(1)} %pad_maximum_fusion), channel_id=1, source_target_pairs={{0,8},{8,16},{16,24},{24,32},{32,40},{40,48},{48,56},{56,64},{64,7... | collective-permute-start | bytes 24584 | tf_op jit(solution)/shard_map/ppermute | solution.py:515
  3.9 7.2 %collective-permute-start.1 = (bf16[32,128]{1,0:T(8,128)(2,1)S(1)}, bf16[32,128]{1,0:T(8,128)(2,1)S(1)}, u32[]{:S(2)}, u32[]{:S(2)}) collective-permute-start(bf16[32,128]{1,0:T(8,128)(2,1)S(1)} %pad_maximum_fusion.1), channel_id=1, source_target_pairs={{8,0},{16,8},{24,16},{32,24},{40,32},{48,40},{56,48},{64,56},{72,6... | collective-permute-start | bytes 24584 | tf_op jit(solution)/shard_map/ppermute | solution.py:516
  11.1 0.6 copy-start
  11.1 0.6 copy-start.1

commit v2 on v1

--- a/solution.py
+++ b/solution.py
@@ -95,12 +95,19 @@
 
 def local_kernel(
     pos, codes, cot, left, right, embed_w, embed_b, depth_k, depth_b, gain, bias, up_w, up_b, down_w, down_b,
-    scale, head_w, head_b, trig, edge, out,
+    scale, head_w, head_b, trig, edge, keep, send,
     tab, feat, conv, cgrad, latg, samp, pair_rows, spec_in, xhat, rstd, normed, hid, dgelu, act, branch, latent, re, im,
-    logit_low, low, big, spec, lg, row_sums, sums, tiles,
+    logit_low, low, big, spec, lg, row_sums, sums, tiles, tall, rows,
 ):
     first_frame, length = pos[0], pos[1]
     last_frame = pos[2]
+    core = pos[3]
+
+    for t in range(FF // 128):
+        rows[0:1, 128 * t : 128 * t + 128] = up_b[t : t + 1, :]
+    for t in range(NFFT // 128):
+        rows[1:2, 128 * t : 128 * t + 128] = head_b[t : t + 1, :]
+    up_row, head_row = rows[0:1, :], rows[1:2, 0:NFFT]
 
     tab[0:96, :] = jnp.zeros((96, NFFT), bf16)
     tab[1376:TAB, :] = jnp.zeros((TAB - 1376, NFFT), bf16)
@@ -169,7 +176,7 @@
 
     def gelu_step(i, _):
         at = pl.ds(pl.multiple_of(i * 16, 16), 16)
-        x = hid[at, :] + up_b[...]
+        x = hid[at, :] + up_row
         cdf = 0.5 + 0.5 * lax.erf(x * np.float32(0.7071067811865476))
         act[at, :] = (x * cdf).astype(bf16)
         dgelu[at, :] = cdf + x * (jnp.exp(-0.5 * x * x) * np.float32(0.3989422804014327))
@@ -185,8 +192,8 @@
 
     def head_step(i, _):
         at = pl.ds(pl.multiple_of(i * 16, 16), 16)
-        magnitude = jnp.exp(big[at, 0:BINS] + head_b[:, 0:BINS])
-        sine, cosine = sine_cosine(big[at, BINS:NFFT] + head_b[:, BINS:])
+        magnitude = jnp.exp(big[at, 0:BINS] + head_row[:, 0:BINS])
+        sine, cosine = sine_cosine(big[at, BINS:NFFT] + head_row[:, BINS:])
         re[at, :] = magnitude * cosine
         im[at, :] = magnitude * sine
         return 0
@@ -268,20 +275,22 @@
 
     latg[...] = dot_cols(logit_low[...], head_w[...])
 
-    def scatter(columns, height, row):
-        def step(f, _):
-            z, yl, c = f // 4, (f // 2) % 2, f % 2
-            for j in range(columns):
-                for h in range(height // 8):
-                    o = row + j * height + h * 8
-                    at = pl.multiple_of(f * height + h * 8, 8)
-                    out[c, yl, o // SUB, z, o % SUB : o % SUB + 8, :] = big[pl.ds(at, 8), 128 * j : 128 * j + 128].astype(bf16)
+    def scatter(big_ref, columns, height, row):
+        def step(p, _):
+            z, yl = p // 2, p % 2
+            for ref, f in ((keep, 2 * p + core), (send, 2 * p + 1 - core)):
+                for j in range(columns):
+                    for h in range(height // 8):
+                        o = row + j * height + h * 8
+                        at = pl.multiple_of(f * height + h * 8, 8)
+                        value = big_ref[pl.ds(at, 8), 128 * j : 128 * j + 128].astype(bf16)
+                        ref[yl, o // SUB, z, o % SUB : o % SUB + 8, :] = value
             return 0
 
-        lax.fori_loop(0, 32, step, 0)
+        lax.fori_loop(0, 16, step, 0)
 
     big[0:D, 0:NFFT] = dot_rows(latent[0:FRAMES, :], logit_low[0:FRAMES, :])
-    scatter(10, 16, 192)
+    scatter(big, 10, 16, 192)
 
     def latent_step(i, carry):
         at = pl.ds(pl.multiple_of(i * 16, 16), 16)
@@ -296,8 +305,8 @@
     sums[20:21, :] = jnp.sum(scale_sum, axis=0, keepdims=True)
     sums[19:20, :] = jnp.sum(latent_sum, axis=0, keepdims=True) * scale[...]
 
-    big[:, 0:D] = dot_rows(act[0:FRAMES, :], low[0:FRAMES, :])
-    scatter(4, 48, 352)
+    tall[...] = dot_rows(act[0:FRAMES, :], low[0:FRAMES, :])
+    scatter(tall, 4, 48, 352)
 
     hid[...] = dot_cols(low[...], down_w[...])
 
@@ -317,7 +326,7 @@
         tiles[t : t + 1, :] = up_sum[:, 128 * t : 128 * t + 128]
 
     big[0:D, 0:FF] = dot_rows(normed[0:FRAMES, :], act[0:FRAMES, :])
-    scatter(12, 16, 0)
+    scatter(big, 12, 16, 0)
 
     lg[...] = dot_cols(act[...], up_w[...])
 
@@ -361,20 +370,24 @@
     sums[0:8, :] = (dot(own_low, hi) + dot(own_low, mid) + dot(own_low, rest)) * np.float32(1.0 / HALF)
     sums[21:24, :] = jnp.zeros((3, D), f32)
 
-    def small_step(f, _):
-        z, yl, c = f // 4, (f // 2) % 2, f % 2
-        row_sums[...] = jnp.zeros((8, 128), f32)
-        row_sums[0:2, :] = tiles[pl.ds((48 * f) // 128, 2), :]
-        row_sums[2:4, :] = tiles[pl.ds(16 + (40 * f) // 128, 2), :]
-        out[c, yl, 7, z, 64:72, :] = row_sums[...].astype(bf16)
-        return 0
-
     tiles[12:16, :] = jnp.zeros((4, 128), f32)
     tiles[26:32, :] = jnp.zeros((6, 128), f32)
-    lax.fori_loop(0, 32, small_step, 0)
-    for f in range(32):
-        column = 128 * (f // 8)
-        out[f % 2, (f // 2) % 2, 7, f // 4, 40:64, :] = sums[:, column : column + 128].astype(bf16)
+    row_sums[...] = jnp.zeros((8, 128), f32)
+
+    def small_step(p, _):
+        z, yl = p // 2, p % 2
+        for ref, f in ((keep, 2 * p + core), (send, 2 * p + 1 - core)):
+            row_sums[0:2, :] = tiles[pl.ds((48 * f) // 128, 2), :]
+            row_sums[2:4, :] = tiles[pl.ds(16 + (40 * f) // 128, 2), :]
+            ref[yl, 7, z, 64:72, :] = row_sums[...].astype(bf16)
+        return 0
+
+    lax.fori_loop(0, 16, small_step, 0)
+    for p in range(16):
+        column = 128 * (p // 4)
+        part = sums[:, column : column + 128].astype(bf16)
+        keep[p % 2, 7, p // 2, 40:64, :] = part
+        send[p % 2, 7, p // 2, 40:64, :] = part
 
 
 def local_grads(pos, codes, cot, left, right, weights):
@@ -400,22 +413,24 @@
         vmem((ROWS, BINS), f32),
         vmem((ROWS, NFFT), bf16),
         vmem((ROWS, D), bf16),
-        vmem((FF, FF), f32),
+        vmem((D, FF), f32),
         vmem((10, ROWS, 128), f32),
         vmem((ROWS, D), f32),
         vmem((8, 128), f32),
         vmem((24, D), f32),
         vmem((32, 128), f32),
+        vmem((FF, D), f32),
+        vmem((8, FF), f32),
     ]
     whole = pl.BlockSpec(memory_space=pltpu.VMEM)
     arrays = [codes, cot, left, right, *weights, jnp.asarray(tables()), jnp.asarray(edges())]
     return pl.pallas_call(
         local_kernel,
-        out_shape=jax.ShapeDtypeStruct((2, 2, 8, 8, SUB, 128), bf16),
+        out_shape=(jax.ShapeDtypeStruct((2, 8, 8, SUB, 128), bf16),) * 2,
         in_specs=[pl.BlockSpec(memory_space=pltpu.SMEM)] + [whole] * len(arrays),
-        out_specs=whole,
+        out_specs=(whole, whole),
         scratch_shapes=scratch,
-        compiler_params=pltpu.CompilerParams(vmem_limit_bytes=56 * 1024 * 1024),
+        compiler_params=pltpu.CompilerParams(vmem_limit_bytes=42 * 1024 * 1024),
         name="local_grads",
     )(pos, *arrays)
 
@@ -495,9 +510,10 @@
     return jnp.sum(array.astype(f32), axis=0)
 
 
-def reduce_all(packed):
-    both = exchange(packed.reshape(2, -1, 128), ("c",))
-    half = summed(both).astype(bf16).reshape(16, 8 * SUB, 128)
+def reduce_all(keep, send):
+    pairs = groups_over(("c",))
+    other = lax.ppermute(send, AXES, [(a, b) for a, b in pairs] + [(b, a) for a, b in pairs])
+    half = (keep.astype(f32) + other.astype(f32)).astype(bf16).reshape(16, 8 * SUB, 128)
     part = summed(exchange(half, ("yl", "yh", "x"))).astype(bf16).reshape(8, SUB, 128)
     mine = summed(exchange(part, ("z",)))
     return lax.all_to_all(jnp.broadcast_to(mine, (8, SUB, 128)), "rec", split_axis=0, concat_axis=0, tiled=True)
@@ -514,10 +530,9 @@
     backward = [(b, a) for a, b in forward]
     left = lax.ppermute(jnp.concatenate([low[640 - LEFT :], codes_low[:, FRAMES - 128 :]]), "frame", forward)
     right = lax.ppermute(jnp.concatenate([low[:LEFT], codes_low[:, :128]]), "frame", backward)
-    pos = jnp.stack([me * FRAMES, lengths[0], count * FRAMES]).astype(jnp.int32)
-    flat = [w if w.ndim == 2 else w[None] for w in weights]
-    packed = local_grads(pos, codes, samples, left, right, flat)
-    t = reduce_all(packed)
+    pos = jnp.stack([me * FRAMES, lengths[0], count * FRAMES, me % 2]).astype(jnp.int32)
+    flat = [w if w.ndim == 2 else w[None] if w.size == D else w.reshape(-1, 128) for w in weights]
+    t = reduce_all(*local_grads(pos, codes, samples, left, right, flat))
     up_g, head_g, down_g, embed_w, embed_b, depth_k, vectors, up_b, head_b = unpack(me.astype(jnp.int32)[None], t)
     depth_b, gain, bias, down_b, scale = (vectors[i] for i in range(5))
     return (

time: 137 us -> 129 us (0.942)
  blocking collectives: 84.7 us -> 68.8 us
  local copies, waits for them, and re-layouts: 5.4 us -> 15.5 us
  other arithmetic: 8.79 us -> 3.09 us
  Pallas kernels: 33.3 us -> 27.9 us
  waiting for transfers between devices: 0.01 us -> 5.23 us
  starting transfers between devices: 3.03 us -> 5.52 us
    all_to_all x3 -> x2, blocking collectives: 72.4 us -> 56.5 us  [exchange(): lax.all_to_all(array, AXES, split_axis=0, concat_axis=0, axis_index_group...]
    unnamed x4 -> x32, local copies, waits for them, and re-layouts: 0.59 us -> 13.3 us
    pallas_call x1, Pallas kernels: 31.6 us -> 26.2 us  [local_grads(): pl.pallas_call(local_kernel, out_shape=(jax.ShapeDtypeStruct((2, 8, 8, SU...]
    reduce_sum x3 -> x2, other arithmetic: 5.45 us -> 0.36 us  [summed(): return jnp.sum(array.astype(f32), axis=0)]
    ppermute x0 -> x1, waiting for transfers between devices: none -> 4.16 us  [reduce_all(): lax.ppermute(send, AXES, [(a, b) for a, b in pairs] + [(b, a) for a, b in...]
    broadcast_in_dim x2 -> x0, local copies, waits for them, and re-layouts: 2.59 us -> none  [body(): flat = [w if w.ndim == 2 else w[None] for w in weights]]
    ppermute x0 -> x1, starting transfers between devices: none -> 2.49 us  [reduce_all(): lax.ppermute(send, AXES, [(a, b) for a, b in pairs] + [(b, a) for a, b in...]
  transfers between devices with their start and end apart: 2 -> 3, of which waited for: 0 -> 2; matrix products, arithmetic and copies ran while one was open for 4% -> 1% of each run, Pallas kernels for 0% -> 0%
where the time goes in v2:
time: 129 us; the launch traced here: 127 us
  blocking collectives  68.8 us (53%)
  Pallas kernels  27.9 us (22%)
  local copies, waits for them, and re-layouts  15.5 us (12%)
  starting transfers between devices  5.52 us (4%)
  waiting for transfers between devices  5.23 us (4%)
  other arithmetic  3.09 us (2%)
  between operations  1.39 us (1%)
    all_to_all x2, blocking collectives, exchange(): lax.all_to_all(array, AXES, split_axis=0, concat_axis=0, axis_index_group...  56.5 us
    pallas_call x1, Pallas kernels, local_grads(): pl.pallas_call(local_kernel, out_shape=(jax.ShapeDtypeStruct((2, 8, 8, SU...  26.2 us
    unnamed x32, local copies, waits for them, and re-layouts  13.3 us
    all_to_all x1, blocking collectives, reduce_all(): lax.all_to_all(jnp.broadcast_to(mine, (8, SUB, 128)), 'rec', split_axis=0...  12.3 us
    ppermute x1, waiting for transfers between devices, reduce_all(): lax.ppermute(send, AXES, [(a, b) for a, b in pairs] + [(b, a) for a, b in...  4.16 us
  transfers between devices with their start and end apart: 3, of which 2 were waited for; matrix products, arithmetic and copies ran while one was open for 1% of the time, Pallas kernels for 0%

profile of v2, /device:TPU:2, one launch (start us, length us, event | category | flops | bytes accessed | tf_op | source)
XLA Modules:
  0.0 127.5 jit_solution(17159263717509086243)
XLA Ops:
  0.6 0.7 bitcast_convert_fusion
  1.4 0.8 slice_reduce_fusion
  2.2 1.7 %collective-permute-start = (bf16[32,128]{1,0:T(8,128)(2,1)S(1)}, bf16[32,128]{1,0:T(8,128)(2,1)S(1)}, u32[]{:S(2)}, u32[]{:S(2)}) collective-permute-start(bf16[32,128]{1,0:T(8,128)(2,1)S(1)} %pad_maximum_fusion), channel_id=1, source_target_pairs={{0,8},{8,16},{16,24},{24,32},{32,40},{40,48},{48,56},{56,64},{64,7... | collective-permute-start | bytes 24584 | tf_op jit(solution)/shard_map/ppermute | solution.py:531
  3.9 1.3 %collective-permute-start.1 = (bf16[32,128]{1,0:T(8,128)(2,1)S(1)}, bf16[32,128]{1,0:T(8,128)(2,1)S(1)}, u32[]{:S(2)}, u32[]{:S(2)}) collective-permute-start(bf16[32,128]{1,0:T(8,128)(2,1)S(1)} %pad_maximum_fusion.1), channel_id=1, source_target_pairs={{8,0},{16,8},{24,16},{32,24},{40,32},{48,40},{56,48},{64,56},{72,6... | collective-permute-start | bytes 24584 | tf_op jit(solution)/shard_map/ppermute | solution.py:532
  5.9 0.1 pad_add_fusion.pos
  6.0 1.3 %convert_element_type.32 = f32[1,81920]{1,0:T(1,128)S(1)} convert(bf16[1,81920]{1,0:T(2,128)(2,1)} %param.20) | non-fusion elementwise | flops 81920 | bytes 491520 | tf_op jit(solution)/shard_map/convert_element_type | solution.py:526
  7.3 0.0 collective-permute-done.left
  7.3 1.1 collective-permute-done.1.right
  8.3 0.0 copy-start
  8.3 1.4 %copy-done = bf16[512,1536]{1,0:T(8,128)(2,1)S(1)} copy-done((bf16[512,1536]{1,0:T(8,128)(2,1)S(1)}, bf16[512,1536]{1,0:T(8,128)(2,1)}, u32[]{:S(2)}) %copy-start) | copy-done | bytes 1572888
  9.8 0.0 copy-start.1
  9.8 1.4 %copy-done.1 = bf16[1536,512]{1,0:T(8,128)(2,1)S(1)} copy-done((bf16[1536,512]{1,0:T(8,128)(2,1)S(1)}, bf16[1536,512]{1,0:T(8,128)(2,1)}, u32[]{:S(2)}) %copy-start.1) | copy-done | bytes 1572888
  11.2 0.0 copy-start.2
  11.2 1.3 %copy-done.2 = bf16[512,1280]{1,0:T(8,128)(2,1)S(1)} copy-done((bf16[512,1280]{1,0:T(8,128)(2,1)S(1)}, bf16[512,1280]{1,0:T(8,128)(2,1)}, u32[]{:S(2)}) %copy-start.2) | copy-done | bytes 1310744
  12.5 0.0 copy-start.3
  12.5 0.9 copy-done.3
  13.4 0.0 copy-start.4
  13.4 0.7 copy-done.4
  14.1 0.7 copy-done.5
  14.8 0.0 copy-start.6
  14.8 0.7 copy-done.6
  15.5 0.0 copy-start.7
  15.5 0.7 copy-done.7
  16.2 0.0 copy-start.8
  16.2 0.7 copy-done.8
  16.9 0.0 copy-start.9
  16.9 0.7 copy-done.9
  17.6 0.0 copy-start.10
  17.6 0.7 copy-done.10
  18.3 0.7 copy-done.11
  19.0 0.0 copy-start.12
  19.0 0.7 copy-done.12
  19.6 0.0 copy-start.13
  19.6 0.7 copy-done.13
  20.3 0.0 copy-start.14
  20.3 0.7 copy-done.14
  21.0 0.0 copy-start.15
  21.0 0.7 copy-done.15
  21.7 26.2 %local_grads.1 = (bf16[2,8,8,72,128]{4,3,2,1,0:T(8,128)(2,1)S(1)}, bf16[2,8,8,72,128]{4,3,2,1,0:T(8,128)(2,1)S(1)}) custom-call(s32[4]{0:T(128)S(1)} %pad_add_fusion.pos, s32[8,256]{1,0:T(8,128)S(1)} %bitcast.34, f32[640,128]{1,0:T(8,128)S(1)} %bitcast.33, bf16[32,128]{1,0:T(8,128)(2,1)S(1)} %collective-permute-done.left, ...), custom_call_target="tpu_custom_call" | custom-call | tf_op jit(solution)/shard_map/local_grads/pallas_call | solution.py:427
  47.9 2.5 %collective-permute-start.2 = (bf16[2,8,8,72,128]{4,3,2,1,0:T(8,128)(2,1)S(1)}, bf16[2,8,8,72,128]{4,3,2,1,0:T(8,128)(2,1)S(1)}, u32[]{:S(2)}, u32[]{:S(2)}) collective-permute-start(bf16[2,8,8,72,128]{4,3,2,1,0:T(8,128)(2,1)S(1)} %get-tuple-element.25), channel_id=1, source_target_pairs={{0,8},{1,9},{2,10},{3,11},{4,12},{5,13},{6,14},{7,15},{16,24},{17,... | collective-permute-start | bytes 7077896 | tf_op jit(solution)/shard_map/ppermute | solution.py:515
  50.4 4.2 %collective-permute-done.2 = bf16[2,8,8,72,128]{4,3,2,1,0:T(8,128)(2,1)S(1)} collective-permute-done((bf16[2,8,8,72,128]{4,3,2,1,0:T(8,128)(2,1)S(1)}, bf16[2,8,8,72,128]{4,3,2,1,0:T(8,128)(2,1)S(1)}, u32[]{:S(2)}, u32[]{:S(2)}) %collective-permute-start.2) | collective-permute-done | bytes 2359328 | tf_op jit(solution)/shard_map/ppermute | solution.py:515
  54.5 0.6 add_convert_fusion
  55.2 39.0 %all_to_all.15 = bf16[16,576,128]{2,1,0:T(8,128)(2,1)S(1)} all-to-all(bf16[16,576,128]{2,1,0:T(8,128)(2,1)S(1)} %bitcast.43), channel_id=1, replica_groups={{0,1,2,3,4,5,6,7,16,17,18,19,20,21,22,23},{8,9,10,11,12,13,14,15,24,25,..., dimensions={0} | all-to-all | bytes 4718592 | tf_op jit(solution)/shard_map/all_to_all | solution.py:506
  94.2 0.3 reduce_sum.21
  94.5 17.5 %all_to_all.16 = bf16[8,72,128]{2,1,0:T(8,128)(2,1)S(1)} all-to-all(bf16[8,72,128]{2,1,0:T(8,128)(2,1)S(1)} %bitcast.44), channel_id=1, replica_groups={{0,32,64,96,128,160,192,224},{1,33,65,97,129,161,193,225},{2,34,66,98,1..., dimensions={0} | all-to-all | bytes 294912 | tf_op jit(solution)/shard_map/all_to_all | solution.py:506
  112.0 12.3 %all_to_all.17.t = f32[8,72,128]{2,1,0:T(8,128)} all-to-all(f32[8,72,128]{2,1,0:T(8,128)S(1)} %broadcast_in_dim.31), channel_id=1, replica_groups=mesh['frame'=32,'rec'=8] {'rec'}, dimensions={0} | all-to-all | bytes 589824 | tf_op jit(solution)/shard_map/all_to_all | solution.py:519
  124.4 1.7 %unpack.1 = (f32[16,1536]{1,0:T(8,128)}, f32[16,1280]{1,0:T(8,128)}, f32[48,512]{1,0:T(8,128)}, f32[8,16]{1,0:T(8,128)}, f32[1,16]{1,0:T(1,128)}, /*index=5*/f32...) custom-call(s32[1]{0:T(128)} %bitcast.pos, f32[8,72,128]{2,1,0:T(8,128)} %all_to_all.17.t), custom_call_target="tpu_custom_call" | custom-call | tf_op jit(solution)/shard_map/unpack/pallas_call | solution.py:475
  126.1 1.4 %slice_bitcast_fusion = (f32[16]{0:T(128)}, f32[16]{0:T(128)}, f32[16]{0:T(128)}, f32[16]{0:T(128)}, f32[16]{0:T(128)}) fusion(f32[8,16]{1,0:T(8,128)} %get-tuple-element.29), kind=kLoop, calls=%fused_computation.7 | loop fusion | bytes 640 | tf_op jit(solution)/shard_map/squeeze | solution.py:537
  (7 shorter events, 0.1 us)
Async XLA Ops:
  2.2 5.1 %collective-permute-start = (bf16[32,128]{1,0:T(8,128)(2,1)S(1)}, bf16[32,128]{1,0:T(8,128)(2,1)S(1)}, u32[]{:S(2)}, u32[]{:S(2)}) collective-permute-start(bf16[32,128]{1,0:T(8,128)(2,1)S(1)} %pad_maximum_fusion), channel_id=1, source_target_pairs={{0,8},{8,16},{16,24},{24,32},{32,40},{40,48},{48,56},{56,64},{64,7... | collective-permute-start | bytes 24584 | tf_op jit(solution)/shard_map/ppermute | solution.py:531
  3.9 4.4 %collective-permute-start.1 = (bf16[32,128]{1,0:T(8,128)(2,1)S(1)}, bf16[32,128]{1,0:T(8,128)(2,1)S(1)}, u32[]{:S(2)}, u32[]{:S(2)}) collective-permute-start(bf16[32,128]{1,0:T(8,128)(2,1)S(1)} %pad_maximum_fusion.1), channel_id=1, source_target_pairs={{8,0},{16,8},{24,16},{32,24},{40,32},{48,40},{56,48},{64,56},{72,6... | collective-permute-start | bytes 24584 | tf_op jit(solution)/shard_map/ppermute | solution.py:532
  8.3 1.4 %copy-start = (bf16[512,1536]{1,0:T(8,128)(2,1)S(1)}, bf16[512,1536]{1,0:T(8,128)(2,1)}, u32[]{:S(2)}) copy-start(bf16[512,1536]{1,0:T(8,128)(2,1)} %up_w.1) | copy-start | bytes 4718596
  9.8 1.4 %copy-start.1 = (bf16[1536,512]{1,0:T(8,128)(2,1)S(1)}, bf16[1536,512]{1,0:T(8,128)(2,1)}, u32[]{:S(2)}) copy-start(bf16[1536,512]{1,0:T(8,128)(2,1)} %down_w.1) | copy-start | bytes 4718596
  11.2 1.3 %copy-start.2 = (bf16[512,1280]{1,0:T(8,128)(2,1)S(1)}, bf16[512,1280]{1,0:T(8,128)(2,1)}, u32[]{:S(2)}) copy-start(bf16[512,1280]{1,0:T(8,128)(2,1)} %head_w.1) | copy-start | bytes 3932164
  12.5 0.9 copy-start.3
  13.4 0.7 copy-start.4
  14.1 0.7 copy-start.5
  14.8 0.7 copy-start.6
  15.5 0.7 copy-start.7
  16.2 0.7 copy-start.8
  16.9 0.7 copy-start.9
  17.6 0.7 copy-start.10
  18.3 0.7 copy-start.11
  19.0 0.7 copy-start.12
  19.6 0.7 copy-start.13
  20.3 0.7 copy-start.14
  21.0 0.7 copy-start.15
  47.9 6.7 %collective-permute-start.2 = (bf16[2,8,8,72,128]{4,3,2,1,0:T(8,128)(2,1)S(1)}, bf16[2,8,8,72,128]{4,3,2,1,0:T(8,128)(2,1)S(1)}, u32[]{:S(2)}, u32[]{:S(2)}) collective-permute-start(bf16[2,8,8,72,128]{4,3,2,1,0:T(8,128)(2,1)S(1)} %get-tuple-element.25), channel_id=1, source_target_pairs={{0,8},{1,9},{2,10},{3,11},{4,12},{5,13},{6,14},{7,15},{16,24},{17,... | collective-permute-start | bytes 7077896 | tf_op jit(solution)/shard_map/ppermute | solution.py:515

commit v3 on v2

--- a/solution.py
+++ b/solution.py
@@ -93,24 +93,19 @@
     return hi, mid, low
 
 
-def local_kernel(
-    pos, codes, cot, left, right, embed_w, embed_b, depth_k, depth_b, gain, bias, up_w, up_b, down_w, down_b,
-    scale, head_w, head_b, trig, edge, keep, send,
-    tab, feat, conv, cgrad, latg, samp, pair_rows, spec_in, xhat, rstd, normed, hid, dgelu, act, branch, latent, re, im,
-    logit_low, low, big, spec, lg, row_sums, sums, tiles, tall, rows,
-):
-    first_frame, length = pos[0], pos[1]
-    last_frame = pos[2]
-    core = pos[3]
-
-    for t in range(FF // 128):
-        rows[0:1, 128 * t : 128 * t + 128] = up_b[t : t + 1, :]
-    for t in range(NFFT // 128):
-        rows[1:2, 128 * t : 128 * t + 128] = head_b[t : t + 1, :]
-    up_row, head_row = rows[0:1, :], rows[1:2, 0:NFFT]
+def setup_kernel(*refs):
+    count = (len(refs) - 4) // 2
+    sources, trig_far, outs = refs[:count], refs[count], refs[count + 1 : -3]
+    tab, trig, sems = refs[-3:]
+    first = pltpu.make_async_copy(trig_far, trig, sems.at[count])
+    copies = [pltpu.make_async_copy(a, b, sems.at[i]) for i, (a, b) in enumerate(zip(sources, outs))]
+    first.start()
+    for copy in copies:
+        copy.start()
 
     tab[0:96, :] = jnp.zeros((96, NFFT), bf16)
     tab[1376:TAB, :] = jnp.zeros((TAB - 1376, NFFT), bf16)
+    first.wait()
     cs, sn = trig[32:33, :], trig[33:34, :]
     real_row, imag_row = trig[34:35, :], trig[35:36, :]
 
@@ -123,6 +118,38 @@
         return c * cs - s * sn, s * cs + c * sn
 
     lax.fori_loop(0, NFFT // 16, table_step, (trig[0:16, :], trig[16:32, :]))
+    for copy in copies:
+        copy.wait()
+
+
+def setup(arrays):
+    whole = pl.BlockSpec(memory_space=pltpu.VMEM)
+    return pl.pallas_call(
+        setup_kernel,
+        out_shape=tuple(jax.ShapeDtypeStruct(a.shape, a.dtype) for a in arrays) + (jax.ShapeDtypeStruct((TAB, NFFT), bf16),),
+        in_specs=[pl.BlockSpec(memory_space=pltpu.HBM)] * (len(arrays) + 1),
+        out_specs=(whole,) * (len(arrays) + 1),
+        scratch_shapes=[pltpu.VMEM((40, BINS), f32), pltpu.SemaphoreType.DMA((len(arrays) + 1,))],
+        compiler_params=pltpu.CompilerParams(vmem_limit_bytes=16 * 1024 * 1024),
+        name="setup",
+    )(*[pltpu.with_memory_space_constraint(a, pltpu.HBM) for a in (*arrays, jnp.asarray(tables()))])
+
+
+def local_kernel(
+    pos, cot, left, right, codes, embed_w, embed_b, depth_k, depth_b, gain, bias, up_w, up_b, down_w, down_b,
+    scale, head_w, head_b, edge, tab, keep, send,
+    feat, conv, cgrad, latg, samp, pair_rows, spec_in, xhat, rstd, normed, hid, dgelu, act, branch, latent, re, im,
+    logit_low, low, big, spec, lg, row_sums, sums, tiles, tall, rows,
+):
+    first_frame, length = pos[0], pos[1]
+    last_frame = pos[2]
+    core = pos[3]
+
+    for t in range(FF // 128):
+        rows[0:1, 128 * t : 128 * t + 128] = up_b[t : t + 1, :]
+    for t in range(NFFT // 128):
+        rows[1:2, 128 * t : 128 * t + 128] = head_b[t : t + 1, :]
+    up_row, head_row = rows[0:1, :], rows[1:2, 0:NFFT]
 
     w_hi, w_mid, w_low = split3(embed_w[...])
 
@@ -159,18 +186,13 @@
 
     to_rows(conv, 8, xhat)
 
-    def norm_step(i, _):
-        at = pl.ds(pl.multiple_of(i * 16, 16), 16)
-        x = xhat[at, :]
-        centre = x - jnp.mean(x, axis=1, keepdims=True)
-        r = lax.rsqrt(jnp.mean(centre * centre, axis=1, keepdims=True) + EPSILON)
-        x = centre * r
-        xhat[at, :] = x
-        rstd[at, :] = jnp.broadcast_to(r, (16, 128))
-        normed[at, :] = (x * gain[...] + bias[...]).astype(bf16)
-        return 0
-
-    lax.fori_loop(0, ROWS // 16, norm_step, 0)
+    x = xhat[...]
+    centre = x - jnp.mean(x, axis=1, keepdims=True)
+    r = lax.rsqrt(jnp.mean(centre * centre, axis=1, keepdims=True) + EPSILON)
+    x = centre * r
+    xhat[...] = x
+    rstd[...] = jnp.broadcast_to(r, (ROWS, 128))
+    normed[...] = (x * gain[...] + bias[...]).astype(bf16)
 
     hid[...] = dot(normed[...], up_w[...])
 
@@ -330,22 +352,13 @@
 
     lg[...] = dot_cols(act[...], up_w[...])
 
-    def norm_grad_of(at):
-        g, x = lg[at, :], xhat[at, :]
-        dx = g * gain[...]
-        m1 = jnp.mean(dx, axis=1, keepdims=True)
-        m2 = jnp.mean(dx * x, axis=1, keepdims=True)
-        lg[at, :] = rstd[at, 0:1] * (dx - m1 - x * m2)
-        return g, g * x
-
-    def norm_grad_step(i, carry):
-        g, gx = norm_grad_of(pl.ds(pl.multiple_of(i * 16, 16), 16))
-        return carry[0] + g[0:8] + g[8:16], carry[1] + gx[0:8] + gx[8:16]
-
-    bias_sum, gain_sum = lax.fori_loop(0, FRAMES // 16, norm_grad_step, (zero, zero))
-    norm_grad_of(pl.ds(FRAMES, 16))
-    sums[17:18, :] = jnp.sum(gain_sum, axis=0, keepdims=True)
-    sums[18:19, :] = jnp.sum(bias_sum, axis=0, keepdims=True)
+    g, x = lg[...], xhat[...]
+    dx = g * gain[...]
+    m1 = jnp.mean(dx, axis=1, keepdims=True)
+    m2 = jnp.mean(dx * x, axis=1, keepdims=True)
+    lg[...] = rstd[:, 0:1] * (dx - m1 - x * m2)
+    sums[17:18, :] = jnp.sum(g[0:FRAMES] * x[0:FRAMES], axis=0, keepdims=True)
+    sums[18:19, :] = jnp.sum(g[0:FRAMES], axis=0, keepdims=True)
 
     i = lax.broadcasted_iota(jnp.int32, (16, D), 0)
     frame = jnp.where(i < 8, i - 8, i + (FRAMES - 8)) + first_frame
@@ -390,10 +403,9 @@
         send[p % 2, 7, p // 2, 40:64, :] = part
 
 
-def local_grads(pos, codes, cot, left, right, weights):
+def local_grads(pos, cot, left, right, ready):
     vmem = pltpu.VMEM
     scratch = [
-        vmem((TAB, NFFT), bf16),
         vmem((FRAMES + 32, D), f32),
         vmem((FRAMES + 16, D), f32),
         vmem((FRAMES + 16, D), f32),
@@ -423,23 +435,23 @@
         vmem((8, FF), f32),
     ]
     whole = pl.BlockSpec(memory_space=pltpu.VMEM)
-    arrays = [codes, cot, left, right, *weights, jnp.asarray(tables()), jnp.asarray(edges())]
+    arrays = [cot, left, right, *ready]
     return pl.pallas_call(
         local_kernel,
         out_shape=(jax.ShapeDtypeStruct((2, 8, 8, SUB, 128), bf16),) * 2,
         in_specs=[pl.BlockSpec(memory_space=pltpu.SMEM)] + [whole] * len(arrays),
         out_specs=(whole, whole),
         scratch_shapes=scratch,
-        compiler_params=pltpu.CompilerParams(vmem_limit_bytes=42 * 1024 * 1024),
+        compiler_params=pltpu.CompilerParams(vmem_limit_bytes=38 * 1024 * 1024),
         name="local_grads",
     )(pos, *arrays)
 
 
-def unpack_kernel(pos, t, up_g, head_g, down_g, embed_w, embed_b, depth_k, vectors, up_b, head_b):
+def unpack_kernel(pos, t, up_g, head_g, down_g, embed_w, embed_b, depth_k, up_b, head_b, *vectors):
     f = pos[0]
 
     def tile(o):
-        return t[o // SUB, o % SUB : o % SUB + 8, :]
+        return t[o // SUB, o % SUB : o % SUB + 8, :].astype(f32)
 
     for columns, height, row, ref in ((12, 16, 0, up_g), (10, 16, 192, head_g), (4, 48, 352, down_g)):
         for j in range(columns):
@@ -456,7 +468,8 @@
     third = rolled(tile(560), back)
     embed_b[...] = second[0:1, 0:16]
     depth_k[...] = second[1:8, 0:16]
-    vectors[...] = third[0:8, 0:16]
+    for i, ref in enumerate(vectors):
+        ref[...] = third[i : i + 1, 0:16]
     last = tile(568)
     lane = lax.broadcasted_iota(jnp.int32, (1, 128), 1)
     for row, width, ref in ((0, 48, up_b), (2, 40, head_b)):
@@ -475,10 +488,10 @@
     return pl.pallas_call(
         unpack_kernel,
         out_shape=(
-            shape(16, FF), shape(16, NFFT), shape(48, D), shape(8, 16), shape(1, 16), shape(7, 16), shape(8, 16), shape(1, 48), shape(1, 40),
-        ),
+            shape(16, FF), shape(16, NFFT), shape(48, D), shape(8, 16), shape(1, 16), shape(7, 16), shape(1, 48), shape(1, 40),
+        ) + (shape(1, 16),) * 5,
         in_specs=[pl.BlockSpec(memory_space=pltpu.SMEM), whole],
-        out_specs=(whole,) * 9,
+        out_specs=(whole,) * 13,
         name="unpack",
     )(pos, t)
 
@@ -515,7 +528,7 @@
     other = lax.ppermute(send, AXES, [(a, b) for a, b in pairs] + [(b, a) for a, b in pairs])
     half = (keep.astype(f32) + other.astype(f32)).astype(bf16).reshape(16, 8 * SUB, 128)
     part = summed(exchange(half, ("yl", "yh", "x"))).astype(bf16).reshape(8, SUB, 128)
-    mine = summed(exchange(part, ("z",)))
+    mine = summed(exchange(part, ("z",))).astype(bf16)
     return lax.all_to_all(jnp.broadcast_to(mine, (8, SUB, 128)), "rec", split_axis=0, concat_axis=0, tiled=True)
 
 
@@ -532,9 +545,10 @@
     right = lax.ppermute(jnp.concatenate([low[:LEFT], codes_low[:, :128]]), "frame", backward)
     pos = jnp.stack([me * FRAMES, lengths[0], count * FRAMES, me % 2]).astype(jnp.int32)
     flat = [w if w.ndim == 2 else w[None] if w.size == D else w.reshape(-1, 128) for w in weights]
-    t = reduce_all(*local_grads(pos, codes, samples, left, right, flat))
-    up_g, head_g, down_g, embed_w, embed_b, depth_k, vectors, up_b, head_b = unpack(me.astype(jnp.int32)[None], t)
-    depth_b, gain, bias, down_b, scale = (vectors[i] for i in range(5))
+    ready = setup([codes, *flat, jnp.asarray(edges())])
+    t = reduce_all(*local_grads(pos, samples, left, right, ready))
+    up_g, head_g, down_g, embed_w, embed_b, depth_k, up_b, head_b, *vectors = unpack(me.astype(jnp.int32)[None], t)
+    depth_b, gain, bias, down_b, scale = (v[0] for v in vectors)
     return (
         embed_w, embed_b[0], depth_k, depth_b, gain, bias, up_g, up_b[0], down_g, down_b, scale, head_g, head_b[0],
     )

time: 129 us -> 109 us (0.84)
  local copies, waits for them, and re-layouts: 15.5 us -> 0.82 us
  Pallas kernels: 27.9 us -> 24.5 us
    unnamed x32 -> x0, local copies, waits for them, and re-layouts: 13.3 us -> none
    pallas_call x1, Pallas kernels: 26.2 us -> 15.4 us  [local_grads(): pl.pallas_call(local_kernel, out_shape=(jax.ShapeDtypeStruct((2, 8, 8, SU...]
    pallas_call x0 -> x1, Pallas kernels: none -> 7.53 us  [setup(): pl.pallas_call(setup_kernel, out_shape=tuple((jax.ShapeDtypeStruct(a.shap...]
    squeeze x1 -> x0, local copies, waits for them, and re-layouts: 1.39 us -> none  [body(): depth_b, gain, bias, down_b, scale = (vectors[i] for i in range(5))]
  transfers between devices with their start and end apart: 3 -> 3, of which waited for: 2 -> 1; matrix products, arithmetic and copies ran while one was open for 1% -> 1% of each run, Pallas kernels for 0% -> 7%
where the time goes in v3:
time: 109 us
  blocking collectives  69 us (63%)
  Pallas kernels  24.5 us (22%)
  starting transfers between devices  5.6 us (5%)
  waiting for transfers between devices  4.17 us (4%)
  other arithmetic  3.08 us (3%)
  between operations  1.39 us (1%)
    all_to_all x2, blocking collectives, exchange(): lax.all_to_all(array, AXES, split_axis=0, concat_axis=0, axis_index_group...  57.4 us
    pallas_call x1, Pallas kernels, local_grads(): pl.pallas_call(local_kernel, out_shape=(jax.ShapeDtypeStruct((2, 8, 8, SU...  15.4 us
    all_to_all x1, blocking collectives, reduce_all(): lax.all_to_all(jnp.broadcast_to(mine, (8, SUB, 128)), 'rec', split_axis=0...  11.5 us
    pallas_call x1, Pallas kernels, setup(): pl.pallas_call(setup_kernel, out_shape=tuple((jax.ShapeDtypeStruct(a.shap...  7.53 us
    ppermute x1, waiting for transfers between devices, reduce_all(): lax.ppermute(send, AXES, [(a, b) for a, b in pairs] + [(b, a) for a, b in...  4.16 us
    ppermute x1, starting transfers between devices, reduce_all(): lax.ppermute(send, AXES, [(a, b) for a, b in pairs] + [(b, a) for a, b in...  2.57 us
  transfers between devices with their start and end apart: 3, of which 1 were waited for; matrix products, arithmetic and copies ran while one was open for 1% of the time, Pallas kernels for 7%

profile of v3, /device:TPU:2, one launch (start us, length us, event | category | flops | bytes accessed | tf_op | source)
XLA Modules:
  0.0 108.6 jit_solution(13752615944711012044)
XLA Ops:
  0.6 0.7 bitcast_convert_fusion
  1.4 0.8 slice_reduce_fusion
  2.2 1.7 %collective-permute-start = (bf16[32,128]{1,0:T(8,128)(2,1)S(1)}, bf16[32,128]{1,0:T(8,128)(2,1)S(1)}, u32[]{:S(2)}, u32[]{:S(2)}) collective-permute-start(bf16[32,128]{1,0:T(8,128)(2,1)S(1)} %pad_maximum_fusion), channel_id=1, source_target_pairs={{0,8},{8,16},{16,24},{24,32},{32,40},{40,48},{48,56},{56,64},{64,7... | collective-permute-start | bytes 24584 | tf_op jit(solution)/shard_map/ppermute | solution.py:544
  3.9 1.3 %collective-permute-start.1 = (bf16[32,128]{1,0:T(8,128)(2,1)S(1)}, bf16[32,128]{1,0:T(8,128)(2,1)S(1)}, u32[]{:S(2)}, u32[]{:S(2)}) collective-permute-start(bf16[32,128]{1,0:T(8,128)(2,1)S(1)} %pad_maximum_fusion.1), channel_id=1, source_target_pairs={{8,0},{16,8},{24,16},{32,24},{40,32},{48,40},{56,48},{64,56},{72,6... | collective-permute-start | bytes 24584 | tf_op jit(solution)/shard_map/ppermute | solution.py:545
  5.9 0.1 pad_add_fusion.pos
  6.0 1.3 %convert_element_type.30 = f32[1,81920]{1,0:T(1,128)S(1)} convert(bf16[1,81920]{1,0:T(2,128)(2,1)} %param.20) | non-fusion elementwise | flops 81920 | bytes 491520 | tf_op jit(solution)/shard_map/convert_element_type | solution.py:539
  7.3 7.5 %setup.1 = (s32[8,256]{1,0:T(8,128)S(1)}, f32[8,512]{1,0:T(8,128)S(1)}, f32[1,512]{1,0:T(1,128)S(1)}, f32[7,512]{1,0:T(8,128)S(1)}, f32[1,512]{1,0:T(1,128)S(1)}...) custom-call(s32[8,256]{1,0:T(8,128)} %bitcast.31, ...), custom_call_target="tpu_custom_call" | custom-call | tf_op jit(solution)/shard_map/setup/pallas_call | solution.py:127
  14.8 0.0 collective-permute-done.left
  14.8 0.0 collective-permute-done.1.right
  14.8 15.4 %local_grads.1 = (bf16[2,8,8,72,128]{4,3,2,1,0:T(8,128)(2,1)S(1)}, bf16[2,8,8,72,128]{4,3,2,1,0:T(8,128)(2,1)S(1)}) custom-call(s32[4]{0:T(128)S(1)} %pad_add_fusion.pos, f32[640,128]{1,0:T(8,128)S(1)} %bitcast.28, bf16[32,128]{1,0:T(8,128)(2,1)S(1)} %collective-permute-done.left, bf16[32,128]{1,0:T(8,128)(2,1)S(1)} %collective-permute-done.1.right, ...), custom_call_target="tpu_custom_call" | custom-call | tf_op jit(solution)/shard_map/local_grads/pallas_call | solution.py:439
  30.2 2.6 %collective-permute-start.2 = (bf16[2,8,8,72,128]{4,3,2,1,0:T(8,128)(2,1)S(1)}, bf16[2,8,8,72,128]{4,3,2,1,0:T(8,128)(2,1)S(1)}, u32[]{:S(2)}, u32[]{:S(2)}) collective-permute-start(bf16[2,8,8,72,128]{4,3,2,1,0:T(8,128)(2,1)S(1)} %get-tuple-element.61), channel_id=1, source_target_pairs={{0,8},{1,9},{2,10},{3,11},{4,12},{5,13},{6,14},{7,15},{16,24},{17,... | collective-permute-start | bytes 7077896 | tf_op jit(solution)/shard_map/ppermute | solution.py:528
  32.8 4.2 %collective-permute-done.2 = bf16[2,8,8,72,128]{4,3,2,1,0:T(8,128)(2,1)S(1)} collective-permute-done((bf16[2,8,8,72,128]{4,3,2,1,0:T(8,128)(2,1)S(1)}, bf16[2,8,8,72,128]{4,3,2,1,0:T(8,128)(2,1)S(1)}, u32[]{:S(2)}, u32[]{:S(2)}) %collective-permute-start.2) | collective-permute-done | bytes 2359328 | tf_op jit(solution)/shard_map/ppermute | solution.py:528
  36.9 0.6 add_convert_fusion
  37.6 38.1 %all_to_all.15 = bf16[16,576,128]{2,1,0:T(8,128)(2,1)S(1)} all-to-all(bf16[16,576,128]{2,1,0:T(8,128)(2,1)S(1)} %bitcast.29), channel_id=1, replica_groups={{0,1,2,3,4,5,6,7,16,17,18,19,20,21,22,23},{8,9,10,11,12,13,14,15,24,25,..., dimensions={0} | all-to-all | bytes 4718592 | tf_op jit(solution)/shard_map/all_to_all | solution.py:519
  75.7 0.3 reduce_sum.24
  76.0 19.3 %all_to_all.16 = bf16[8,72,128]{2,1,0:T(8,128)(2,1)S(1)} all-to-all(bf16[8,72,128]{2,1,0:T(8,128)(2,1)S(1)} %bitcast.30), channel_id=1, replica_groups={{0,32,64,96,128,160,192,224},{1,33,65,97,129,161,193,225},{2,34,66,98,1..., dimensions={0} | all-to-all | bytes 294912 | tf_op jit(solution)/shard_map/all_to_all | solution.py:519
  95.4 11.5 %all_to_all.17.t = bf16[8,72,128]{2,1,0:T(8,128)(2,1)} all-to-all(bf16[8,72,128]{2,1,0:T(8,128)(2,1)S(1)} %broadcast_in_dim.31), channel_id=1, replica_groups=mesh['frame'=32,'rec'=8] {'rec'}, dimensions={0} | all-to-all | bytes 294912 | tf_op jit(solution)/shard_map/all_to_all | solution.py:532
  106.9 1.6 %unpack.1 = (f32[16,1536]{1,0:T(8,128)}, f32[16,1280]{1,0:T(8,128)}, f32[48,512]{1,0:T(8,128)}, f32[8,16]{1,0:T(8,128)}, f32[1,16]{1,0:T(1,128)}, /*index=5*/f32...) custom-call(s32[1]{0:T(128)} %bitcast.pos, ...), custom_call_target="tpu_custom_call" | custom-call | tf_op jit(solution)/shard_map/unpack/pallas_call | solution.py:488
  (5 shorter events, 0.1 us)
Async XLA Ops:
  2.2 12.7 %collective-permute-start = (bf16[32,128]{1,0:T(8,128)(2,1)S(1)}, bf16[32,128]{1,0:T(8,128)(2,1)S(1)}, u32[]{:S(2)}, u32[]{:S(2)}) collective-permute-start(bf16[32,128]{1,0:T(8,128)(2,1)S(1)} %pad_maximum_fusion), channel_id=1, source_target_pairs={{0,8},{8,16},{16,24},{24,32},{32,40},{40,48},{48,56},{56,64},{64,7... | collective-permute-start | bytes 24584 | tf_op jit(solution)/shard_map/ppermute | solution.py:544
  3.9 10.9 %collective-permute-start.1 = (bf16[32,128]{1,0:T(8,128)(2,1)S(1)}, bf16[32,128]{1,0:T(8,128)(2,1)S(1)}, u32[]{:S(2)}, u32[]{:S(2)}) collective-permute-start(bf16[32,128]{1,0:T(8,128)(2,1)S(1)} %pad_maximum_fusion.1), channel_id=1, source_target_pairs={{8,0},{16,8},{24,16},{32,24},{40,32},{48,40},{56,48},{64,56},{72,6... | collective-permute-start | bytes 24584 | tf_op jit(solution)/shard_map/ppermute | solution.py:545
  30.2 6.7 %collective-permute-start.2 = (bf16[2,8,8,72,128]{4,3,2,1,0:T(8,128)(2,1)S(1)}, bf16[2,8,8,72,128]{4,3,2,1,0:T(8,128)(2,1)S(1)}, u32[]{:S(2)}, u32[]{:S(2)}) collective-permute-start(bf16[2,8,8,72,128]{4,3,2,1,0:T(8,128)(2,1)S(1)} %get-tuple-element.61), channel_id=1, source_target_pairs={{0,8},{1,9},{2,10},{3,11},{4,12},{5,13},{6,14},{7,15},{16,24},{17,... | collective-permute-start | bytes 7077896 | tf_op jit(solution)/shard_map/ppermute | solution.py:528

commit v4 on v3

--- a/solution.py
+++ b/solution.py
@@ -31,13 +31,17 @@
     n = np.arange(16)[:, None]
     k = np.arange(BINS)[None, :]
     turn = 2.0 * np.pi / NFFT
-    out = np.zeros((40, BINS), np.float64)
+    out = np.zeros((64, BINS), np.float64)
     out[0:16] = np.cos(turn * (n * k % NFFT))
     out[16:32] = np.sin(turn * (n * k % NFFT))
     out[32] = np.cos(turn * (16 * k[0] % NFFT))
     out[33] = np.sin(turn * (16 * k[0] % NFFT))
     out[34] = np.where(k[0] == 0, 1.0, 2.0) / NFFT
     out[35] = np.where(k[0] == 0, 0.0, -2.0) / NFFT
+    out[36] = np.cos(turn * 16)
+    out[37] = np.sin(turn * 16)
+    out[40:56, 0:128] = np.cos(turn * n)
+    out[40:56, 128:256] = np.sin(turn * n)
     return out.astype(np.float32)
 
 
@@ -108,16 +112,17 @@
     first.wait()
     cs, sn = trig[32:33, :], trig[33:34, :]
     real_row, imag_row = trig[34:35, :], trig[35:36, :]
+    wcs, wsn = trig[36:37, 0:128], trig[37:38, 0:128]
 
     def table_step(i, carry):
-        c, s = carry
-        window = 0.5 - 0.5 * c[:, 1:2]
+        c, s, wc, ws = carry
+        window = jnp.concatenate([0.5 - 0.5 * wc] * 5, axis=1)
         at = pl.multiple_of(96 + i * 16, 16)
         tab[pl.ds(at, 16), 0:BINS] = (c * (window * real_row)).astype(bf16)
         tab[pl.ds(at, 16), BINS:] = (s * (window * imag_row)).astype(bf16)
-        return c * cs - s * sn, s * cs + c * sn
-
-    lax.fori_loop(0, NFFT // 16, table_step, (trig[0:16, :], trig[16:32, :]))
+        return c * cs - s * sn, s * cs + c * sn, wc * wcs - ws * wsn, ws * wcs + wc * wsn
+
+    lax.fori_loop(0, NFFT // 16, table_step, (trig[0:16, :], trig[16:32, :], trig[40:56, 0:128], trig[40:56, 128:256]))
     for copy in copies:
         copy.wait()
 
@@ -129,7 +134,7 @@
         out_shape=tuple(jax.ShapeDtypeStruct(a.shape, a.dtype) for a in arrays) + (jax.ShapeDtypeStruct((TAB, NFFT), bf16),),
         in_specs=[pl.BlockSpec(memory_space=pltpu.HBM)] * (len(arrays) + 1),
         out_specs=(whole,) * (len(arrays) + 1),
-        scratch_shapes=[pltpu.VMEM((40, BINS), f32), pltpu.SemaphoreType.DMA((len(arrays) + 1,))],
+        scratch_shapes=[pltpu.VMEM((64, BINS), f32), pltpu.SemaphoreType.DMA((len(arrays) + 1,))],
         compiler_params=pltpu.CompilerParams(vmem_limit_bytes=16 * 1024 * 1024),
         name="setup",
     )(*[pltpu.with_memory_space_constraint(a, pltpu.HBM) for a in (*arrays, jnp.asarray(tables()))])
@@ -143,7 +148,11 @@
 ):
     first_frame, length = pos[0], pos[1]
     last_frame = pos[2]
-    core = pos[3]
+    core, my, mx = pos[3], pos[4], pos[5]
+
+    def place(o, yl):
+        part = o // SUB
+        return (2 * (part // 4) + yl) ^ my, (part % 4) ^ mx
 
     for t in range(FF // 128):
         rows[0:1, 128 * t : 128 * t + 128] = up_b[t : t + 1, :]
@@ -306,7 +315,8 @@
                         o = row + j * height + h * 8
                         at = pl.multiple_of(f * height + h * 8, 8)
                         value = big_ref[pl.ds(at, 8), 128 * j : 128 * j + 128].astype(bf16)
-                        ref[yl, o // SUB, z, o % SUB : o % SUB + 8, :] = value
+                        dy, dx = place(o, yl)
+                        ref[dy, dx, z, o % SUB : o % SUB + 8, :] = value
             return 0
 
         lax.fori_loop(0, 16, step, 0)
@@ -392,15 +402,17 @@
         for ref, f in ((keep, 2 * p + core), (send, 2 * p + 1 - core)):
             row_sums[0:2, :] = tiles[pl.ds((48 * f) // 128, 2), :]
             row_sums[2:4, :] = tiles[pl.ds(16 + (40 * f) // 128, 2), :]
-            ref[yl, 7, z, 64:72, :] = row_sums[...].astype(bf16)
+            dy, dx = place(7 * SUB, yl)
+            ref[dy, dx, z, 64:72, :] = row_sums[...].astype(bf16)
         return 0
 
     lax.fori_loop(0, 16, small_step, 0)
     for p in range(16):
         column = 128 * (p // 4)
         part = sums[:, column : column + 128].astype(bf16)
-        keep[p % 2, 7, p // 2, 40:64, :] = part
-        send[p % 2, 7, p // 2, 40:64, :] = part
+        dy, dx = place(7 * SUB, p % 2)
+        keep[dy, dx, p // 2, 40:64, :] = part
+        send[dy, dx, p // 2, 40:64, :] = part
 
 
 def local_grads(pos, cot, left, right, ready):
@@ -438,7 +450,7 @@
     arrays = [cot, left, right, *ready]
     return pl.pallas_call(
         local_kernel,
-        out_shape=(jax.ShapeDtypeStruct((2, 8, 8, SUB, 128), bf16),) * 2,
+        out_shape=(jax.ShapeDtypeStruct((4, 4, 8, SUB, 128), bf16),) * 2,
         in_specs=[pl.BlockSpec(memory_space=pltpu.SMEM)] + [whole] * len(arrays),
         out_specs=(whole, whole),
         scratch_shapes=scratch,
@@ -523,18 +535,103 @@
     return jnp.sum(array.astype(f32), axis=0)
 
 
+def partners(which, offset=0):
+    pairs = []
+    for z in range(8):
+        for y in range(4):
+            for c in range(2):
+                for x in range(4):
+                    flip = 3 if offset else 1
+                    to = dict(c=(y, 1 - c, x), x=(y, c, x ^ flip), y=(y ^ flip, c, x))[which]
+                    pairs.append((index_of(z, y % 2, c, y // 2, x), index_of(z, to[0] % 2, to[1], to[0] // 2, to[2])))
+    return pairs
+
+
+ORDERS = ((0, 3, 1, 2), (0, 1, 3, 2))
+AXIS_OF = ("x", "x", "y", "y")
+
+
+def split_first(keep, other, *outs):
+    for k in range(4):
+        for i, d in enumerate(ORDERS[k % 2]):
+            for e in range(4):
+                for z in range(2):
+                    at = ((e, d) if k < 2 else (d, e)) + (2 * k + z,)
+                    total = keep[at].astype(f32) + other[at].astype(f32)
+                    if i < 2:
+                        outs[4 + k][i, e, z] = total
+                    else:
+                        outs[k][i - 2, e, z] = total.astype(bf16)
+
+
+def split_second(*refs):
+    keeps, others, outs = refs[0:4], refs[4:8], refs[8:]
+    for k in range(4):
+        for e in range(4):
+            for z in range(2):
+                outs[4 + k][e, z] = keeps[k][0, e, z] + others[k][0, e, z].astype(f32)
+                outs[k][e, z] = (keeps[k][1, e, z] + others[k][1, e, z].astype(f32)).astype(bf16)
+
+
+def split_third(*refs):
+    keeps, others, outs = refs[0:4], refs[4:8], refs[8:]
+    for g in range(2):
+        for h in range(2):
+            k = 2 * g + h
+            for i, d in enumerate(ORDERS[0]):
+                for z in range(2):
+                    total = keeps[k][d, z] + others[k][d, z].astype(f32)
+                    if i < 2:
+                        outs[2 + g][i, 2 * h + z] = total
+                    else:
+                        outs[g][i - 2, 2 * h + z] = total.astype(bf16)
+
+
+def split_fourth(*refs):
+    keeps, others, outs = refs[0:2], refs[2:4], refs[4:]
+    for g in range(2):
+        for z in range(4):
+            outs[2 + g][z] = keeps[g][0, z] + others[g][0, z].astype(f32)
+            outs[g][z] = (keeps[g][1, z] + others[g][1, z].astype(f32)).astype(bf16)
+
+
+def join(*refs):
+    for g in range(2):
+        for z in range(4):
+            refs[4][4 * g + z] = (refs[g][z] + refs[2 + g][z].astype(f32)).astype(bf16)
+
+
+def step(kernel, arrays, shape, count, limit):
+    whole = pl.BlockSpec(memory_space=pltpu.VMEM)
+    kinds = (bf16,) * count + (f32,) * (count if kernel is not join else 0)
+    return pl.pallas_call(
+        kernel,
+        out_shape=tuple(jax.ShapeDtypeStruct(shape + (SUB, 128), kind) for kind in kinds),
+        in_specs=[whole] * len(arrays),
+        out_specs=(whole,) * len(kinds),
+        compiler_params=pltpu.CompilerParams(vmem_limit_bytes=limit * 1024 * 1024),
+        name=kernel.__name__,
+    )(*arrays)
+
+
 def reduce_all(keep, send):
-    pairs = groups_over(("c",))
-    other = lax.ppermute(send, AXES, [(a, b) for a, b in pairs] + [(b, a) for a, b in pairs])
-    half = (keep.astype(f32) + other.astype(f32)).astype(bf16).reshape(16, 8 * SUB, 128)
-    part = summed(exchange(half, ("yl", "yh", "x"))).astype(bf16).reshape(8, SUB, 128)
+    other = lax.ppermute(send, AXES, partners("c"))
+    parts = step(split_first, (keep, other), (2, 4, 2), 4, 24)
+    moved = [lax.ppermute(a, AXES, partners(AXIS_OF[k], k % 2)) for k, a in enumerate(parts[:4])]
+    parts = step(split_second, (*parts[4:], *moved), (4, 2), 4, 16)
+    moved = [lax.ppermute(a, AXES, partners(AXIS_OF[k], 1 - k % 2)) for k, a in enumerate(parts[:4])]
+    parts = step(split_third, (*parts[4:], *moved), (2, 4), 2, 8)
+    moved = [lax.ppermute(a, AXES, partners("yx"[g], 0)) for g, a in enumerate(parts[:2])]
+    parts = step(split_fourth, (*parts[2:], *moved), (4,), 2, 8)
+    moved = [lax.ppermute(a, AXES, partners("yx"[g], 1)) for g, a in enumerate(parts[:2])]
+    (part,) = step(join, (*parts[2:], *moved), (8,), 1, 8)
     mine = summed(exchange(part, ("z",))).astype(bf16)
     return lax.all_to_all(jnp.broadcast_to(mine, (8, SUB, 128)), "rec", split_axis=0, concat_axis=0, tiled=True)
 
 
 def body(code_indices, lengths, cotangent, *weights):
     count = lax.axis_size("frame")
-    me = lax.axis_index("frame")
+    me, rec = lax.axis_index("frame"), lax.axis_index("rec")
     codes = code_indices[0].T
     samples = cotangent[0].astype(f32).reshape(640, 128)
     low = samples.astype(bf16)
@@ -543,7 +640,7 @@
     backward = [(b, a) for a, b in forward]
     left = lax.ppermute(jnp.concatenate([low[640 - LEFT :], codes_low[:, FRAMES - 128 :]]), "frame", forward)
     right = lax.ppermute(jnp.concatenate([low[:LEFT], codes_low[:, :128]]), "frame", backward)
-    pos = jnp.stack([me * FRAMES, lengths[0], count * FRAMES, me % 2]).astype(jnp.int32)
+    pos = jnp.stack([me * FRAMES, lengths[0], count * FRAMES, me % 2, 2 * (rec // 4) + me // 2 % 2, rec % 4]).astype(jnp.int32)
     flat = [w if w.ndim == 2 else w[None] if w.size == D else w.reshape(-1, 128) for w in weights]
     ready = setup([codes, *flat, jnp.asarray(edges())])
     t = reduce_all(*local_grads(pos, samples, left, right, ready))

time: 109 us -> 105 us (0.963)
  blocking collectives: 69 us -> 34.2 us
  waiting for transfers between devices: 4.17 us -> 25.7 us
  starting transfers between devices: 5.6 us -> 19.3 us
  Pallas kernels: 24.5 us -> 21 us
    all_to_all x2 -> x1, blocking collectives: 57.4 us -> 20.3 us  [exchange(): lax.all_to_all(array, AXES, split_axis=0, concat_axis=0, axis_index_group...]
    ppermute x1 -> x13, waiting for transfers between devices: 4.16 us -> 25.7 us  [the longest x4 7.93 us: reduce_all(): lax.ppermute(a, AXES, partners(AXIS_OF[k], k % 2))]
    ppermute x1 -> x13, starting transfers between devices: 2.57 us -> 16.3 us  [the longest x4 6.31 us: reduce_all(): lax.ppermute(a, AXES, partners(AXIS_OF[k], k % 2))]
    pallas_call x1, Pallas kernels: 7.53 us -> 2.82 us  [setup(): pl.pallas_call(setup_kernel, out_shape=tuple((jax.ShapeDtypeStruct(a.shap...]
    all_to_all x1, blocking collectives: 11.5 us -> 14 us  [reduce_all(): lax.all_to_all(jnp.broadcast_to(mine, (8, SUB, 128)), 'rec', split_axis=0...]
    pallas_call x1 -> x6, Pallas kernels: 15.4 us -> 16.5 us  [the longest x1 15.7 us: local_grads(): pl.pallas_call(local_kernel, out_shape=(jax.ShapeDtypeStruct((4, 4, 8, SU...]
  transfers between devices with their start and end apart: 3 -> 15, of which waited for: 1 -> 12; matrix products, arithmetic and copies ran while one was open for 1% -> 1% of each run, Pallas kernels for 7% -> 3%
where the time goes in v4:
time: 105 us
  blocking collectives  34.2 us (33%)
  waiting for transfers between devices  25.7 us (24%)
  Pallas kernels  21 us (20%)
  starting transfers between devices  19.3 us (18%)
  other arithmetic  2.05 us (2%)
  between operations  1.65 us (2%)
    all_to_all x1, blocking collectives, exchange(): lax.all_to_all(array, AXES, split_axis=0, concat_axis=0, axis_index_group...  20.3 us
    pallas_call x1, Pallas kernels, local_grads(): pl.pallas_call(local_kernel, out_shape=(jax.ShapeDtypeStruct((4, 4, 8, SU...  15.7 us
    all_to_all x1, blocking collectives, reduce_all(): lax.all_to_all(jnp.broadcast_to(mine, (8, SUB, 128)), 'rec', split_axis=0...  14 us
    ppermute x4, waiting for transfers between devices, reduce_all(): lax.ppermute(a, AXES, partners(AXIS_OF[k], k % 2))  7.93 us
    ppermute x4, starting transfers between devices, reduce_all(): lax.ppermute(a, AXES, partners(AXIS_OF[k], k % 2))  6.31 us
    ppermute x4, waiting for transfers between devices, reduce_all(): lax.ppermute(a, AXES, partners(AXIS_OF[k], 1 - k % 2))  5.39 us
    ppermute x2, waiting for transfers between devices, reduce_all(): lax.ppermute(a, AXES, partners('yx'[g], 0))  5.13 us
    ppermute x4, starting transfers between devices, reduce_all(): lax.ppermute(a, AXES, partners(AXIS_OF[k], 1 - k % 2))  4.68 us
  transfers between devices with their start and end apart: 15, of which 12 were waited for; matrix products, arithmetic and copies ran while one was open for 1% of the time, Pallas kernels for 3%

profile of v4, /device:TPU:2, one launch (start us, length us, event | category | flops | bytes accessed | tf_op | source)
XLA Modules:
  0.0 104.8 jit_solution(3481186680702514146)
XLA Ops:
  0.6 0.7 bitcast_convert_fusion
  1.4 0.8 slice_reduce_fusion
  2.2 1.7 %collective-permute-start = (bf16[32,128]{1,0:T(8,128)(2,1)S(1)}, bf16[32,128]{1,0:T(8,128)(2,1)S(1)}, u32[]{:S(2)}, u32[]{:S(2)}) collective-permute-start(bf16[32,128]{1,0:T(8,128)(2,1)S(1)} %pad_maximum_fusion), channel_id=1, source_target_pairs={{0,8},{8,16},{16,24},{24,32},{32,40},{40,48},{48,56},{56,64},{64,7... | collective-permute-start | bytes 24584 | tf_op jit(solution)/shard_map/ppermute | solution.py:641
  3.9 1.3 %collective-permute-start.1 = (bf16[32,128]{1,0:T(8,128)(2,1)S(1)}, bf16[32,128]{1,0:T(8,128)(2,1)S(1)}, u32[]{:S(2)}, u32[]{:S(2)}) collective-permute-start(bf16[32,128]{1,0:T(8,128)(2,1)S(1)} %pad_maximum_fusion.1), channel_id=1, source_target_pairs={{8,0},{16,8},{24,16},{32,24},{40,32},{48,40},{56,48},{64,56},{72,6... | collective-permute-start | bytes 24584 | tf_op jit(solution)/shard_map/ppermute | solution.py:642
  5.3 1.3 %convert_element_type.16 = f32[1,81920]{1,0:T(1,128)S(1)} convert(bf16[1,81920]{1,0:T(2,128)(2,1)} %param.20) | non-fusion elementwise | flops 81920 | bytes 491520 | tf_op jit(solution)/shard_map/convert_element_type | solution.py:636
  7.3 0.1 stack.19.pos
  7.3 2.8 %setup.1 = (s32[8,256]{1,0:T(8,128)S(1)}, f32[8,512]{1,0:T(8,128)S(1)}, f32[1,512]{1,0:T(1,128)S(1)}, f32[7,512]{1,0:T(8,128)S(1)}, f32[1,512]{1,0:T(1,128)S(1)}...) custom-call(s32[8,256]{1,0:T(8,128)} %bitcast.29, ...), custom_call_target="tpu_custom_call" | custom-call | tf_op jit(solution)/shard_map/setup/pallas_call | solution.py:132
  10.2 0.0 collective-permute-done.left
  10.2 0.0 collective-permute-done.1.right
  10.2 15.7 %local_grads.1 = (bf16[4,4,8,72,128]{4,3,2,1,0:T(8,128)(2,1)S(1)}, bf16[4,4,8,72,128]{4,3,2,1,0:T(8,128)(2,1)S(1)}) custom-call(s32[6]{0:T(128)S(1)} %stack.19.pos, f32[640,128]{1,0:T(8,128)S(1)} %bitcast.28, bf16[32,128]{1,0:T(8,128)(2,1)S(1)} %collective-permute-done.left, bf16[32,128]{1,0:T(8,128)(2,1)S(1)} %collective-permute-done.1.right, ...), custom_call_target="tpu_custom_call" | custom-call | tf_op jit(solution)/shard_map/local_grads/pallas_call | solution.py:451
  25.9 2.6 %collective-permute-start.2 = (bf16[4,4,8,72,128]{4,3,2,1,0:T(8,128)(2,1)S(1)}, bf16[4,4,8,72,128]{4,3,2,1,0:T(8,128)(2,1)S(1)}, u32[]{:S(2)}, u32[]{:S(2)}) collective-permute-start(bf16[4,4,8,72,128]{4,3,2,1,0:T(8,128)(2,1)S(1)} %get-tuple-element.85), channel_id=1, source_target_pairs={{0,8},{1,9},{2,10},{3,11},{8,0},{9,1},{10,2},{11,3},{16,24},{17,25... | collective-permute-start | bytes 7077896 | tf_op jit(solution)/shard_map/ppermute | solution.py:618
  28.4 4.2 %collective-permute-done.2.other = bf16[4,4,8,72,128]{4,3,2,1,0:T(8,128)(2,1)S(1)} collective-permute-done((bf16[4,4,8,72,128]{4,3,2,1,0:T(8,128)(2,1)S(1)}, bf16[4,4,8,72,128]{4,3,2,1,0:T(8,128)(2,1)S(1)}, u32[]{:S(2)}, u32[]{:S(2)}) %collective-permute-start.2) | collective-permute-done | bytes 2359328 | tf_op jit(solution)/shard_map/ppermute | solution.py:618
  32.6 0.5 split_first.1
  33.1 0.6 collective-permute-start.3
  33.7 2.2 %collective-permute-start.4 = (bf16[2,4,2,72,128]{4,3,2,1,0:T(8,128)(2,1)S(1)}, bf16[2,4,2,72,128]{4,3,2,1,0:T(8,128)(2,1)S(1)}, u32[]{:S(2)}, u32[]{:S(2)}) collective-permute-start(bf16[2,4,2,72,128]{4,3,2,1,0:T(8,128)(2,1)S(1)} %get-tuple-element.91), channel_id=1, source_target_pairs={{0,3},{1,2},{2,1},{3,0},{8,11},{9,10},{10,9},{11,8},{16,19},{17,18... | collective-permute-start | bytes 884744 | tf_op jit(solution)/shard_map/ppermute | solution.py:620
  35.9 2.0 %collective-permute-start.5 = (bf16[2,4,2,72,128]{4,3,2,1,0:T(8,128)(2,1)S(1)}, bf16[2,4,2,72,128]{4,3,2,1,0:T(8,128)(2,1)S(1)}, u32[]{:S(2)}, u32[]{:S(2)}) collective-permute-start(bf16[2,4,2,72,128]{4,3,2,1,0:T(8,128)(2,1)S(1)} %get-tuple-element.92), channel_id=1, source_target_pairs={{0,16},{1,17},{2,18},{3,19},{8,24},{9,25},{10,26},{11,27},{16,0},{... | collective-permute-start | bytes 884744 | tf_op jit(solution)/shard_map/ppermute | solution.py:620
  37.9 1.6 %collective-permute-start.6 = (bf16[2,4,2,72,128]{4,3,2,1,0:T(8,128)(2,1)S(1)}, bf16[2,4,2,72,128]{4,3,2,1,0:T(8,128)(2,1)S(1)}, u32[]{:S(2)}, u32[]{:S(2)}) collective-permute-start(bf16[2,4,2,72,128]{4,3,2,1,0:T(8,128)(2,1)S(1)} %get-tuple-element.93), channel_id=1, source_target_pairs={{0,20},{1,21},{2,22},{3,23},{8,28},{9,29},{10,30},{11,31},{16,4},{... | collective-permute-start | bytes 884744 | tf_op jit(solution)/shard_map/ppermute | solution.py:620
  39.4 3.1 %collective-permute-done.3.refs_4_ = bf16[2,4,2,72,128]{4,3,2,1,0:T(8,128)(2,1)S(1)} collective-permute-done((bf16[2,4,2,72,128]{4,3,2,1,0:T(8,128)(2,1)S(1)}, bf16[2,4,2,72,128]{4,3,2,1,0:T(8,128)(2,1)S(1)}, u32[]{:S(2)}, u32[]{:S(2)}) %collective-permute-start.3) | collective-permute-done | bytes 294944 | tf_op jit(solution)/shard_map/ppermute | solution.py:620
  42.5 0.7 collective-permute-done.4.refs_5_
  43.1 1.5 %collective-permute-done.5.refs_6_ = bf16[2,4,2,72,128]{4,3,2,1,0:T(8,128)(2,1)S(1)} collective-permute-done((bf16[2,4,2,72,128]{4,3,2,1,0:T(8,128)(2,1)S(1)}, bf16[2,4,2,72,128]{4,3,2,1,0:T(8,128)(2,1)S(1)}, u32[]{:S(2)}, u32[]{:S(2)}) %collective-permute-start.5) | collective-permute-done | bytes 294944 | tf_op jit(solution)/shard_map/ppermute | solution.py:620
  44.7 2.7 %collective-permute-done.6.refs_7_ = bf16[2,4,2,72,128]{4,3,2,1,0:T(8,128)(2,1)S(1)} collective-permute-done((bf16[2,4,2,72,128]{4,3,2,1,0:T(8,128)(2,1)S(1)}, bf16[2,4,2,72,128]{4,3,2,1,0:T(8,128)(2,1)S(1)}, u32[]{:S(2)}, u32[]{:S(2)}) %collective-permute-start.6) | collective-permute-done | bytes 294944 | tf_op jit(solution)/shard_map/ppermute | solution.py:620
  47.3 0.2 split_second.1
  47.5 0.4 collective-permute-start.7
  47.9 2.3 %collective-permute-start.8 = (bf16[4,2,72,128]{3,2,1,0:T(8,128)(2,1)S(1)}, bf16[4,2,72,128]{3,2,1,0:T(8,128)(2,1)S(1)}, u32[]{:S(2)}, u32[]{:S(2)}) collective-permute-start(bf16[4,2,72,128]{3,2,1,0:T(8,128)(2,1)S(1)} %get-tuple-element.99), channel_id=1, source_target_pairs={{0,1},{1,0},{2,3},{3,2},{8,9},{9,8},{10,11},{11,10},{16,17},{17,16... | collective-permute-start | bytes 442376 | tf_op jit(solution)/shard_map/ppermute | solution.py:622
  50.2 2.0 %collective-permute-start.9 = (bf16[4,2,72,128]{3,2,1,0:T(8,128)(2,1)S(1)}, bf16[4,2,72,128]{3,2,1,0:T(8,128)(2,1)S(1)}, u32[]{:S(2)}, u32[]{:S(2)}) collective-permute-start(bf16[4,2,72,128]{3,2,1,0:T(8,128)(2,1)S(1)} %get-tuple-element.100), channel_id=1, source_target_pairs={{0,20},{1,21},{2,22},{3,23},{8,28},{9,29},{10,30},{11,31},{16,4},{... | collective-permute-start | bytes 442376 | tf_op jit(solution)/shard_map/ppermute | solution.py:622
  52.2 0.0 collective-permute-start.10
  52.2 0.6 collective-permute-done.7.refs_4_
  52.8 0.5 collective-permute-done.8.refs_5_
  53.3 3.2 %collective-permute-done.9.refs_6_ = bf16[4,2,72,128]{3,2,1,0:T(8,128)(2,1)S(1)} collective-permute-done((bf16[4,2,72,128]{3,2,1,0:T(8,128)(2,1)S(1)}, bf16[4,2,72,128]{3,2,1,0:T(8,128)(2,1)S(1)}, u32[]{:S(2)}, u32[]{:S(2)}) %collective-permute-start.9) | collective-permute-done | bytes 147488 | tf_op jit(solution)/shard_map/ppermute | solution.py:622
  56.5 1.1 %collective-permute-done.10.refs_7_ = bf16[4,2,72,128]{3,2,1,0:T(8,128)(2,1)S(1)} collective-permute-done((bf16[4,2,72,128]{3,2,1,0:T(8,128)(2,1)S(1)}, bf16[4,2,72,128]{3,2,1,0:T(8,128)(2,1)S(1)}, u32[]{:S(2)}, u32[]{:S(2)}) %collective-permute-start.10) | collective-permute-done | bytes 147488 | tf_op jit(solution)/shard_map/ppermute | solution.py:622
  57.6 0.1 split_third.1
  57.7 0.1 collective-permute-start.11
  57.8 0.1 collective-permute-start.12
  57.9 5.0 %collective-permute-done.11.refs_2_ = bf16[2,4,72,128]{3,2,1,0:T(8,128)(2,1)S(1)} collective-permute-done((bf16[2,4,72,128]{3,2,1,0:T(8,128)(2,1)S(1)}, bf16[2,4,72,128]{3,2,1,0:T(8,128)(2,1)S(1)}, u32[]{:S(2)}, u32[]{:S(2)}) %collective-permute-start.11) | collective-permute-done | bytes 147488 | tf_op jit(solution)/shard_map/ppermute | solution.py:624
  62.9 0.1 collective-permute-done.12.refs_3_
  63.1 1.1 %collective-permute-start.13 = (bf16[4,72,128]{2,1,0:T(8,128)(2,1)S(1)}, bf16[4,72,128]{2,1,0:T(8,128)(2,1)S(1)}, u32[]{:S(2)}, u32[]{:S(2)}) collective-permute-start(bf16[4,72,128]{2,1,0:T(8,128)(2,1)S(1)} %get-tuple-element.108), channel_id=1, source_target_pairs={{0,20},{1,21},{2,22},{3,23},{8,28},{9,29},{10,30},{11,31},{16,4},{... | collective-permute-start | bytes 221192 | tf_op jit(solution)/shard_map/ppermute | solution.py:626
  64.1 1.5 %collective-permute-start.14 = (bf16[4,72,128]{2,1,0:T(8,128)(2,1)S(1)}, bf16[4,72,128]{2,1,0:T(8,128)(2,1)S(1)}, u32[]{:S(2)}, u32[]{:S(2)}) collective-permute-start(bf16[4,72,128]{2,1,0:T(8,128)(2,1)S(1)} %get-tuple-element.109), channel_id=1, source_target_pairs={{0,3},{1,2},{2,1},{3,0},{8,11},{9,10},{10,9},{11,8},{16,19},{17,18... | collective-permute-start | bytes 221192 | tf_op jit(solution)/shard_map/ppermute | solution.py:626
  65.6 3.1 %collective-permute-done.13.refs_2_ = bf16[4,72,128]{2,1,0:T(8,128)(2,1)S(1)} collective-permute-done((bf16[4,72,128]{2,1,0:T(8,128)(2,1)S(1)}, bf16[4,72,128]{2,1,0:T(8,128)(2,1)S(1)}, u32[]{:S(2)}, u32[]{:S(2)}) %collective-permute-start.13) | collective-permute-done | bytes 73760 | tf_op jit(solution)/shard_map/ppermute | solution.py:626
  68.7 0.0 collective-permute-done.14.refs_3_
  68.8 20.3 %all_to_all.10 = bf16[8,72,128]{2,1,0:T(8,128)(2,1)S(1)} all-to-all(bf16[8,72,128]{2,1,0:T(8,128)(2,1)S(1)} %join.1), channel_id=1, replica_groups={{0,32,64,96,128,160,192,224},{1,33,65,97,129,161,193,225},{2,34,66,98,1..., dimensions={0} | all-to-all | bytes 294912 | tf_op jit(solution)/shard_map/all_to_all | solution.py:531
  89.1 14.0 %all_to_all.11.t = bf16[8,72,128]{2,1,0:T(8,128)(2,1)} all-to-all(bf16[8,72,128]{2,1,0:T(8,128)(2,1)S(1)} %broadcast_in_dim.31), channel_id=1, replica_groups=mesh['frame'=32,'rec'=8] {'rec'}, dimensions={0} | all-to-all | bytes 294912 | tf_op jit(solution)/shard_map/all_to_all | solution.py:629
  103.1 1.6 %unpack.1 = (f32[16,1536]{1,0:T(8,128)}, f32[16,1280]{1,0:T(8,128)}, f32[48,512]{1,0:T(8,128)}, f32[8,16]{1,0:T(8,128)}, f32[1,16]{1,0:T(1,128)}, /*index=5*/f32...) custom-call(s32[1]{0:T(128)} %bitcast.pos, ...), custom_call_target="tpu_custom_call" | custom-call | tf_op jit(solution)/shard_map/unpack/pallas_call | solution.py:500
  (7 shorter events, 0.1 us)
Async XLA Ops:
  2.2 8.0 %collective-permute-start = (bf16[32,128]{1,0:T(8,128)(2,1)S(1)}, bf16[32,128]{1,0:T(8,128)(2,1)S(1)}, u32[]{:S(2)}, u32[]{:S(2)}) collective-permute-start(bf16[32,128]{1,0:T(8,128)(2,1)S(1)} %pad_maximum_fusion), channel_id=1, source_target_pairs={{0,8},{8,16},{16,24},{24,32},{32,40},{40,48},{48,56},{56,64},{64,7... | collective-permute-start | bytes 24584 | tf_op jit(solution)/shard_map/ppermute | solution.py:641
  3.9 6.3 %collective-permute-start.1 = (bf16[32,128]{1,0:T(8,128)(2,1)S(1)}, bf16[32,128]{1,0:T(8,128)(2,1)S(1)}, u32[]{:S(2)}, u32[]{:S(2)}) collective-permute-start(bf16[32,128]{1,0:T(8,128)(2,1)S(1)} %pad_maximum_fusion.1), channel_id=1, source_target_pairs={{8,0},{16,8},{24,16},{32,24},{40,32},{48,40},{56,48},{64,56},{72,6... | collective-permute-start | bytes 24584 | tf_op jit(solution)/shard_map/ppermute | solution.py:642
  25.9 6.7 %collective-permute-start.2 = (bf16[4,4,8,72,128]{4,3,2,1,0:T(8,128)(2,1)S(1)}, bf16[4,4,8,72,128]{4,3,2,1,0:T(8,128)(2,1)S(1)}, u32[]{:S(2)}, u32[]{:S(2)}) collective-permute-start(bf16[4,4,8,72,128]{4,3,2,1,0:T(8,128)(2,1)S(1)} %get-tuple-element.85), channel_id=1, source_target_pairs={{0,8},{1,9},{2,10},{3,11},{8,0},{9,1},{10,2},{11,3},{16,24},{17,25... | collective-permute-start | bytes 7077896 | tf_op jit(solution)/shard_map/ppermute | solution.py:618
  33.1 9.4 %collective-permute-start.3 = (bf16[2,4,2,72,128]{4,3,2,1,0:T(8,128)(2,1)S(1)}, bf16[2,4,2,72,128]{4,3,2,1,0:T(8,128)(2,1)S(1)}, u32[]{:S(2)}, u32[]{:S(2)}) collective-permute-start(bf16[2,4,2,72,128]{4,3,2,1,0:T(8,128)(2,1)S(1)} %get-tuple-element.90), channel_id=1, source_target_pairs={{0,1},{1,0},{2,3},{3,2},{8,9},{9,8},{10,11},{11,10},{16,17},{17,16... | collective-permute-start | bytes 884744 | tf_op jit(solution)/shard_map/ppermute | solution.py:620
  33.7 9.4 %collective-permute-start.4 = (bf16[2,4,2,72,128]{4,3,2,1,0:T(8,128)(2,1)S(1)}, bf16[2,4,2,72,128]{4,3,2,1,0:T(8,128)(2,1)S(1)}, u32[]{:S(2)}, u32[]{:S(2)}) collective-permute-start(bf16[2,4,2,72,128]{4,3,2,1,0:T(8,128)(2,1)S(1)} %get-tuple-element.91), channel_id=1, source_target_pairs={{0,3},{1,2},{2,1},{3,0},{8,11},{9,10},{10,9},{11,8},{16,19},{17,18... | collective-permute-start | bytes 884744 | tf_op jit(solution)/shard_map/ppermute | solution.py:620
  35.9 8.8 %collective-permute-start.5 = (bf16[2,4,2,72,128]{4,3,2,1,0:T(8,128)(2,1)S(1)}, bf16[2,4,2,72,128]{4,3,2,1,0:T(8,128)(2,1)S(1)}, u32[]{:S(2)}, u32[]{:S(2)}) collective-permute-start(bf16[2,4,2,72,128]{4,3,2,1,0:T(8,128)(2,1)S(1)} %get-tuple-element.92), channel_id=1, source_target_pairs={{0,16},{1,17},{2,18},{3,19},{8,24},{9,25},{10,26},{11,27},{16,0},{... | collective-permute-start | bytes 884744 | tf_op jit(solution)/shard_map/ppermute | solution.py:620
  37.9 9.5 %collective-permute-start.6 = (bf16[2,4,2,72,128]{4,3,2,1,0:T(8,128)(2,1)S(1)}, bf16[2,4,2,72,128]{4,3,2,1,0:T(8,128)(2,1)S(1)}, u32[]{:S(2)}, u32[]{:S(2)}) collective-permute-start(bf16[2,4,2,72,128]{4,3,2,1,0:T(8,128)(2,1)S(1)} %get-tuple-element.93), channel_id=1, source_target_pairs={{0,20},{1,21},{2,22},{3,23},{8,28},{9,29},{10,30},{11,31},{16,4},{... | collective-permute-start | bytes 884744 | tf_op jit(solution)/shard_map/ppermute | solution.py:620
  47.5 5.2 %collective-permute-start.7 = (bf16[4,2,72,128]{3,2,1,0:T(8,128)(2,1)S(1)}, bf16[4,2,72,128]{3,2,1,0:T(8,128)(2,1)S(1)}, u32[]{:S(2)}, u32[]{:S(2)}) collective-permute-start(bf16[4,2,72,128]{3,2,1,0:T(8,128)(2,1)S(1)} %get-tuple-element.98), channel_id=1, source_target_pairs={{0,3},{1,2},{2,1},{3,0},{8,11},{9,10},{10,9},{11,8},{16,19},{17,18... | collective-permute-start | bytes 442376 | tf_op jit(solution)/shard_map/ppermute | solution.py:622
  47.9 5.4 %collective-permute-start.8 = (bf16[4,2,72,128]{3,2,1,0:T(8,128)(2,1)S(1)}, bf16[4,2,72,128]{3,2,1,0:T(8,128)(2,1)S(1)}, u32[]{:S(2)}, u32[]{:S(2)}) collective-permute-start(bf16[4,2,72,128]{3,2,1,0:T(8,128)(2,1)S(1)} %get-tuple-element.99), channel_id=1, source_target_pairs={{0,1},{1,0},{2,3},{3,2},{8,9},{9,8},{10,11},{11,10},{16,17},{17,16... | collective-permute-start | bytes 442376 | tf_op jit(solution)/shard_map/ppermute | solution.py:622
  50.2 6.4 %collective-permute-start.9 = (bf16[4,2,72,128]{3,2,1,0:T(8,128)(2,1)S(1)}, bf16[4,2,72,128]{3,2,1,0:T(8,128)(2,1)S(1)}, u32[]{:S(2)}, u32[]{:S(2)}) collective-permute-start(bf16[4,2,72,128]{3,2,1,0:T(8,128)(2,1)S(1)} %get-tuple-element.100), channel_id=1, source_target_pairs={{0,20},{1,21},{2,22},{3,23},{8,28},{9,29},{10,30},{11,31},{16,4},{... | collective-permute-start | bytes 442376 | tf_op jit(solution)/shard_map/ppermute | solution.py:622
  52.2 5.4 %collective-permute-start.10 = (bf16[4,2,72,128]{3,2,1,0:T(8,128)(2,1)S(1)}, bf16[4,2,72,128]{3,2,1,0:T(8,128)(2,1)S(1)}, u32[]{:S(2)}, u32[]{:S(2)}) collective-permute-start(bf16[4,2,72,128]{3,2,1,0:T(8,128)(2,1)S(1)} %get-tuple-element.101), channel_id=1, source_target_pairs={{0,16},{1,17},{2,18},{3,19},{8,24},{9,25},{10,26},{11,27},{16,0},{... | collective-permute-start | bytes 442376 | tf_op jit(solution)/shard_map/ppermute | solution.py:622
  57.7 5.2 %collective-permute-start.11 = (bf16[2,4,72,128]{3,2,1,0:T(8,128)(2,1)S(1)}, bf16[2,4,72,128]{3,2,1,0:T(8,128)(2,1)S(1)}, u32[]{:S(2)}, u32[]{:S(2)}) collective-permute-start(bf16[2,4,72,128]{3,2,1,0:T(8,128)(2,1)S(1)} %get-tuple-element.104), channel_id=1, source_target_pairs={{0,16},{1,17},{2,18},{3,19},{8,24},{9,25},{10,26},{11,27},{16,0},{... | collective-permute-start | bytes 442376 | tf_op jit(solution)/shard_map/ppermute | solution.py:624
  57.8 5.2 %collective-permute-start.12 = (bf16[2,4,72,128]{3,2,1,0:T(8,128)(2,1)S(1)}, bf16[2,4,72,128]{3,2,1,0:T(8,128)(2,1)S(1)}, u32[]{:S(2)}, u32[]{:S(2)}) collective-permute-start(bf16[2,4,72,128]{3,2,1,0:T(8,128)(2,1)S(1)} %get-tuple-element.105), channel_id=1, source_target_pairs={{0,1},{1,0},{2,3},{3,2},{8,9},{9,8},{10,11},{11,10},{16,17},{17,16... | collective-permute-start | bytes 442376 | tf_op jit(solution)/shard_map/ppermute | solution.py:624
  63.1 5.7 %collective-permute-start.13 = (bf16[4,72,128]{2,1,0:T(8,128)(2,1)S(1)}, bf16[4,72,128]{2,1,0:T(8,128)(2,1)S(1)}, u32[]{:S(2)}, u32[]{:S(2)}) collective-permute-start(bf16[4,72,128]{2,1,0:T(8,128)(2,1)S(1)} %get-tuple-element.108), channel_id=1, source_target_pairs={{0,20},{1,21},{2,22},{3,23},{8,28},{9,29},{10,30},{11,31},{16,4},{... | collective-permute-start | bytes 221192 | tf_op jit(solution)/shard_map/ppermute | solution.py:626
  64.1 4.6 %collective-permute-start.14 = (bf16[4,72,128]{2,1,0:T(8,128)(2,1)S(1)}, bf16[4,72,128]{2,1,0:T(8,128)(2,1)S(1)}, u32[]{:S(2)}, u32[]{:S(2)}) collective-permute-start(bf16[4,72,128]{2,1,0:T(8,128)(2,1)S(1)} %get-tuple-element.109), channel_id=1, source_target_pairs={{0,3},{1,2},{2,1},{3,0},{8,11},{9,10},{10,9},{11,8},{16,19},{17,18... | collective-permute-start | bytes 221192 | tf_op jit(solution)/shard_map/ppermute | solution.py:626

commit v5 on v4

--- a/solution.py
+++ b/solution.py
@@ -144,11 +144,12 @@
     pos, cot, left, right, codes, embed_w, embed_b, depth_k, depth_b, gain, bias, up_w, up_b, down_w, down_b,
     scale, head_w, head_b, edge, tab, keep, send,
     feat, conv, cgrad, latg, samp, pair_rows, spec_in, xhat, rstd, normed, hid, dgelu, act, branch, latent, re, im,
-    logit_low, low, big, spec, lg, row_sums, sums, tiles, tall, rows,
+    logit_low, low, big, spec, lg, sums, tiles, tall, rows,
 ):
-    first_frame, length = pos[0], pos[1]
-    last_frame = pos[2]
-    core, my, mx = pos[3], pos[4], pos[5]
+    me, rec = lax.axis_index("frame"), lax.axis_index("rec")
+    first_frame, length = me * FRAMES, pos[0]
+    last_frame = lax.axis_size("frame") * FRAMES
+    core, my, mx = me & 1, 2 * (rec >> 2) + ((me >> 1) & 1), rec & 3
 
     def place(o, yl):
         part = o // SUB
@@ -395,18 +396,17 @@
 
     tiles[12:16, :] = jnp.zeros((4, 128), f32)
     tiles[26:32, :] = jnp.zeros((6, 128), f32)
-    row_sums[...] = jnp.zeros((8, 128), f32)
-
-    def small_step(p, _):
-        z, yl = p // 2, p % 2
-        for ref, f in ((keep, 2 * p + core), (send, 2 * p + 1 - core)):
-            row_sums[0:2, :] = tiles[pl.ds((48 * f) // 128, 2), :]
-            row_sums[2:4, :] = tiles[pl.ds(16 + (40 * f) // 128, 2), :]
-            dy, dx = place(7 * SUB, yl)
-            ref[dy, dx, z, 64:72, :] = row_sums[...].astype(bf16)
-        return 0
-
-    lax.fori_loop(0, 16, small_step, 0)
+    blank = jnp.zeros((4, 128), f32)
+
+    def bias_rows(f):
+        up, head = 48 * f // 128, 16 + 40 * f // 128
+        return jnp.concatenate([tiles[up : up + 2, :], tiles[head : head + 2, :], blank], axis=0).astype(bf16)
+
+    for p in range(16):
+        pair = [bias_rows(2 * p), bias_rows(2 * p + 1)]
+        dy, dx = place(7 * SUB, p % 2)
+        for ref, c in ((keep, core), (send, 1 - core)):
+            ref[dy, dx, p // 2, 64:72, :] = jnp.where(c == 0, pair[0], pair[1])
     for p in range(16):
         column = 128 * (p // 4)
         part = sums[:, column : column + 128].astype(bf16)
@@ -440,7 +440,6 @@
         vmem((D, FF), f32),
         vmem((10, ROWS, 128), f32),
         vmem((ROWS, D), f32),
-        vmem((8, 128), f32),
         vmem((24, D), f32),
         vmem((32, 128), f32),
         vmem((FF, D), f32),
@@ -459,8 +458,8 @@
     )(pos, *arrays)
 
 
-def unpack_kernel(pos, t, up_g, head_g, down_g, embed_w, embed_b, depth_k, up_b, head_b, *vectors):
-    f = pos[0]
+def unpack_kernel(t, up_g, head_g, down_g, embed_w, embed_b, depth_k, up_b, head_b, *vectors):
+    f = lax.axis_index("frame")
 
     def tile(o):
         return t[o // SUB, o % SUB : o % SUB + 8, :].astype(f32)
@@ -492,7 +491,7 @@
         ref[...] = joined[:, 0:width]
 
 
-def unpack(pos, t):
+def unpack(t):
     def shape(*s):
         return jax.ShapeDtypeStruct(s, f32)
 
@@ -502,10 +501,10 @@
         out_shape=(
             shape(16, FF), shape(16, NFFT), shape(48, D), shape(8, 16), shape(1, 16), shape(7, 16), shape(1, 48), shape(1, 40),
         ) + (shape(1, 16),) * 5,
-        in_specs=[pl.BlockSpec(memory_space=pltpu.SMEM), whole],
+        in_specs=[whole],
         out_specs=(whole,) * 13,
         name="unpack",
-    )(pos, t)
+    )(t)
 
 
 AXES = ("frame", "rec")
@@ -631,7 +630,6 @@
 
 def body(code_indices, lengths, cotangent, *weights):
     count = lax.axis_size("frame")
-    me, rec = lax.axis_index("frame"), lax.axis_index("rec")
     codes = code_indices[0].T
     samples = cotangent[0].astype(f32).reshape(640, 128)
     low = samples.astype(bf16)
@@ -640,11 +638,10 @@
     backward = [(b, a) for a, b in forward]
     left = lax.ppermute(jnp.concatenate([low[640 - LEFT :], codes_low[:, FRAMES - 128 :]]), "frame", forward)
     right = lax.ppermute(jnp.concatenate([low[:LEFT], codes_low[:, :128]]), "frame", backward)
-    pos = jnp.stack([me * FRAMES, lengths[0], count * FRAMES, me % 2, 2 * (rec // 4) + me // 2 % 2, rec % 4]).astype(jnp.int32)
     flat = [w if w.ndim == 2 else w[None] if w.size == D else w.reshape(-1, 128) for w in weights]
     ready = setup([codes, *flat, jnp.asarray(edges())])
-    t = reduce_all(*local_grads(pos, samples, left, right, ready))
-    up_g, head_g, down_g, embed_w, embed_b, depth_k, up_b, head_b, *vectors = unpack(me.astype(jnp.int32)[None], t)
+    t = reduce_all(*local_grads(lengths, samples, left, right, ready))
+    up_g, head_g, down_g, embed_w, embed_b, depth_k, up_b, head_b, *vectors = unpack(t)
     depth_b, gain, bias, down_b, scale = (v[0] for v in vectors)
     return (
         embed_w, embed_b[0], depth_k, depth_b, gain, bias, up_g, up_b[0], down_g, down_b, scale, head_g, head_b[0],

time: 105 us -> 104 us (level)
  Pallas kernels: 21 us -> 19.9 us
    pallas_call x1, Pallas kernels: 15.7 us -> 14.6 us  [local_grads(): pl.pallas_call(local_kernel, out_shape=(jax.ShapeDtypeStruct((4, 4, 8, SU...]
where the time goes in v5:
time: 104 us
  blocking collectives  34.2 us (33%)
  waiting for transfers between devices  25.7 us (25%)
  Pallas kernels  19.9 us (19%)
  starting transfers between devices  19.3 us (19%)
  other arithmetic  2.05 us (2%)
  between operations  1.57 us (2%)
    all_to_all x1, blocking collectives, exchange(): lax.all_to_all(array, AXES, split_axis=0, concat_axis=0, axis_index_group...  20.3 us
    pallas_call x1, Pallas kernels, local_grads(): pl.pallas_call(local_kernel, out_shape=(jax.ShapeDtypeStruct((4, 4, 8, SU...  14.6 us
    all_to_all x1, blocking collectives, reduce_all(): lax.all_to_all(jnp.broadcast_to(mine, (8, SUB, 128)), 'rec', split_axis=0...  14 us
    ppermute x4, waiting for transfers between devices, reduce_all(): lax.ppermute(a, AXES, partners(AXIS_OF[k], k % 2))  7.92 us
    ppermute x4, starting transfers between devices, reduce_all(): lax.ppermute(a, AXES, partners(AXIS_OF[k], k % 2))  6.32 us
    ppermute x4, waiting for transfers between devices, reduce_all(): lax.ppermute(a, AXES, partners(AXIS_OF[k], 1 - k % 2))  5.39 us
    ppermute x2, waiting for transfers between devices, reduce_all(): lax.ppermute(a, AXES, partners('yx'[g], 0))  5.13 us
    ppermute x4, starting transfers between devices, reduce_all(): lax.ppermute(a, AXES, partners(AXIS_OF[k], 1 - k % 2))  4.68 us
  transfers between devices with their start and end apart: 15, of which 12 were waited for; matrix products, arithmetic and copies ran while one was open for 1% of the time, Pallas kernels for 3%

profile of v5, /device:TPU:2, one launch (start us, length us, event | category | flops | bytes accessed | tf_op | source)
XLA Modules:
  0.0 103.7 jit_solution(16185887786370079843)
XLA Ops:
  0.6 0.7 bitcast_convert_fusion
  1.4 0.8 slice_reduce_fusion
  2.2 1.7 %collective-permute-start = (bf16[32,128]{1,0:T(8,128)(2,1)S(1)}, bf16[32,128]{1,0:T(8,128)(2,1)S(1)}, u32[]{:S(2)}, u32[]{:S(2)}) collective-permute-start(bf16[32,128]{1,0:T(8,128)(2,1)S(1)} %pad_maximum_fusion), channel_id=1, source_target_pairs={{0,8},{8,16},{16,24},{24,32},{32,40},{40,48},{48,56},{56,64},{64,7... | collective-permute-start | bytes 24584 | tf_op jit(solution)/shard_map/ppermute | solution.py:639
  3.9 1.3 %collective-permute-start.1 = (bf16[32,128]{1,0:T(8,128)(2,1)S(1)}, bf16[32,128]{1,0:T(8,128)(2,1)S(1)}, u32[]{:S(2)}, u32[]{:S(2)}) collective-permute-start(bf16[32,128]{1,0:T(8,128)(2,1)S(1)} %pad_maximum_fusion.1), channel_id=1, source_target_pairs={{8,0},{16,8},{24,16},{32,24},{40,32},{48,40},{56,48},{64,56},{72,6... | collective-permute-start | bytes 24584 | tf_op jit(solution)/shard_map/ppermute | solution.py:640
  5.2 1.3 %convert_element_type.16 = f32[1,81920]{1,0:T(1,128)S(1)} convert(bf16[1,81920]{1,0:T(2,128)(2,1)} %param.20) | non-fusion elementwise | flops 81920 | bytes 491520 | tf_op jit(solution)/shard_map/convert_element_type | solution.py:634
  7.2 2.9 %setup.1 = (s32[8,256]{1,0:T(8,128)S(1)}, f32[8,512]{1,0:T(8,128)S(1)}, f32[1,512]{1,0:T(1,128)S(1)}, f32[7,512]{1,0:T(8,128)S(1)}, f32[1,512]{1,0:T(1,128)S(1)}...) custom-call(s32[8,256]{1,0:T(8,128)} %bitcast.24, ...), custom_call_target="tpu_custom_call" | custom-call | tf_op jit(solution)/shard_map/setup/pallas_call | solution.py:132
  10.1 0.0 collective-permute-done.left
  10.1 0.0 collective-permute-done.1.right
  10.1 14.6 %local_grads.1 = (bf16[4,4,8,72,128]{4,3,2,1,0:T(8,128)(2,1)S(1)}, bf16[4,4,8,72,128]{4,3,2,1,0:T(8,128)(2,1)S(1)}) custom-call(s32[1]{0:T(128)S(6)} %copy.31.pos, f32[640,128]{1,0:T(8,128)S(1)} %bitcast.23, bf16[32,128]{1,0:T(8,128)(2,1)S(1)} %collective-permute-done.left, bf16[32,128]{1,0:T(8,128)(2,1)S(1)} %collective-permute-done.1.right, ...), custom_call_target="tpu_custom_call" | custom-call | tf_op jit(solution)/shard_map/local_grads/pallas_call | solution.py:450
  24.7 2.6 %collective-permute-start.2 = (bf16[4,4,8,72,128]{4,3,2,1,0:T(8,128)(2,1)S(1)}, bf16[4,4,8,72,128]{4,3,2,1,0:T(8,128)(2,1)S(1)}, u32[]{:S(2)}, u32[]{:S(2)}) collective-permute-start(bf16[4,4,8,72,128]{4,3,2,1,0:T(8,128)(2,1)S(1)} %get-tuple-element.85), channel_id=1, source_target_pairs={{0,8},{1,9},{2,10},{3,11},{8,0},{9,1},{10,2},{11,3},{16,24},{17,25... | collective-permute-start | bytes 7077896 | tf_op jit(solution)/shard_map/ppermute | solution.py:617
  27.2 4.2 %collective-permute-done.2.other = bf16[4,4,8,72,128]{4,3,2,1,0:T(8,128)(2,1)S(1)} collective-permute-done((bf16[4,4,8,72,128]{4,3,2,1,0:T(8,128)(2,1)S(1)}, bf16[4,4,8,72,128]{4,3,2,1,0:T(8,128)(2,1)S(1)}, u32[]{:S(2)}, u32[]{:S(2)}) %collective-permute-start.2) | collective-permute-done | bytes 2359328 | tf_op jit(solution)/shard_map/ppermute | solution.py:617
  31.4 0.5 split_first.1
  31.9 0.6 collective-permute-start.3
  32.5 2.2 %collective-permute-start.4 = (bf16[2,4,2,72,128]{4,3,2,1,0:T(8,128)(2,1)S(1)}, bf16[2,4,2,72,128]{4,3,2,1,0:T(8,128)(2,1)S(1)}, u32[]{:S(2)}, u32[]{:S(2)}) collective-permute-start(bf16[2,4,2,72,128]{4,3,2,1,0:T(8,128)(2,1)S(1)} %get-tuple-element.91), channel_id=1, source_target_pairs={{0,3},{1,2},{2,1},{3,0},{8,11},{9,10},{10,9},{11,8},{16,19},{17,18... | collective-permute-start | bytes 884744 | tf_op jit(solution)/shard_map/ppermute | solution.py:619
  34.7 2.0 %collective-permute-start.5 = (bf16[2,4,2,72,128]{4,3,2,1,0:T(8,128)(2,1)S(1)}, bf16[2,4,2,72,128]{4,3,2,1,0:T(8,128)(2,1)S(1)}, u32[]{:S(2)}, u32[]{:S(2)}) collective-permute-start(bf16[2,4,2,72,128]{4,3,2,1,0:T(8,128)(2,1)S(1)} %get-tuple-element.92), channel_id=1, source_target_pairs={{0,16},{1,17},{2,18},{3,19},{8,24},{9,25},{10,26},{11,27},{16,0},{... | collective-permute-start | bytes 884744 | tf_op jit(solution)/shard_map/ppermute | solution.py:619
  36.7 1.5 %collective-permute-start.6 = (bf16[2,4,2,72,128]{4,3,2,1,0:T(8,128)(2,1)S(1)}, bf16[2,4,2,72,128]{4,3,2,1,0:T(8,128)(2,1)S(1)}, u32[]{:S(2)}, u32[]{:S(2)}) collective-permute-start(bf16[2,4,2,72,128]{4,3,2,1,0:T(8,128)(2,1)S(1)} %get-tuple-element.93), channel_id=1, source_target_pairs={{0,20},{1,21},{2,22},{3,23},{8,28},{9,29},{10,30},{11,31},{16,4},{... | collective-permute-start | bytes 884744 | tf_op jit(solution)/shard_map/ppermute | solution.py:619
  38.2 3.1 %collective-permute-done.3.refs_4_ = bf16[2,4,2,72,128]{4,3,2,1,0:T(8,128)(2,1)S(1)} collective-permute-done((bf16[2,4,2,72,128]{4,3,2,1,0:T(8,128)(2,1)S(1)}, bf16[2,4,2,72,128]{4,3,2,1,0:T(8,128)(2,1)S(1)}, u32[]{:S(2)}, u32[]{:S(2)}) %collective-permute-start.3) | collective-permute-done | bytes 294944 | tf_op jit(solution)/shard_map/ppermute | solution.py:619
  41.3 0.7 collective-permute-done.4.refs_5_
  41.9 1.5 %collective-permute-done.5.refs_6_ = bf16[2,4,2,72,128]{4,3,2,1,0:T(8,128)(2,1)S(1)} collective-permute-done((bf16[2,4,2,72,128]{4,3,2,1,0:T(8,128)(2,1)S(1)}, bf16[2,4,2,72,128]{4,3,2,1,0:T(8,128)(2,1)S(1)}, u32[]{:S(2)}, u32[]{:S(2)}) %collective-permute-start.5) | collective-permute-done | bytes 294944 | tf_op jit(solution)/shard_map/ppermute | solution.py:619
  43.5 2.7 %collective-permute-done.6.refs_7_ = bf16[2,4,2,72,128]{4,3,2,1,0:T(8,128)(2,1)S(1)} collective-permute-done((bf16[2,4,2,72,128]{4,3,2,1,0:T(8,128)(2,1)S(1)}, bf16[2,4,2,72,128]{4,3,2,1,0:T(8,128)(2,1)S(1)}, u32[]{:S(2)}, u32[]{:S(2)}) %collective-permute-start.6) | collective-permute-done | bytes 294944 | tf_op jit(solution)/shard_map/ppermute | solution.py:619
  46.1 0.2 split_second.1
  46.3 0.4 collective-permute-start.7
  46.7 2.3 %collective-permute-start.8 = (bf16[4,2,72,128]{3,2,1,0:T(8,128)(2,1)S(1)}, bf16[4,2,72,128]{3,2,1,0:T(8,128)(2,1)S(1)}, u32[]{:S(2)}, u32[]{:S(2)}) collective-permute-start(bf16[4,2,72,128]{3,2,1,0:T(8,128)(2,1)S(1)} %get-tuple-element.99), channel_id=1, source_target_pairs={{0,1},{1,0},{2,3},{3,2},{8,9},{9,8},{10,11},{11,10},{16,17},{17,16... | collective-permute-start | bytes 442376 | tf_op jit(solution)/shard_map/ppermute | solution.py:621
  49.0 2.0 %collective-permute-start.9 = (bf16[4,2,72,128]{3,2,1,0:T(8,128)(2,1)S(1)}, bf16[4,2,72,128]{3,2,1,0:T(8,128)(2,1)S(1)}, u32[]{:S(2)}, u32[]{:S(2)}) collective-permute-start(bf16[4,2,72,128]{3,2,1,0:T(8,128)(2,1)S(1)} %get-tuple-element.100), channel_id=1, source_target_pairs={{0,20},{1,21},{2,22},{3,23},{8,28},{9,29},{10,30},{11,31},{16,4},{... | collective-permute-start | bytes 442376 | tf_op jit(solution)/shard_map/ppermute | solution.py:621
  51.0 0.0 collective-permute-start.10
  51.0 0.6 collective-permute-done.7.refs_4_
  51.6 0.5 collective-permute-done.8.refs_5_
  52.1 3.2 %collective-permute-done.9.refs_6_ = bf16[4,2,72,128]{3,2,1,0:T(8,128)(2,1)S(1)} collective-permute-done((bf16[4,2,72,128]{3,2,1,0:T(8,128)(2,1)S(1)}, bf16[4,2,72,128]{3,2,1,0:T(8,128)(2,1)S(1)}, u32[]{:S(2)}, u32[]{:S(2)}) %collective-permute-start.9) | collective-permute-done | bytes 147488 | tf_op jit(solution)/shard_map/ppermute | solution.py:621
  55.3 1.1 %collective-permute-done.10.refs_7_ = bf16[4,2,72,128]{3,2,1,0:T(8,128)(2,1)S(1)} collective-permute-done((bf16[4,2,72,128]{3,2,1,0:T(8,128)(2,1)S(1)}, bf16[4,2,72,128]{3,2,1,0:T(8,128)(2,1)S(1)}, u32[]{:S(2)}, u32[]{:S(2)}) %collective-permute-start.10) | collective-permute-done | bytes 147488 | tf_op jit(solution)/shard_map/ppermute | solution.py:621
  56.4 0.1 split_third.1
  56.5 0.1 collective-permute-start.11
  56.6 0.1 collective-permute-start.12
  56.7 5.0 %collective-permute-done.11.refs_2_ = bf16[2,4,72,128]{3,2,1,0:T(8,128)(2,1)S(1)} collective-permute-done((bf16[2,4,72,128]{3,2,1,0:T(8,128)(2,1)S(1)}, bf16[2,4,72,128]{3,2,1,0:T(8,128)(2,1)S(1)}, u32[]{:S(2)}, u32[]{:S(2)}) %collective-permute-start.11) | collective-permute-done | bytes 147488 | tf_op jit(solution)/shard_map/ppermute | solution.py:623
  61.7 0.1 collective-permute-done.12.refs_3_
  61.9 1.1 %collective-permute-start.13 = (bf16[4,72,128]{2,1,0:T(8,128)(2,1)S(1)}, bf16[4,72,128]{2,1,0:T(8,128)(2,1)S(1)}, u32[]{:S(2)}, u32[]{:S(2)}) collective-permute-start(bf16[4,72,128]{2,1,0:T(8,128)(2,1)S(1)} %get-tuple-element.108), channel_id=1, source_target_pairs={{0,20},{1,21},{2,22},{3,23},{8,28},{9,29},{10,30},{11,31},{16,4},{... | collective-permute-start | bytes 221192 | tf_op jit(solution)/shard_map/ppermute | solution.py:625
  62.9 1.5 %collective-permute-start.14 = (bf16[4,72,128]{2,1,0:T(8,128)(2,1)S(1)}, bf16[4,72,128]{2,1,0:T(8,128)(2,1)S(1)}, u32[]{:S(2)}, u32[]{:S(2)}) collective-permute-start(bf16[4,72,128]{2,1,0:T(8,128)(2,1)S(1)} %get-tuple-element.109), channel_id=1, source_target_pairs={{0,3},{1,2},{2,1},{3,0},{8,11},{9,10},{10,9},{11,8},{16,19},{17,18... | collective-permute-start | bytes 221192 | tf_op jit(solution)/shard_map/ppermute | solution.py:625
  64.4 3.1 %collective-permute-done.13.refs_2_ = bf16[4,72,128]{2,1,0:T(8,128)(2,1)S(1)} collective-permute-done((bf16[4,72,128]{2,1,0:T(8,128)(2,1)S(1)}, bf16[4,72,128]{2,1,0:T(8,128)(2,1)S(1)}, u32[]{:S(2)}, u32[]{:S(2)}) %collective-permute-start.13) | collective-permute-done | bytes 73760 | tf_op jit(solution)/shard_map/ppermute | solution.py:625
  67.5 0.0 collective-permute-done.14.refs_3_
  67.6 20.3 %all_to_all.10 = bf16[8,72,128]{2,1,0:T(8,128)(2,1)S(1)} all-to-all(bf16[8,72,128]{2,1,0:T(8,128)(2,1)S(1)} %join.1), channel_id=1, replica_groups={{0,32,64,96,128,160,192,224},{1,33,65,97,129,161,193,225},{2,34,66,98,1..., dimensions={0} | all-to-all | bytes 294912 | tf_op jit(solution)/shard_map/all_to_all | solution.py:530
  87.9 14.0 %all_to_all.11.t = bf16[8,72,128]{2,1,0:T(8,128)(2,1)} all-to-all(bf16[8,72,128]{2,1,0:T(8,128)(2,1)S(1)} %broadcast_in_dim.27), channel_id=1, replica_groups=mesh['frame'=32,'rec'=8] {'rec'}, dimensions={0} | all-to-all | bytes 294912 | tf_op jit(solution)/shard_map/all_to_all | solution.py:628
  101.9 1.6 %unpack.1 = (f32[16,1536]{1,0:T(8,128)}, f32[16,1280]{1,0:T(8,128)}, f32[48,512]{1,0:T(8,128)}, f32[8,16]{1,0:T(8,128)}, f32[1,16]{1,0:T(1,128)}, /*index=5*/f32...) custom-call(bf16[8,72,128]{2,1,0:T(8,128)(2,1)} %all_to_all.11.t), custom_call_target="tpu_custom_call" | custom-call | tf_op jit(solution)/shard_map/unpack/pallas_call | solution.py:499
  (7 shorter events, 0.1 us)
Async XLA Ops:
  2.2 7.9 %collective-permute-start = (bf16[32,128]{1,0:T(8,128)(2,1)S(1)}, bf16[32,128]{1,0:T(8,128)(2,1)S(1)}, u32[]{:S(2)}, u32[]{:S(2)}) collective-permute-start(bf16[32,128]{1,0:T(8,128)(2,1)S(1)} %pad_maximum_fusion), channel_id=1, source_target_pairs={{0,8},{8,16},{16,24},{24,32},{32,40},{40,48},{48,56},{56,64},{64,7... | collective-permute-start | bytes 24584 | tf_op jit(solution)/shard_map/ppermute | solution.py:639
  3.9 6.2 %collective-permute-start.1 = (bf16[32,128]{1,0:T(8,128)(2,1)S(1)}, bf16[32,128]{1,0:T(8,128)(2,1)S(1)}, u32[]{:S(2)}, u32[]{:S(2)}) collective-permute-start(bf16[32,128]{1,0:T(8,128)(2,1)S(1)} %pad_maximum_fusion.1), channel_id=1, source_target_pairs={{8,0},{16,8},{24,16},{32,24},{40,32},{48,40},{56,48},{64,56},{72,6... | collective-permute-start | bytes 24584 | tf_op jit(solution)/shard_map/ppermute | solution.py:640
  24.7 6.7 %collective-permute-start.2 = (bf16[4,4,8,72,128]{4,3,2,1,0:T(8,128)(2,1)S(1)}, bf16[4,4,8,72,128]{4,3,2,1,0:T(8,128)(2,1)S(1)}, u32[]{:S(2)}, u32[]{:S(2)}) collective-permute-start(bf16[4,4,8,72,128]{4,3,2,1,0:T(8,128)(2,1)S(1)} %get-tuple-element.85), channel_id=1, source_target_pairs={{0,8},{1,9},{2,10},{3,11},{8,0},{9,1},{10,2},{11,3},{16,24},{17,25... | collective-permute-start | bytes 7077896 | tf_op jit(solution)/shard_map/ppermute | solution.py:617
  31.9 9.4 %collective-permute-start.3 = (bf16[2,4,2,72,128]{4,3,2,1,0:T(8,128)(2,1)S(1)}, bf16[2,4,2,72,128]{4,3,2,1,0:T(8,128)(2,1)S(1)}, u32[]{:S(2)}, u32[]{:S(2)}) collective-permute-start(bf16[2,4,2,72,128]{4,3,2,1,0:T(8,128)(2,1)S(1)} %get-tuple-element.90), channel_id=1, source_target_pairs={{0,1},{1,0},{2,3},{3,2},{8,9},{9,8},{10,11},{11,10},{16,17},{17,16... | collective-permute-start | bytes 884744 | tf_op jit(solution)/shard_map/ppermute | solution.py:619
  32.5 9.4 %collective-permute-start.4 = (bf16[2,4,2,72,128]{4,3,2,1,0:T(8,128)(2,1)S(1)}, bf16[2,4,2,72,128]{4,3,2,1,0:T(8,128)(2,1)S(1)}, u32[]{:S(2)}, u32[]{:S(2)}) collective-permute-start(bf16[2,4,2,72,128]{4,3,2,1,0:T(8,128)(2,1)S(1)} %get-tuple-element.91), channel_id=1, source_target_pairs={{0,3},{1,2},{2,1},{3,0},{8,11},{9,10},{10,9},{11,8},{16,19},{17,18... | collective-permute-start | bytes 884744 | tf_op jit(solution)/shard_map/ppermute | solution.py:619
  34.7 8.8 %collective-permute-start.5 = (bf16[2,4,2,72,128]{4,3,2,1,0:T(8,128)(2,1)S(1)}, bf16[2,4,2,72,128]{4,3,2,1,0:T(8,128)(2,1)S(1)}, u32[]{:S(2)}, u32[]{:S(2)}) collective-permute-start(bf16[2,4,2,72,128]{4,3,2,1,0:T(8,128)(2,1)S(1)} %get-tuple-element.92), channel_id=1, source_target_pairs={{0,16},{1,17},{2,18},{3,19},{8,24},{9,25},{10,26},{11,27},{16,0},{... | collective-permute-start | bytes 884744 | tf_op jit(solution)/shard_map/ppermute | solution.py:619
  36.7 9.5 %collective-permute-start.6 = (bf16[2,4,2,72,128]{4,3,2,1,0:T(8,128)(2,1)S(1)}, bf16[2,4,2,72,128]{4,3,2,1,0:T(8,128)(2,1)S(1)}, u32[]{:S(2)}, u32[]{:S(2)}) collective-permute-start(bf16[2,4,2,72,128]{4,3,2,1,0:T(8,128)(2,1)S(1)} %get-tuple-element.93), channel_id=1, source_target_pairs={{0,20},{1,21},{2,22},{3,23},{8,28},{9,29},{10,30},{11,31},{16,4},{... | collective-permute-start | bytes 884744 | tf_op jit(solution)/shard_map/ppermute | solution.py:619
  46.3 5.2 %collective-permute-start.7 = (bf16[4,2,72,128]{3,2,1,0:T(8,128)(2,1)S(1)}, bf16[4,2,72,128]{3,2,1,0:T(8,128)(2,1)S(1)}, u32[]{:S(2)}, u32[]{:S(2)}) collective-permute-start(bf16[4,2,72,128]{3,2,1,0:T(8,128)(2,1)S(1)} %get-tuple-element.98), channel_id=1, source_target_pairs={{0,3},{1,2},{2,1},{3,0},{8,11},{9,10},{10,9},{11,8},{16,19},{17,18... | collective-permute-start | bytes 442376 | tf_op jit(solution)/shard_map/ppermute | solution.py:621
  46.7 5.4 %collective-permute-start.8 = (bf16[4,2,72,128]{3,2,1,0:T(8,128)(2,1)S(1)}, bf16[4,2,72,128]{3,2,1,0:T(8,128)(2,1)S(1)}, u32[]{:S(2)}, u32[]{:S(2)}) collective-permute-start(bf16[4,2,72,128]{3,2,1,0:T(8,128)(2,1)S(1)} %get-tuple-element.99), channel_id=1, source_target_pairs={{0,1},{1,0},{2,3},{3,2},{8,9},{9,8},{10,11},{11,10},{16,17},{17,16... | collective-permute-start | bytes 442376 | tf_op jit(solution)/shard_map/ppermute | solution.py:621
  49.0 6.4 %collective-permute-start.9 = (bf16[4,2,72,128]{3,2,1,0:T(8,128)(2,1)S(1)}, bf16[4,2,72,128]{3,2,1,0:T(8,128)(2,1)S(1)}, u32[]{:S(2)}, u32[]{:S(2)}) collective-permute-start(bf16[4,2,72,128]{3,2,1,0:T(8,128)(2,1)S(1)} %get-tuple-element.100), channel_id=1, source_target_pairs={{0,20},{1,21},{2,22},{3,23},{8,28},{9,29},{10,30},{11,31},{16,4},{... | collective-permute-start | bytes 442376 | tf_op jit(solution)/shard_map/ppermute | solution.py:621
  51.0 5.4 %collective-permute-start.10 = (bf16[4,2,72,128]{3,2,1,0:T(8,128)(2,1)S(1)}, bf16[4,2,72,128]{3,2,1,0:T(8,128)(2,1)S(1)}, u32[]{:S(2)}, u32[]{:S(2)}) collective-permute-start(bf16[4,2,72,128]{3,2,1,0:T(8,128)(2,1)S(1)} %get-tuple-element.101), channel_id=1, source_target_pairs={{0,16},{1,17},{2,18},{3,19},{8,24},{9,25},{10,26},{11,27},{16,0},{... | collective-permute-start | bytes 442376 | tf_op jit(solution)/shard_map/ppermute | solution.py:621
  56.5 5.2 %collective-permute-start.11 = (bf16[2,4,72,128]{3,2,1,0:T(8,128)(2,1)S(1)}, bf16[2,4,72,128]{3,2,1,0:T(8,128)(2,1)S(1)}, u32[]{:S(2)}, u32[]{:S(2)}) collective-permute-start(bf16[2,4,72,128]{3,2,1,0:T(8,128)(2,1)S(1)} %get-tuple-element.104), channel_id=1, source_target_pairs={{0,16},{1,17},{2,18},{3,19},{8,24},{9,25},{10,26},{11,27},{16,0},{... | collective-permute-start | bytes 442376 | tf_op jit(solution)/shard_map/ppermute | solution.py:623
  56.6 5.2 %collective-permute-start.12 = (bf16[2,4,72,128]{3,2,1,0:T(8,128)(2,1)S(1)}, bf16[2,4,72,128]{3,2,1,0:T(8,128)(2,1)S(1)}, u32[]{:S(2)}, u32[]{:S(2)}) collective-permute-start(bf16[2,4,72,128]{3,2,1,0:T(8,128)(2,1)S(1)} %get-tuple-element.105), channel_id=1, source_target_pairs={{0,1},{1,0},{2,3},{3,2},{8,9},{9,8},{10,11},{11,10},{16,17},{17,16... | collective-permute-start | bytes 442376 | tf_op jit(solution)/shard_map/ppermute | solution.py:623
  61.9 5.7 %collective-permute-start.13 = (bf16[4,72,128]{2,1,0:T(8,128)(2,1)S(1)}, bf16[4,72,128]{2,1,0:T(8,128)(2,1)S(1)}, u32[]{:S(2)}, u32[]{:S(2)}) collective-permute-start(bf16[4,72,128]{2,1,0:T(8,128)(2,1)S(1)} %get-tuple-element.108), channel_id=1, source_target_pairs={{0,20},{1,21},{2,22},{3,23},{8,28},{9,29},{10,30},{11,31},{16,4},{... | collective-permute-start | bytes 221192 | tf_op jit(solution)/shard_map/ppermute | solution.py:625
  62.9 4.6 %collective-permute-start.14 = (bf16[4,72,128]{2,1,0:T(8,128)(2,1)S(1)}, bf16[4,72,128]{2,1,0:T(8,128)(2,1)S(1)}, u32[]{:S(2)}, u32[]{:S(2)}) collective-permute-start(bf16[4,72,128]{2,1,0:T(8,128)(2,1)S(1)} %get-tuple-element.109), channel_id=1, source_target_pairs={{0,3},{1,2},{2,1},{3,0},{8,11},{9,10},{10,9},{11,8},{16,19},{17,18... | collective-permute-start | bytes 221192 | tf_op jit(solution)/shard_map/ppermute | solution.py:625

commit v6 on v5

--- a/solution.py
+++ b/solution.py
@@ -122,7 +122,7 @@
         tab[pl.ds(at, 16), BINS:] = (s * (window * imag_row)).astype(bf16)
         return c * cs - s * sn, s * cs + c * sn, wc * wcs - ws * wsn, ws * wcs + wc * wsn
 
-    lax.fori_loop(0, NFFT // 16, table_step, (trig[0:16, :], trig[16:32, :], trig[40:56, 0:128], trig[40:56, 128:256]))
+    lax.fori_loop(0, NFFT // 16, table_step, (trig[0:16, :], trig[16:32, :], trig[40:56, 0:128], trig[40:56, 128:256]), unroll=4)
     for copy in copies:
         copy.wait()
 
@@ -181,7 +181,7 @@
         feat[pl.ds(at, 8), :] = jnp.where(keep, feat[pl.ds(at, 8), :], 0.0).astype(bf16).astype(f32)
         return 0
 
-    lax.fori_loop(0, (FRAMES + 16) // 8, mask_step, 0)
+    lax.fori_loop(0, (FRAMES + 16) // 8, mask_step, 0, unroll=2)
 
     taps = [depth_k[j : j + 1, :] for j in range(KERNEL)]
     total = jnp.broadcast_to(depth_b[...], (FRAMES + 16, D))
@@ -251,7 +251,7 @@
         s = start + row * 128 + lax.broadcasted_iota(jnp.int32, (4, 128), 1)
         samp[at : at + 4, :] = jnp.where(s < limit, cot[at - LEFT : at - LEFT + 4, :] * values, 0.0)
 
-    lax.fori_loop(0, (LEFT * 2 + 640) // 8, sample_step, 0)
+    lax.fori_loop(0, (LEFT * 2 + 640) // 8, sample_step, 0, unroll=2)
 
     @pl.when(first_frame == 0)
     def _():
@@ -299,7 +299,7 @@
         return carry[0] + da[0:8] + da[8:16], carry[1] + dp[0:8] + dp[8:16]
 
     zero = jnp.zeros((8, BINS), f32)
-    da, dp = lax.fori_loop(0, FRAMES // 16, logit_step, (zero, zero))
+    da, dp = lax.fori_loop(0, FRAMES // 16, logit_step, (zero, zero), unroll=2)
     logit_grad_of(pl.ds(FRAMES, 16))
     head_sum = jnp.concatenate([jnp.sum(da, axis=0, keepdims=True), jnp.sum(dp, axis=0, keepdims=True)], axis=1)
     for t in range(10):
@@ -333,7 +333,7 @@
         return carry[0] + b[0:8] + b[8:16], carry[1] + g[0:8] + g[8:16]
 
     zero = jnp.zeros((8, D), f32)
-    scale_sum, latent_sum = lax.fori_loop(0, FRAMES // 16, latent_step, (zero, zero))
+    scale_sum, latent_sum = lax.fori_loop(0, FRAMES // 16, latent_step, (zero, zero), unroll=2)
     low[FRAMES:, :] = (scale[...] * latg[FRAMES:, :]).astype(bf16)
     sums[20:21, :] = jnp.sum(scale_sum, axis=0, keepdims=True)
     sums[19:20, :] = jnp.sum(latent_sum, axis=0, keepdims=True) * scale[...]
@@ -352,7 +352,7 @@
         g = hidden_grad_of(pl.ds(pl.multiple_of(i * 16, 16), 16))
         return carry + g[0:8] + g[8:16]
 
-    up_sum = lax.fori_loop(0, FRAMES // 16, hidden_step, jnp.zeros((8, FF), f32))
+    up_sum = lax.fori_loop(0, FRAMES // 16, hidden_step, jnp.zeros((8, FF), f32), unroll=2)
     hidden_grad_of(pl.ds(FRAMES, 16))
     up_sum = jnp.sum(up_sum, axis=0, keepdims=True)
     for t in range(12):

time: 104 us -> 104 us (level)
  no operation moved by 1% of the time
where the time goes in v6:
time: 104 us; the launch traced here: 103 us
  blocking collectives  34.2 us (33%)
  waiting for transfers between devices  25.7 us (25%)
  Pallas kernels  19.4 us (19%)
  starting transfers between devices  19.3 us (19%)
  other arithmetic  2.05 us (2%)
  between operations  1.57 us (2%)
    all_to_all x1, blocking collectives, exchange(): lax.all_to_all(array, AXES, split_axis=0, concat_axis=0, axis_index_group...  20.3 us
    pallas_call x1, Pallas kernels, local_grads(): pl.pallas_call(local_kernel, out_shape=(jax.ShapeDtypeStruct((4, 4, 8, SU...  14.1 us
    all_to_all x1, blocking collectives, reduce_all(): lax.all_to_all(jnp.broadcast_to(mine, (8, SUB, 128)), 'rec', split_axis=0...  14 us
    ppermute x4, waiting for transfers between devices, reduce_all(): lax.ppermute(a, AXES, partners(AXIS_OF[k], k % 2))  7.92 us
    ppermute x4, starting transfers between devices, reduce_all(): lax.ppermute(a, AXES, partners(AXIS_OF[k], k % 2))  6.32 us
    ppermute x4, waiting for transfers between devices, reduce_all(): lax.ppermute(a, AXES, partners(AXIS_OF[k], 1 - k % 2))  5.39 us
    ppermute x2, waiting for transfers between devices, reduce_all(): lax.ppermute(a, AXES, partners('yx'[g], 0))  5.13 us
    ppermute x4, starting transfers between devices, reduce_all(): lax.ppermute(a, AXES, partners(AXIS_OF[k], 1 - k % 2))  4.68 us
  transfers between devices with their start and end apart: 15, of which 12 were waited for; matrix products, arithmetic and copies ran while one was open for 1% of the time, Pallas kernels for 3%

profile of v6, /device:TPU:2, one launch (start us, length us, event | category | flops | bytes accessed | tf_op | source)
XLA Modules:
  0.0 103.1 jit_solution(9111974685444926153)
XLA Ops:
  0.6 0.7 bitcast_convert_fusion
  1.4 0.8 slice_reduce_fusion
  2.2 1.7 %collective-permute-start = (bf16[32,128]{1,0:T(8,128)(2,1)S(1)}, bf16[32,128]{1,0:T(8,128)(2,1)S(1)}, u32[]{:S(2)}, u32[]{:S(2)}) collective-permute-start(bf16[32,128]{1,0:T(8,128)(2,1)S(1)} %pad_maximum_fusion), channel_id=1, source_target_pairs={{0,8},{8,16},{16,24},{24,32},{32,40},{40,48},{48,56},{56,64},{64,7... | collective-permute-start | bytes 24584 | tf_op jit(solution)/shard_map/ppermute | solution.py:639
  3.9 1.3 %collective-permute-start.1 = (bf16[32,128]{1,0:T(8,128)(2,1)S(1)}, bf16[32,128]{1,0:T(8,128)(2,1)S(1)}, u32[]{:S(2)}, u32[]{:S(2)}) collective-permute-start(bf16[32,128]{1,0:T(8,128)(2,1)S(1)} %pad_maximum_fusion.1), channel_id=1, source_target_pairs={{8,0},{16,8},{24,16},{32,24},{40,32},{48,40},{56,48},{64,56},{72,6... | collective-permute-start | bytes 24584 | tf_op jit(solution)/shard_map/ppermute | solution.py:640
  5.2 1.3 %convert_element_type.16 = f32[1,81920]{1,0:T(1,128)S(1)} convert(bf16[1,81920]{1,0:T(2,128)(2,1)} %param.20) | non-fusion elementwise | flops 81920 | bytes 491520 | tf_op jit(solution)/shard_map/convert_element_type | solution.py:634
  7.2 2.8 %setup.1 = (s32[8,256]{1,0:T(8,128)S(1)}, f32[8,512]{1,0:T(8,128)S(1)}, f32[1,512]{1,0:T(1,128)S(1)}, f32[7,512]{1,0:T(8,128)S(1)}, f32[1,512]{1,0:T(1,128)S(1)}...) custom-call(s32[8,256]{1,0:T(8,128)} %bitcast.24, ...), custom_call_target="tpu_custom_call" | custom-call | tf_op jit(solution)/shard_map/setup/pallas_call | solution.py:132
  10.0 0.0 collective-permute-done.left
  10.0 0.0 collective-permute-done.1.right
  10.0 14.1 %local_grads.1 = (bf16[4,4,8,72,128]{4,3,2,1,0:T(8,128)(2,1)S(1)}, bf16[4,4,8,72,128]{4,3,2,1,0:T(8,128)(2,1)S(1)}) custom-call(s32[1]{0:T(128)S(6)} %copy.31.pos, f32[640,128]{1,0:T(8,128)S(1)} %bitcast.23, bf16[32,128]{1,0:T(8,128)(2,1)S(1)} %collective-permute-done.left, bf16[32,128]{1,0:T(8,128)(2,1)S(1)} %collective-permute-done.1.right, ...), custom_call_target="tpu_custom_call" | custom-call | tf_op jit(solution)/shard_map/local_grads/pallas_call | solution.py:450
  24.1 2.6 %collective-permute-start.2 = (bf16[4,4,8,72,128]{4,3,2,1,0:T(8,128)(2,1)S(1)}, bf16[4,4,8,72,128]{4,3,2,1,0:T(8,128)(2,1)S(1)}, u32[]{:S(2)}, u32[]{:S(2)}) collective-permute-start(bf16[4,4,8,72,128]{4,3,2,1,0:T(8,128)(2,1)S(1)} %get-tuple-element.85), channel_id=1, source_target_pairs={{0,8},{1,9},{2,10},{3,11},{8,0},{9,1},{10,2},{11,3},{16,24},{17,25... | collective-permute-start | bytes 7077896 | tf_op jit(solution)/shard_map/ppermute | solution.py:617
  26.7 4.2 %collective-permute-done.2.other = bf16[4,4,8,72,128]{4,3,2,1,0:T(8,128)(2,1)S(1)} collective-permute-done((bf16[4,4,8,72,128]{4,3,2,1,0:T(8,128)(2,1)S(1)}, bf16[4,4,8,72,128]{4,3,2,1,0:T(8,128)(2,1)S(1)}, u32[]{:S(2)}, u32[]{:S(2)}) %collective-permute-start.2) | collective-permute-done | bytes 2359328 | tf_op jit(solution)/shard_map/ppermute | solution.py:617
  30.8 0.5 split_first.1
  31.3 0.6 collective-permute-start.3
  32.0 2.2 %collective-permute-start.4 = (bf16[2,4,2,72,128]{4,3,2,1,0:T(8,128)(2,1)S(1)}, bf16[2,4,2,72,128]{4,3,2,1,0:T(8,128)(2,1)S(1)}, u32[]{:S(2)}, u32[]{:S(2)}) collective-permute-start(bf16[2,4,2,72,128]{4,3,2,1,0:T(8,128)(2,1)S(1)} %get-tuple-element.91), channel_id=1, source_target_pairs={{0,3},{1,2},{2,1},{3,0},{8,11},{9,10},{10,9},{11,8},{16,19},{17,18... | collective-permute-start | bytes 884744 | tf_op jit(solution)/shard_map/ppermute | solution.py:619
  34.1 2.0 %collective-permute-start.5 = (bf16[2,4,2,72,128]{4,3,2,1,0:T(8,128)(2,1)S(1)}, bf16[2,4,2,72,128]{4,3,2,1,0:T(8,128)(2,1)S(1)}, u32[]{:S(2)}, u32[]{:S(2)}) collective-permute-start(bf16[2,4,2,72,128]{4,3,2,1,0:T(8,128)(2,1)S(1)} %get-tuple-element.92), channel_id=1, source_target_pairs={{0,16},{1,17},{2,18},{3,19},{8,24},{9,25},{10,26},{11,27},{16,0},{... | collective-permute-start | bytes 884744 | tf_op jit(solution)/shard_map/ppermute | solution.py:619
  36.1 1.6 %collective-permute-start.6 = (bf16[2,4,2,72,128]{4,3,2,1,0:T(8,128)(2,1)S(1)}, bf16[2,4,2,72,128]{4,3,2,1,0:T(8,128)(2,1)S(1)}, u32[]{:S(2)}, u32[]{:S(2)}) collective-permute-start(bf16[2,4,2,72,128]{4,3,2,1,0:T(8,128)(2,1)S(1)} %get-tuple-element.93), channel_id=1, source_target_pairs={{0,20},{1,21},{2,22},{3,23},{8,28},{9,29},{10,30},{11,31},{16,4},{... | collective-permute-start | bytes 884744 | tf_op jit(solution)/shard_map/ppermute | solution.py:619
  37.7 3.1 %collective-permute-done.3.refs_4_ = bf16[2,4,2,72,128]{4,3,2,1,0:T(8,128)(2,1)S(1)} collective-permute-done((bf16[2,4,2,72,128]{4,3,2,1,0:T(8,128)(2,1)S(1)}, bf16[2,4,2,72,128]{4,3,2,1,0:T(8,128)(2,1)S(1)}, u32[]{:S(2)}, u32[]{:S(2)}) %collective-permute-start.3) | collective-permute-done | bytes 294944 | tf_op jit(solution)/shard_map/ppermute | solution.py:619
  40.7 0.7 collective-permute-done.4.refs_5_
  41.4 1.5 %collective-permute-done.5.refs_6_ = bf16[2,4,2,72,128]{4,3,2,1,0:T(8,128)(2,1)S(1)} collective-permute-done((bf16[2,4,2,72,128]{4,3,2,1,0:T(8,128)(2,1)S(1)}, bf16[2,4,2,72,128]{4,3,2,1,0:T(8,128)(2,1)S(1)}, u32[]{:S(2)}, u32[]{:S(2)}) %collective-permute-start.5) | collective-permute-done | bytes 294944 | tf_op jit(solution)/shard_map/ppermute | solution.py:619
  42.9 2.7 %collective-permute-done.6.refs_7_ = bf16[2,4,2,72,128]{4,3,2,1,0:T(8,128)(2,1)S(1)} collective-permute-done((bf16[2,4,2,72,128]{4,3,2,1,0:T(8,128)(2,1)S(1)}, bf16[2,4,2,72,128]{4,3,2,1,0:T(8,128)(2,1)S(1)}, u32[]{:S(2)}, u32[]{:S(2)}) %collective-permute-start.6) | collective-permute-done | bytes 294944 | tf_op jit(solution)/shard_map/ppermute | solution.py:619
  45.6 0.2 split_second.1
  45.8 0.4 collective-permute-start.7
  46.1 2.3 %collective-permute-start.8 = (bf16[4,2,72,128]{3,2,1,0:T(8,128)(2,1)S(1)}, bf16[4,2,72,128]{3,2,1,0:T(8,128)(2,1)S(1)}, u32[]{:S(2)}, u32[]{:S(2)}) collective-permute-start(bf16[4,2,72,128]{3,2,1,0:T(8,128)(2,1)S(1)} %get-tuple-element.99), channel_id=1, source_target_pairs={{0,1},{1,0},{2,3},{3,2},{8,9},{9,8},{10,11},{11,10},{16,17},{17,16... | collective-permute-start | bytes 442376 | tf_op jit(solution)/shard_map/ppermute | solution.py:621
  48.4 2.0 %collective-permute-start.9 = (bf16[4,2,72,128]{3,2,1,0:T(8,128)(2,1)S(1)}, bf16[4,2,72,128]{3,2,1,0:T(8,128)(2,1)S(1)}, u32[]{:S(2)}, u32[]{:S(2)}) collective-permute-start(bf16[4,2,72,128]{3,2,1,0:T(8,128)(2,1)S(1)} %get-tuple-element.100), channel_id=1, source_target_pairs={{0,20},{1,21},{2,22},{3,23},{8,28},{9,29},{10,30},{11,31},{16,4},{... | collective-permute-start | bytes 442376 | tf_op jit(solution)/shard_map/ppermute | solution.py:621
  50.4 0.0 collective-permute-start.10
  50.4 0.6 collective-permute-done.7.refs_4_
  51.0 0.5 collective-permute-done.8.refs_5_
  51.5 3.2 %collective-permute-done.9.refs_6_ = bf16[4,2,72,128]{3,2,1,0:T(8,128)(2,1)S(1)} collective-permute-done((bf16[4,2,72,128]{3,2,1,0:T(8,128)(2,1)S(1)}, bf16[4,2,72,128]{3,2,1,0:T(8,128)(2,1)S(1)}, u32[]{:S(2)}, u32[]{:S(2)}) %collective-permute-start.9) | collective-permute-done | bytes 147488 | tf_op jit(solution)/shard_map/ppermute | solution.py:621
  54.8 1.1 %collective-permute-done.10.refs_7_ = bf16[4,2,72,128]{3,2,1,0:T(8,128)(2,1)S(1)} collective-permute-done((bf16[4,2,72,128]{3,2,1,0:T(8,128)(2,1)S(1)}, bf16[4,2,72,128]{3,2,1,0:T(8,128)(2,1)S(1)}, u32[]{:S(2)}, u32[]{:S(2)}) %collective-permute-start.10) | collective-permute-done | bytes 147488 | tf_op jit(solution)/shard_map/ppermute | solution.py:621
  55.8 0.1 split_third.1
  55.9 0.1 collective-permute-start.11
  56.0 0.1 collective-permute-start.12
  56.1 5.0 %collective-permute-done.11.refs_2_ = bf16[2,4,72,128]{3,2,1,0:T(8,128)(2,1)S(1)} collective-permute-done((bf16[2,4,72,128]{3,2,1,0:T(8,128)(2,1)S(1)}, bf16[2,4,72,128]{3,2,1,0:T(8,128)(2,1)S(1)}, u32[]{:S(2)}, u32[]{:S(2)}) %collective-permute-start.11) | collective-permute-done | bytes 147488 | tf_op jit(solution)/shard_map/ppermute | solution.py:623
  61.2 0.1 collective-permute-done.12.refs_3_
  61.3 1.1 %collective-permute-start.13 = (bf16[4,72,128]{2,1,0:T(8,128)(2,1)S(1)}, bf16[4,72,128]{2,1,0:T(8,128)(2,1)S(1)}, u32[]{:S(2)}, u32[]{:S(2)}) collective-permute-start(bf16[4,72,128]{2,1,0:T(8,128)(2,1)S(1)} %get-tuple-element.108), channel_id=1, source_target_pairs={{0,20},{1,21},{2,22},{3,23},{8,28},{9,29},{10,30},{11,31},{16,4},{... | collective-permute-start | bytes 221192 | tf_op jit(solution)/shard_map/ppermute | solution.py:625
  62.4 1.5 %collective-permute-start.14 = (bf16[4,72,128]{2,1,0:T(8,128)(2,1)S(1)}, bf16[4,72,128]{2,1,0:T(8,128)(2,1)S(1)}, u32[]{:S(2)}, u32[]{:S(2)}) collective-permute-start(bf16[4,72,128]{2,1,0:T(8,128)(2,1)S(1)} %get-tuple-element.109), channel_id=1, source_target_pairs={{0,3},{1,2},{2,1},{3,0},{8,11},{9,10},{10,9},{11,8},{16,19},{17,18... | collective-permute-start | bytes 221192 | tf_op jit(solution)/shard_map/ppermute | solution.py:625
  63.9 3.1 %collective-permute-done.13.refs_2_ = bf16[4,72,128]{2,1,0:T(8,128)(2,1)S(1)} collective-permute-done((bf16[4,72,128]{2,1,0:T(8,128)(2,1)S(1)}, bf16[4,72,128]{2,1,0:T(8,128)(2,1)S(1)}, u32[]{:S(2)}, u32[]{:S(2)}) %collective-permute-start.13) | collective-permute-done | bytes 73760 | tf_op jit(solution)/shard_map/ppermute | solution.py:625
  67.0 0.0 collective-permute-done.14.refs_3_
  67.0 20.3 %all_to_all.10 = bf16[8,72,128]{2,1,0:T(8,128)(2,1)S(1)} all-to-all(bf16[8,72,128]{2,1,0:T(8,128)(2,1)S(1)} %join.1), channel_id=1, replica_groups={{0,32,64,96,128,160,192,224},{1,33,65,97,129,161,193,225},{2,34,66,98,1..., dimensions={0} | all-to-all | bytes 294912 | tf_op jit(solution)/shard_map/all_to_all | solution.py:530
  87.3 14.0 %all_to_all.11.t = bf16[8,72,128]{2,1,0:T(8,128)(2,1)} all-to-all(bf16[8,72,128]{2,1,0:T(8,128)(2,1)S(1)} %broadcast_in_dim.27), channel_id=1, replica_groups=mesh['frame'=32,'rec'=8] {'rec'}, dimensions={0} | all-to-all | bytes 294912 | tf_op jit(solution)/shard_map/all_to_all | solution.py:628
  101.3 1.6 %unpack.1 = (f32[16,1536]{1,0:T(8,128)}, f32[16,1280]{1,0:T(8,128)}, f32[48,512]{1,0:T(8,128)}, f32[8,16]{1,0:T(8,128)}, f32[1,16]{1,0:T(1,128)}, /*index=5*/f32...) custom-call(bf16[8,72,128]{2,1,0:T(8,128)(2,1)} %all_to_all.11.t), custom_call_target="tpu_custom_call" | custom-call | tf_op jit(solution)/shard_map/unpack/pallas_call | solution.py:499
  (7 shorter events, 0.1 us)
Async XLA Ops:
  2.2 7.8 %collective-permute-start = (bf16[32,128]{1,0:T(8,128)(2,1)S(1)}, bf16[32,128]{1,0:T(8,128)(2,1)S(1)}, u32[]{:S(2)}, u32[]{:S(2)}) collective-permute-start(bf16[32,128]{1,0:T(8,128)(2,1)S(1)} %pad_maximum_fusion), channel_id=1, source_target_pairs={{0,8},{8,16},{16,24},{24,32},{32,40},{40,48},{48,56},{56,64},{64,7... | collective-permute-start | bytes 24584 | tf_op jit(solution)/shard_map/ppermute | solution.py:639
  3.9 6.0 %collective-permute-start.1 = (bf16[32,128]{1,0:T(8,128)(2,1)S(1)}, bf16[32,128]{1,0:T(8,128)(2,1)S(1)}, u32[]{:S(2)}, u32[]{:S(2)}) collective-permute-start(bf16[32,128]{1,0:T(8,128)(2,1)S(1)} %pad_maximum_fusion.1), channel_id=1, source_target_pairs={{8,0},{16,8},{24,16},{32,24},{40,32},{48,40},{56,48},{64,56},{72,6... | collective-permute-start | bytes 24584 | tf_op jit(solution)/shard_map/ppermute | solution.py:640
  24.1 6.7 %collective-permute-start.2 = (bf16[4,4,8,72,128]{4,3,2,1,0:T(8,128)(2,1)S(1)}, bf16[4,4,8,72,128]{4,3,2,1,0:T(8,128)(2,1)S(1)}, u32[]{:S(2)}, u32[]{:S(2)}) collective-permute-start(bf16[4,4,8,72,128]{4,3,2,1,0:T(8,128)(2,1)S(1)} %get-tuple-element.85), channel_id=1, source_target_pairs={{0,8},{1,9},{2,10},{3,11},{8,0},{9,1},{10,2},{11,3},{16,24},{17,25... | collective-permute-start | bytes 7077896 | tf_op jit(solution)/shard_map/ppermute | solution.py:617
  31.3 9.4 %collective-permute-start.3 = (bf16[2,4,2,72,128]{4,3,2,1,0:T(8,128)(2,1)S(1)}, bf16[2,4,2,72,128]{4,3,2,1,0:T(8,128)(2,1)S(1)}, u32[]{:S(2)}, u32[]{:S(2)}) collective-permute-start(bf16[2,4,2,72,128]{4,3,2,1,0:T(8,128)(2,1)S(1)} %get-tuple-element.90), channel_id=1, source_target_pairs={{0,1},{1,0},{2,3},{3,2},{8,9},{9,8},{10,11},{11,10},{16,17},{17,16... | collective-permute-start | bytes 884744 | tf_op jit(solution)/shard_map/ppermute | solution.py:619
  32.0 9.4 %collective-permute-start.4 = (bf16[2,4,2,72,128]{4,3,2,1,0:T(8,128)(2,1)S(1)}, bf16[2,4,2,72,128]{4,3,2,1,0:T(8,128)(2,1)S(1)}, u32[]{:S(2)}, u32[]{:S(2)}) collective-permute-start(bf16[2,4,2,72,128]{4,3,2,1,0:T(8,128)(2,1)S(1)} %get-tuple-element.91), channel_id=1, source_target_pairs={{0,3},{1,2},{2,1},{3,0},{8,11},{9,10},{10,9},{11,8},{16,19},{17,18... | collective-permute-start | bytes 884744 | tf_op jit(solution)/shard_map/ppermute | solution.py:619
  34.1 8.8 %collective-permute-start.5 = (bf16[2,4,2,72,128]{4,3,2,1,0:T(8,128)(2,1)S(1)}, bf16[2,4,2,72,128]{4,3,2,1,0:T(8,128)(2,1)S(1)}, u32[]{:S(2)}, u32[]{:S(2)}) collective-permute-start(bf16[2,4,2,72,128]{4,3,2,1,0:T(8,128)(2,1)S(1)} %get-tuple-element.92), channel_id=1, source_target_pairs={{0,16},{1,17},{2,18},{3,19},{8,24},{9,25},{10,26},{11,27},{16,0},{... | collective-permute-start | bytes 884744 | tf_op jit(solution)/shard_map/ppermute | solution.py:619
  36.1 9.5 %collective-permute-start.6 = (bf16[2,4,2,72,128]{4,3,2,1,0:T(8,128)(2,1)S(1)}, bf16[2,4,2,72,128]{4,3,2,1,0:T(8,128)(2,1)S(1)}, u32[]{:S(2)}, u32[]{:S(2)}) collective-permute-start(bf16[2,4,2,72,128]{4,3,2,1,0:T(8,128)(2,1)S(1)} %get-tuple-element.93), channel_id=1, source_target_pairs={{0,20},{1,21},{2,22},{3,23},{8,28},{9,29},{10,30},{11,31},{16,4},{... | collective-permute-start | bytes 884744 | tf_op jit(solution)/shard_map/ppermute | solution.py:619
  45.8 5.2 %collective-permute-start.7 = (bf16[4,2,72,128]{3,2,1,0:T(8,128)(2,1)S(1)}, bf16[4,2,72,128]{3,2,1,0:T(8,128)(2,1)S(1)}, u32[]{:S(2)}, u32[]{:S(2)}) collective-permute-start(bf16[4,2,72,128]{3,2,1,0:T(8,128)(2,1)S(1)} %get-tuple-element.98), channel_id=1, source_target_pairs={{0,3},{1,2},{2,1},{3,0},{8,11},{9,10},{10,9},{11,8},{16,19},{17,18... | collective-permute-start | bytes 442376 | tf_op jit(solution)/shard_map/ppermute | solution.py:621
  46.1 5.4 %collective-permute-start.8 = (bf16[4,2,72,128]{3,2,1,0:T(8,128)(2,1)S(1)}, bf16[4,2,72,128]{3,2,1,0:T(8,128)(2,1)S(1)}, u32[]{:S(2)}, u32[]{:S(2)}) collective-permute-start(bf16[4,2,72,128]{3,2,1,0:T(8,128)(2,1)S(1)} %get-tuple-element.99), channel_id=1, source_target_pairs={{0,1},{1,0},{2,3},{3,2},{8,9},{9,8},{10,11},{11,10},{16,17},{17,16... | collective-permute-start | bytes 442376 | tf_op jit(solution)/shard_map/ppermute | solution.py:621
  48.4 6.4 %collective-permute-start.9 = (bf16[4,2,72,128]{3,2,1,0:T(8,128)(2,1)S(1)}, bf16[4,2,72,128]{3,2,1,0:T(8,128)(2,1)S(1)}, u32[]{:S(2)}, u32[]{:S(2)}) collective-permute-start(bf16[4,2,72,128]{3,2,1,0:T(8,128)(2,1)S(1)} %get-tuple-element.100), channel_id=1, source_target_pairs={{0,20},{1,21},{2,22},{3,23},{8,28},{9,29},{10,30},{11,31},{16,4},{... | collective-permute-start | bytes 442376 | tf_op jit(solution)/shard_map/ppermute | solution.py:621
  50.4 5.4 %collective-permute-start.10 = (bf16[4,2,72,128]{3,2,1,0:T(8,128)(2,1)S(1)}, bf16[4,2,72,128]{3,2,1,0:T(8,128)(2,1)S(1)}, u32[]{:S(2)}, u32[]{:S(2)}) collective-permute-start(bf16[4,2,72,128]{3,2,1,0:T(8,128)(2,1)S(1)} %get-tuple-element.101), channel_id=1, source_target_pairs={{0,16},{1,17},{2,18},{3,19},{8,24},{9,25},{10,26},{11,27},{16,0},{... | collective-permute-start | bytes 442376 | tf_op jit(solution)/shard_map/ppermute | solution.py:621
  55.9 5.2 %collective-permute-start.11 = (bf16[2,4,72,128]{3,2,1,0:T(8,128)(2,1)S(1)}, bf16[2,4,72,128]{3,2,1,0:T(8,128)(2,1)S(1)}, u32[]{:S(2)}, u32[]{:S(2)}) collective-permute-start(bf16[2,4,72,128]{3,2,1,0:T(8,128)(2,1)S(1)} %get-tuple-element.104), channel_id=1, source_target_pairs={{0,16},{1,17},{2,18},{3,19},{8,24},{9,25},{10,26},{11,27},{16,0},{... | collective-permute-start | bytes 442376 | tf_op jit(solution)/shard_map/ppermute | solution.py:623
  56.0 5.2 %collective-permute-start.12 = (bf16[2,4,72,128]{3,2,1,0:T(8,128)(2,1)S(1)}, bf16[2,4,72,128]{3,2,1,0:T(8,128)(2,1)S(1)}, u32[]{:S(2)}, u32[]{:S(2)}) collective-permute-start(bf16[2,4,72,128]{3,2,1,0:T(8,128)(2,1)S(1)} %get-tuple-element.105), channel_id=1, source_target_pairs={{0,1},{1,0},{2,3},{3,2},{8,9},{9,8},{10,11},{11,10},{16,17},{17,16... | collective-permute-start | bytes 442376 | tf_op jit(solution)/shard_map/ppermute | solution.py:623
  61.3 5.7 %collective-permute-start.13 = (bf16[4,72,128]{2,1,0:T(8,128)(2,1)S(1)}, bf16[4,72,128]{2,1,0:T(8,128)(2,1)S(1)}, u32[]{:S(2)}, u32[]{:S(2)}) collective-permute-start(bf16[4,72,128]{2,1,0:T(8,128)(2,1)S(1)} %get-tuple-element.108), channel_id=1, source_target_pairs={{0,20},{1,21},{2,22},{3,23},{8,28},{9,29},{10,30},{11,31},{16,4},{... | collective-permute-start | bytes 221192 | tf_op jit(solution)/shard_map/ppermute | solution.py:625
  62.4 4.6 %collective-permute-start.14 = (bf16[4,72,128]{2,1,0:T(8,128)(2,1)S(1)}, bf16[4,72,128]{2,1,0:T(8,128)(2,1)S(1)}, u32[]{:S(2)}, u32[]{:S(2)}) collective-permute-start(bf16[4,72,128]{2,1,0:T(8,128)(2,1)S(1)} %get-tuple-element.109), channel_id=1, source_target_pairs={{0,3},{1,2},{2,1},{3,0},{8,11},{9,10},{10,9},{11,8},{16,19},{17,18... | collective-permute-start | bytes 221192 | tf_op jit(solution)/shard_map/ppermute | solution.py:625
